TPU v7x, 256 devices: a whole 4x4x8 slice. The times are simulated.
256 devices in a mesh: rows: 128 (over y, x, z), cols: 2 (over core).
Axes of the slice: x: 4, y: 4, z: 8, core: 2. Of those that a mesh axis runs over, the one named last changes fastest.
Arguments:
- points: float32 [65536, 768], P('rows'), may hold values from -83 to 83
- landmark_index: int32 [32768], P('rows'), may hold values from 0 to 65535, as said below
- targets: float32 [32768, 512], P('rows', 'cols'), may hold values from -6 to 6
- ridge_shift: float32 [1], replicated, may hold values from 0.5 to 2
Outputs:
- projected: float32 [512, 2048], P('rows', 'cols')
- panels: float32 [32768, 256], P('rows')
- remainder: float32 [32768, 1792], P('rows', 'cols')
Inputs may be any that keep to these rules, and one draw needn't show every extreme that they name: `landmark_index`: landmark i is a point of the block [(i // 256) * 512, (i // 256 + 1) * 512); the 256 landmarks of one block are distinct.
All inputs are finite; a program needn't handle non-finite values.
Results may differ from a plain program's by a relative error of at most 0.00028.
Values sent between devices are 32-bit elements; how exact they have to be, the bound alone decides.
No kernel may reach another device: no remote copies, remote signals or barrier semaphores. Data moves between devices by JAX's collectives and lax.ppermute only.
A program may use at most 64 MiB of HBM per device.

v0:
```python
import jax
import jax.numpy as jnp
from jax import lax
from jax.sharding import Mesh
from jax.sharding import PartitionSpec as P

C = 2048
PW = 128
ROWS = ("rows_0", "rows_1", "rows_2")


exact_mode = lax.Precision.HIGHEST


def in_order(pieces, dim):
    pieces = jnp.moveaxis(pieces, 0, dim)
    shape = pieces.shape
    return pieces.reshape(*shape[:dim], shape[dim] * shape[dim + 1], *shape[dim + 2 :])


def stacked_from(x, axes, turns):
    pieces = x
    for k in turns:
        pieces = lax.all_gather(pieces, axes[k])
    done = turns[::-1]
    back = [done.index(k) for k in range(len(axes))]
    pieces = pieces.transpose(*back, *range(len(axes), pieces.ndim))
    return pieces.reshape(-1, *x.shape)


def gather_axes(x, axes, turns, dim):
    return in_order(stacked_from(x, axes, turns), dim)


def from_everyone(x, axis):
    peers = lax.axis_size(axis)
    return lax.all_to_all(jnp.broadcast_to(x[None], (peers, *x.shape)), axis, 0, 0, tiled=True)


def gathered_copies(x, axis, dim):
    pieces = from_everyone(x, axis)
    return in_order(pieces, dim)


def in_blocks(x, dim, peers):
    before, after = (x.shape[:dim], x.shape[dim + 1 :])
    return jnp.moveaxis(x.reshape(*before, peers, -1, *after), dim, 0)


def summed_on_arrival(x, axis, dim):
    pieces = in_blocks(x, dim, lax.axis_size(axis))
    arrived = lax.all_to_all(pieces, axis, split_axis=0, concat_axis=0, tiled=True)
    return arrived.sum(axis=0)


def summed_rows(x, axes, dim):
    far, near = axes
    pieces = in_blocks(x, dim, lax.axis_size(far))
    nearer = summed_on_arrival(pieces, near, dim + 1)
    arrived = lax.all_to_all(nearer, far, split_axis=0, concat_axis=0, tiled=True)
    return arrived.sum(axis=0)


def from_root(x, axis, root):
    return lax.dynamic_index_in_dim(lax.all_gather(x, axis), root, 0, keepdims=False)


def whole_of(x, axes, dim):
    far, near = axes
    pieces = from_everyone(from_everyone(x, far), near)
    return in_order(pieces.swapaxes(0, 1).reshape(-1, *x.shape), dim)


def gaussian(left_rows, right_rows):
    left_sq = jnp.sum(left_rows * left_rows, axis=1)
    right_sq = jnp.sum(right_rows * right_rows, axis=1)
    cross_term = jnp.dot(
        left_rows, right_rows.T, precision=exact_mode, preferred_element_type=jnp.float32
    )
    return jnp.exp(
        -(left_sq[:, None] + right_sq[None, :] - 2.0 * cross_term) / (2.0 * left_rows.shape[1])
    )


def product(left_rows, right_rows):
    return jnp.dot(
        left_rows, right_rows.T, precision=exact_mode, preferred_element_type=jnp.float32
    )


def per_device(points, landmark_index, targets, ridge_shift):
    rows_here = landmark_index.shape[0]
    block_points = points.shape[0]
    row_pos = lax.axis_index(ROWS)
    col_pos = lax.axis_index("cols")
    n_rows = lax.axis_size(ROWS)
    half_cols = C // 2
    quarter = half_cols // n_rows
    local_index = landmark_index - row_pos * block_points
    embedded = jnp.take(points, local_index, axis=0)
    own_landmarks = lax.dynamic_slice_in_dim(embedded, col_pos * quarter, quarter, 0)
    column_emb = gather_axes(own_landmarks, ROWS, (0, 1, 2), 0)
    row_ids = lax.broadcasted_iota(jnp.int32, (rows_here, half_cols), 0)
    col_ids = lax.broadcasted_iota(jnp.int32, (rows_here, half_cols), 1)
    offset = row_ids - col_pos * quarter
    ridge_hits = (offset >= 0) & (offset < quarter) & (col_ids == row_pos * quarter + offset)
    kernel_slab = gaussian(embedded, column_emb) + jnp.where(ridge_hits, ridge_shift[0], 0.0)
    all_targets = gathered_copies(targets, "cols", 1)
    projected = summed_rows(
        lax.dot_general(
            all_targets,
            kernel_slab,
            (((0,), (0,)), ((), ())),
            precision=exact_mode,
            preferred_element_type=jnp.float32,
        ),
        ("rows_0", ("rows_1", "rows_2")),
        0,
    )
    head_emb = column_emb[:PW]
    diag_base = gaussian(head_emb, head_emb) + ridge_shift[0] * jnp.eye(PW, dtype=jnp.float32)
    panel_list = []
    earlier = None
    for panel_index in range(2):
        diag_block = diag_base
        if panel_index == 1:
            diag_block = diag_block - product(earlier[:PW], earlier[:PW])
        diag_block = jnp.where(col_pos == panel_index, diag_block, jnp.eye(PW, dtype=jnp.float32))
        factor = jnp.linalg.cholesky(diag_block)
        local_panel = jax.scipy.linalg.solve_triangular(factor, kernel_slab[:, :PW].T, lower=True).T
        local_panel = from_root(local_panel, "cols", panel_index)
        landmark_rows = whole_of(
            lax.dynamic_slice_in_dim(local_panel, col_pos * quarter, quarter, 0),
            ("rows_0", ("rows_1", "rows_2")),
            0,
        )
        kernel_slab = kernel_slab - product(local_panel, landmark_rows)
        panel_list.append(local_panel)
        earlier = landmark_rows
    return (projected, jnp.concatenate(panel_list, axis=1), kernel_slab[:, PW:])


def solution(mesh):
    split = Mesh(
        mesh.devices.reshape(4, 4, 8, mesh.shape["cols"]), ("rows_0", "rows_1", "rows_2", "cols")
    )
    placed = (P(ROWS, None), P(ROWS), P(ROWS, "cols"), P())
    return jax.shard_map(
        per_device,
        mesh=split,
        in_specs=placed,
        out_specs=(P(ROWS, "cols"), P(ROWS, None), P(ROWS, "cols")),
        check_vma=False,
    )
```

profile of v0, /device:TPU:1, one launch (start us, length us, event | category | flops | bytes accessed | tf_op | source)
XLA Modules:
  0.0 293.8 jit_solution(3059606876171282473)
XLA Ops:
  7.2 0.8 compare_and_fusion.1
  8.6 1.1 gather_fusion
  9.9 10.5 %all-gather = f32[32,768]{1,0:T(8,128)S(1)} all-gather(f32[8,768]{1,0:T(8,128)S(1)} %constant_dynamic-slice_fusion.2), channel_id=2, replica_groups=mesh['rows_0'=4,'rows_1'=4,'rows_2'=8,'cols'=2] {'rows_0'}, dimensions={0}, use_global_device_ids=true | all-gather | bytes 122880 | tf_op jit(solution)/shard_map/all_gather | solution.py:24
  20.4 10.7 %all-gather.1 = f32[16,8,768]{2,1,0:T(8,128)} all-gather(f32[4,8,768]{2,1,0:T(8,128)S(1)} %bitcast.70), channel_id=3, replica_groups=mesh['rows_0'=4,'rows_1'=4,'rows_2'=8,'cols'=2] {'rows_1'}, dimensions={0}, use_global_device_ids=true | all-gather | bytes 491520 | tf_op jit(solution)/shard_map/all_gather | solution.py:24
  31.8 51.2 %all-gather.7.cloned.1.call-done = f32[32,4,8,768]{3,2,1,0:T(8,128)} async-done(((f32[4,4,8,768]{3,2,1,0:T(8,128)}), f32[32,4,8,768]{3,2,1,0:T(8,128)}) %all-gather.7.cloned.1.call-update) | async-done | bytes 3145744 | tf_op jit(solution)/shard_map/all_gather | solution.py:24
  83.1 2.4 copy.57
  86.3 1.2 copy-done.1
  87.6 1.1 convert_select_fusion
  88.8 11.7 %cholesky.44 = f32[128,128]{1,0:T(8,128)S(1)} custom-call(f32[128,128]{1,0:T(8,128)S(1)} %fusion.19), custom_call_target="Cholesky" | custom-call | tf_op jit(solution)/shard_map/jit(cholesky)/cholesky | solution.py:129
  100.5 0.6 compare_reduce_fusion.1
  101.2 0.7 fusion.13
  101.8 9.8 %custom-call.6 = f32[1,128,128]{1,2,0:T(8,128)S(1)} custom-call(f32[1,128,128]{2,1,0:T(8,128)S(1)} %fusion.13), custom_call_target="InvertDiagBlocksLowerTriangular" | custom-call | tf_op jit(solution)/shard_map/jit(_solve_triangular)/triangular_solve | solution.py:130
  111.8 4.9 %fusion.4 = f32[256,1024]{1,0:T(8,128)S(1)} fusion(f32[256,768]{1,0:T(8,128)S(1)} %get-tuple-element.24, f32[1024,768]{1,0:T(8,128)} %bitcast.61, f32[]{:T(128)} %bitcast.57, s32[256]{0:T(256)S(1)} %fusion.20, f32[1024]{0:T(1024)S(1)} %add.78, f32[256]{0:T(256)S(1)} %get-tuple-element.23, pred[256]{0:T(512)(128)(4,1)S(1)} %compare_and_fusion), kind=kOutput, calls=%fused_computation.10 | convolution fusion | flops 2418278400 | bytes 4987140 | tf_op jit(solution)/shard_map/dot_general | solution.py:77
  117.0 2.9 all-gather.3
  119.9 0.7 copy-done.5
  120.7 8.0 %all_to_all.35 = f32[4,8,128]{2,1,0:T(8,128)S(1)} all-to-all(f32[4,8,128]{2,1,0:T(8,128)S(1)} %broadcast_in_dim.66), channel_id=1, replica_groups=mesh['rows_0'=4,'rows_1'=4,'rows_2'=8,'cols'=2] {'rows_0'}, dimensions={0} | all-to-all | bytes 32768 | tf_op jit(solution)/shard_map/all_to_all | solution.py:37
  128.7 0.9 broadcast_in_dim.67
  129.6 7.0 %all-to-all-start.4 = ((f32[32,4,8,128]{3,2,1,0:T(8,128)}), f32[32,4,8,128]{3,2,1,0:T(8,128)S(1)}, u32[]{:S(2)}, u32[]{:S(2)}) async-start(f32[32,4,8,128]{3,2,1,0:T(8,128)} %broadcast_in_dim.67), calls=%async_computation.4 | async-start | bytes 1048576 | tf_op jit(solution)/shard_map/all_to_all | solution.py:37
  136.7 1.1 copy.58
  137.7 11.9 %all-to-all-done.4 = f32[32,4,8,128]{3,2,1,0:T(8,128)S(1)} async-done(((f32[32,4,8,128]{3,2,1,0:T(8,128)}), f32[32,4,8,128]{3,2,1,0:T(8,128)S(1)}, u32[]{:S(2)}, u32[]{:S(2)}) %all-to-all-start.4) | async-done | bytes 524320 | tf_op jit(solution)/shard_map/all_to_all | solution.py:37
  149.7 0.9 broadcast_in_dim.64
  150.7 8.6 %all-to-all-start = ((f32[2,256,256]{1,2,0:T(8,128)}), f32[2,256,256]{1,2,0:T(8,128)S(1)}, u32[]{:S(2)}, u32[]{:S(2)}) async-start(f32[2,256,256]{1,2,0:T(8,128)} %broadcast_in_dim.64), calls=%async_computation | async-start | bytes 1048576 | tf_op jit(solution)/shard_map/all_to_all | solution.py:37
  159.3 1.1 copy.63
  160.3 2.9 convolution_subtract_fusion
  163.6 11.7 %cholesky.55 = f32[128,128]{1,0:T(8,128)S(1)} custom-call(f32[128,128]{1,0:T(8,128)S(1)} %fusion.17), custom_call_target="Cholesky" | custom-call | tf_op jit(solution)/shard_map/jit(cholesky)/cholesky | solution.py:129
  176.0 0.7 fusion.14
  176.7 9.8 %custom-call.7 = f32[1,128,128]{1,2,0:T(8,128)S(1)} custom-call(f32[1,128,128]{2,1,0:T(8,128)S(1)} %fusion.14), custom_call_target="InvertDiagBlocksLowerTriangular" | custom-call | tf_op jit(solution)/shard_map/jit(_solve_triangular)/triangular_solve | solution.py:130
  186.5 1.2 convolution_bitcast_fusion.1
  187.7 2.0 all-gather.4
  189.8 0.6 copy-done.6
  190.4 0.7 constant_dynamic-slice_fusion
  191.1 0.9 copy.66
  192.0 6.6 %all_to_all.36 = f32[4,8,128]{2,1,0:T(8,128)S(1)} all-to-all(f32[4,8,128]{2,1,0:T(8,128)S(1)} %broadcast_in_dim.69), channel_id=1, replica_groups=mesh['rows_0'=4,'rows_1'=4,'rows_2'=8,'cols'=2] {'rows_0'}, dimensions={0} | all-to-all | bytes 32768 | tf_op jit(solution)/shard_map/all_to_all | solution.py:37
  198.6 0.9 broadcast_in_dim.70
  199.4 5.1 %all-to-all-start.6 = ((f32[32,4,8,128]{3,2,1,0:T(8,128)}), f32[32,4,8,128]{3,2,1,0:T(8,128)}, u32[]{:S(2)}, u32[]{:S(2)}) async-start(f32[32,4,8,128]{3,2,1,0:T(8,128)} %broadcast_in_dim.70), calls=%async_computation.6 | async-start | bytes 1048576 | tf_op jit(solution)/shard_map/all_to_all | solution.py:37
  204.6 3.2 %convolution_bitcast_fusion = f32[512,1024]{1,0:T(8,128)} fusion(f32[256,1024]{1,0:T(8,128)S(1)} %fusion.4, f32[256,512]{0,1:T(8,128)S(1)} %bitcast.67), kind=kOutput, calls=%fused_computation.3 | convolution fusion | flops 1610612736 | bytes 3670016 | tf_op jit(solution)/shard_map/dot_general | solution.py:110
  207.7 2.9 reshape_reshape.13
  210.6 3.1 %copy.72 = f32[4,32,4,1024]{3,2,0,1:T(4,128)} copy(f32[4,32,4,1024]{3,2,1,0:T(4,128)} %reshape_reshape.13) | data formatting | bytes 4194304 | tf_op jit(solution)/shard_map/reshape;reshape | solution.py:47
  213.8 4.4 %all-to-all-done.6 = f32[32,4,8,128]{3,2,1,0:T(8,128)} async-done(((f32[32,4,8,128]{3,2,1,0:T(8,128)}), f32[32,4,8,128]{3,2,1,0:T(8,128)}, u32[]{:S(2)}, u32[]{:S(2)}) %all-to-all-start.6) | async-done | bytes 524320 | tf_op jit(solution)/shard_map/all_to_all | solution.py:37
  218.2 8.2 %all-to-all-start.1 = ((f32[32,4,4,1024]{3,2,1,0:T(4,128)}), f32[32,4,4,1024]{3,2,1,0:T(4,128)}, u32[]{:S(2)}, u32[]{:S(2)}) async-start(f32[32,4,4,1024]{3,2,1,0:T(4,128)} %bitcast.64), calls=%async_computation.1 | async-start | bytes 4194304 | tf_op jit(solution)/shard_map/all_to_all | solution.py:52
  226.4 0.8 copy.68
  227.2 1.1 copy.67
  228.3 2.1 fusion.21
  230.4 45.6 %all-to-all-done.1 = f32[32,4,4,1024]{3,2,1,0:T(4,128)} async-done(((f32[32,4,4,1024]{3,2,1,0:T(4,128)}), f32[32,4,4,1024]{3,2,1,0:T(4,128)}, u32[]{:S(2)}, u32[]{:S(2)}) %all-to-all-start.1) | async-done | bytes 2097184 | tf_op jit(solution)/shard_map/all_to_all | solution.py:52
  275.9 2.7 reduce_sum.51
  278.6 3.3 %all-to-all-start.2 = ((f32[4,4,1024]{2,1,0:T(4,128)}), f32[4,4,1024]{2,1,0:T(4,128)S(1)}, u32[]{:S(2)}, u32[]{:S(2)}) async-start(f32[4,4,1024]{2,1,0:T(4,128)} %reduce_sum.51), calls=%async_computation.2 | async-start | bytes 131072 | tf_op jit(solution)/shard_map/all_to_all | solution.py:60
  281.9 2.2 slice_subtract_fusion
  284.1 2.2 all-to-all-done.2
  (44 shorter events, 4.3 us)
Async XLA Ops:
  7.2 1.4 copy-start
  7.2 75.9 %all-gather.7.cloned.1.call-start = ((), (), s32[]{:S(2)}) async-start(), calls=%async_computation.7 | async-start | bytes 3538944 | tf_op jit(solution)/shard_map/all_gather | solution.py:24
  83.1 2.8 copy-start.2
  85.9 1.7 copy-start.1
  119.9 0.7 copy-start.5
  129.6 20.1 %all-to-all-start.4 = ((f32[32,4,8,128]{3,2,1,0:T(8,128)}), f32[32,4,8,128]{3,2,1,0:T(8,128)S(1)}, u32[]{:S(2)}, u32[]{:S(2)}) async-start(f32[32,4,8,128]{3,2,1,0:T(8,128)} %broadcast_in_dim.67), calls=%async_computation.4 | async-start | bytes 1048576 | tf_op jit(solution)/shard_map/all_to_all | solution.py:37
  149.7 1.0 copy-start.4
  150.6 12.7 %copy-start.8 = (f32[128,128]{0,1:T(8,128)S(1)}, f32[128,128]{0,1:T(8,128)}, u32[]{:S(2)}) copy-start(f32[128,128]{0,1:T(8,128)} %get-tuple-element.28) | copy-start | bytes 196612
  150.7 41.3 %all-to-all-start = ((f32[2,256,256]{1,2,0:T(8,128)}), f32[2,256,256]{1,2,0:T(8,128)S(1)}, u32[]{:S(2)}, u32[]{:S(2)}) async-start(f32[2,256,256]{1,2,0:T(8,128)} %broadcast_in_dim.64), calls=%async_computation | async-start | bytes 1048576 | tf_op jit(solution)/shard_map/all_to_all | solution.py:37
  189.7 0.7 copy-start.6
  199.4 18.8 %all-to-all-start.6 = ((f32[32,4,8,128]{3,2,1,0:T(8,128)}), f32[32,4,8,128]{3,2,1,0:T(8,128)}, u32[]{:S(2)}, u32[]{:S(2)}) async-start(f32[32,4,8,128]{3,2,1,0:T(8,128)} %broadcast_in_dim.70), calls=%async_computation.6 | async-start | bytes 1048576 | tf_op jit(solution)/shard_map/all_to_all | solution.py:37
  213.7 12.6 %copy-start.7 = (f32[256,128]{0,1:T(8,128)S(1)}, f32[256,128]{0,1:T(8,128)}, u32[]{:S(2)}) copy-start(f32[256,128]{0,1:T(8,128)} %copy-done.6) | copy-start | bytes 393220
  218.2 57.7 %all-to-all-start.1 = ((f32[32,4,4,1024]{3,2,1,0:T(4,128)}), f32[32,4,4,1024]{3,2,1,0:T(4,128)}, u32[]{:S(2)}, u32[]{:S(2)}) async-start(f32[32,4,4,1024]{3,2,1,0:T(4,128)} %bitcast.64), calls=%async_computation.1 | async-start | bytes 4194304 | tf_op jit(solution)/shard_map/all_to_all | solution.py:52
  226.4 55.5 %copy-start.3 = (f32[256,1024]{1,0:T(8,128)S(1)}, f32[256,1024]{1,0:T(8,128)}, u32[]{:S(2)}) copy-start(f32[256,1024]{1,0:T(8,128)} %convolution_subtract_fusion) | copy-start | bytes 3145732
  278.6 7.7 %all-to-all-start.2 = ((f32[4,4,1024]{2,1,0:T(4,128)}), f32[4,4,1024]{2,1,0:T(4,128)S(1)}, u32[]{:S(2)}, u32[]{:S(2)}) async-start(f32[4,4,1024]{2,1,0:T(4,128)} %reduce_sum.51), calls=%async_computation.2 | async-start | bytes 131072 | tf_op jit(solution)/shard_map/all_to_all | solution.py:60
Sparse Core Ops, SparseCore 0:
  31.3 51.7 all-gather.6
where the time goes:
time: 296 us; the launch traced here: 294 us
  waiting for transfers between devices  115 us (39%)
  other arithmetic  52.7 us (18%)
  blocking collectives  40.6 us (14%)
  starting transfers between devices  32.3 us (11%)
  local copies, waits for them, and re-layouts  21.9 us (7%)
  matrix products  15.9 us (5%)
  between operations  15 us (5%)
    all_gather x1, waiting for transfers between devices, stacked_from(): pieces = lax.all_gather(pieces, axes[k])  51.2 us
    all_to_all x1, waiting for transfers between devices, summed_on_arrival(): lax.all_to_all(pieces, axis, split_axis=0, concat_axis=0, tiled=True)  45.6 us
    another operation x6, other arithmetic, per_device(): factor = jnp.linalg.cholesky(diag_block)  24.8 us
    all_gather x2, blocking collectives, stacked_from(): pieces = lax.all_gather(pieces, axes[k])  21.2 us
    another operation x4, other arithmetic, per_device(): jax.scipy.linalg.solve_triangular(factor, kernel_slab[:, :PW].T, lower=True)  20.9 us
    all_to_all x3, starting transfers between devices, from_everyone(): lax.all_to_all(jnp.broadcast_to(x[None], (peers, *x.shape)), axis, 0, 0,...  20.8 us
    all_to_all x3, waiting for transfers between devices, from_everyone(): lax.all_to_all(jnp.broadcast_to(x[None], (peers, *x.shape)), axis, 0, 0,...  16.4 us
    all_to_all x2, blocking collectives, from_everyone(): lax.all_to_all(jnp.broadcast_to(x[None], (peers, *x.shape)), axis, 0, 0,...  14.6 us
  transfers between devices with their start and end apart: 6, of which 5 were waited for; matrix products, arithmetic and copies ran while one was open for 16% of the time, Pallas kernels for 0%

commit v1 on v0

v1 whole, which is shorter than its diff:
```python
import jax
import jax.numpy as jnp
from jax import lax
from jax.sharding import Mesh
from jax.sharding import PartitionSpec as P

C = 2048
PW = 128
ROWS = ("rows_0", "rows_1", "rows_2")
PLANE = ("rows_0", "rows_1")

exact_mode = lax.Precision.HIGHEST


def to_all(x, axis):
    peers = lax.axis_size(axis)
    return lax.all_to_all(jnp.broadcast_to(x[None], (peers, *x.shape)), axis, 0, 0, tiled=True)


def summed(x, axis):
    peers = lax.axis_size(axis)
    pieces = x.reshape(peers, x.shape[0] // peers, *x.shape[1:])
    return lax.all_to_all(pieces, axis, 0, 0, tiled=True).sum(axis=0)


def dot_t(left, right):
    return lax.dot_general(
        left, right, (((1,), (1,)), ((), ())), precision=exact_mode, preferred_element_type=jnp.float32
    )


def gaussian(left, left_sq, right, right_sq):
    cross = dot_t(left, right)
    return jnp.exp(-(left_sq[:, None] + right_sq[None, :] - 2.0 * cross) / (2.0 * left.shape[1]))


def squares(x):
    return jnp.sum(x * x, axis=1)


def lower_inverse(block):
    factor = jnp.linalg.cholesky(block)
    eye = jnp.eye(PW, dtype=jnp.float32)
    return jax.scipy.linalg.solve_triangular(factor, eye, lower=True)


def per_device(points, landmark_index, targets, ridge_shift):
    rows_here = landmark_index.shape[0]
    block_points = points.shape[0]
    row_pos = lax.axis_index(ROWS)
    col_pos = lax.axis_index("cols")
    n_rows = lax.axis_size(ROWS)
    half_cols = C // 2
    quarter = half_cols // n_rows
    ridge = ridge_shift[0]

    peer_targets = lax.ppermute(targets, "cols", [(0, 1), (1, 0)])
    first = col_pos == 0
    all_targets = jnp.concatenate(
        [jnp.where(first, targets, peer_targets), jnp.where(first, peer_targets, targets)], axis=1
    )

    embedded = jnp.take(points, landmark_index - row_pos * block_points, axis=0)
    own = lax.dynamic_slice_in_dim(embedded, col_pos * quarter, quarter, 0)
    column_emb = to_all(to_all(own, "rows_2"), PLANE).reshape(half_cols, -1)

    emb_sq = squares(embedded)
    col_sq = squares(column_emb)
    row_ids = lax.broadcasted_iota(jnp.int32, (rows_here, half_cols), 0)
    col_ids = lax.broadcasted_iota(jnp.int32, (rows_here, half_cols), 1)
    offset = row_ids - col_pos * quarter
    ridge_hits = (offset >= 0) & (offset < quarter) & (col_ids == row_pos * quarter + offset)
    slab = gaussian(embedded, emb_sq, column_emb, col_sq) + jnp.where(ridge_hits, ridge, 0.0)

    partial = lax.dot_general(
        all_targets, slab, (((0,), (0,)), ((), ())), precision=exact_mode, preferred_element_type=jnp.float32
    )
    projected = summed(summed(partial, PLANE), "rows_2")

    own_heads = column_emb[:PW]
    peer_heads = lax.ppermute(own_heads, "cols", [(0, 1), (1, 0)])
    heads = jnp.concatenate(
        [jnp.where(first, own_heads, peer_heads), jnp.where(first, peer_heads, own_heads)], axis=0
    )
    heads_sq = squares(heads)

    def at_heads(emb, emb_sq, landmark):
        base = gaussian(emb, emb_sq, heads, heads_sq)
        head = lax.broadcasted_iota(jnp.int32, base.shape, 1)
        block, within = head // PW, head % PW
        place = within // quarter * rows_here + block * quarter + within % quarter
        return base + jnp.where(place == landmark[:, None], ridge, 0.0)

    here = row_pos * rows_here + lax.iota(jnp.int32, rows_here)
    column = lax.iota(jnp.int32, half_cols)
    there = column // quarter * rows_here + col_pos * quarter + column % quarter
    head = lax.iota(jnp.int32, 2 * PW)
    head_place = head % PW // quarter * rows_here + head // PW * quarter + head % quarter
    rows_local = at_heads(embedded, emb_sq, here)
    rows_column = at_heads(column_emb, col_sq, there)
    block = at_heads(heads, heads_sq, head_place)

    inv_0 = lower_inverse(block[:PW, :PW])
    corner = dot_t(block[PW:, :PW], inv_0)
    inv_1 = lower_inverse(block[PW:, PW:] - dot_t(corner, corner))

    def panels_of(rows):
        left = dot_t(rows[:, :PW], inv_0)
        right = dot_t(rows[:, PW:] - dot_t(left, corner), inv_1)
        return jnp.concatenate([left, right], axis=1)

    panels = panels_of(rows_local)
    at_columns = panels_of(rows_column[PW:])
    remainder = slab[:, PW:] - dot_t(panels, at_columns)
    return projected, panels, remainder


def solution(mesh):
    split = Mesh(
        mesh.devices.reshape(4, 4, 8, mesh.shape["cols"]), ("rows_0", "rows_1", "rows_2", "cols")
    )
    placed = (P(ROWS, None), P(ROWS), P(ROWS, "cols"), P())
    return jax.shard_map(
        per_device,
        mesh=split,
        in_specs=placed,
        out_specs=(P(ROWS, "cols"), P(ROWS, None), P(ROWS, "cols")),
        check_vma=False,
    )
```

time: 296 us -> 184 us (0.62)
  waiting for transfers between devices: 115 us -> 41.7 us
  blocking collectives: 40.6 us -> 17.8 us
  between operations: 15 us -> 1.69 us
  local copies, waits for them, and re-layouts: 21.9 us -> 10 us
  matrix products: 15.9 us -> 26 us
  other arithmetic: 52.7 us -> 62 us
  starting transfers between devices: 32.3 us -> 24.3 us
    all_gather x1 -> x0, waiting for transfers between devices: 51.2 us -> none  [stacked_from(): pieces = lax.all_gather(pieces, axes[k])]
    all_gather x4 -> x0, blocking collectives: 26 us -> none  [the longest x2 21.2 us: stacked_from(): pieces = lax.all_gather(pieces, axes[k])]
    all_to_all x5 -> x3, waiting for transfers between devices: 64.2 us -> 41.7 us  [the longest x1 36.2 us: to_all(): lax.all_to_all(jnp.broadcast_to(x[None], (peers, *x.shape)), axis, 0, 0,...]
    all_to_all x5 -> x3, starting transfers between devices: 32.2 us -> 17.6 us  [the longest x2 10.7 us: summed(): return lax.all_to_all(pieces, axis, 0, 0, tiled=True).sum(axis=0)]
    dot_general x6 -> x14, matrix products: 14.4 us -> 25.5 us  [the longest x13 22.2 us: dot_t(): lax.dot_general(left, right, (((1,), (1,)), ((), ())), precision=exact_mo...]
    ppermute x0 -> x2, starting transfers between devices: none -> 6.62 us  [the longest x1 3.82 us: per_device(): peer_heads = lax.ppermute(own_heads, 'cols', [(0, 1), (1, 0)])]
    another operation x2 -> x0, local copies, waits for them, and re-layouts: 6.01 us -> none  [in_blocks(): return jnp.moveaxis(x.reshape(*before, peers, -1, *after), dim, 0)]
    another operation x10, other arithmetic: 45.7 us -> 51.3 us  [the longest x6 27.2 us: lower_inverse(): factor = jnp.linalg.cholesky(block)]
  transfers between devices with their start and end apart: 6 -> 5, of which waited for: 5 -> 2; matrix products, arithmetic and copies ran while one was open for 16% -> 48% of each run, Pallas kernels for 0% -> 0%
where the time goes in v1:
time: 184 us; the launch traced here: 183 us
  other arithmetic  62 us (34%)
  waiting for transfers between devices  41.7 us (23%)
  matrix products  26 us (14%)
  starting transfers between devices  24.3 us (13%)
  blocking collectives  17.8 us (10%)
  local copies, waits for them, and re-layouts  10 us (5%)
    all_to_all x1, waiting for transfers between devices, to_all(): lax.all_to_all(jnp.broadcast_to(x[None], (peers, *x.shape)), axis, 0, 0,...  36.2 us
    another operation x6, other arithmetic, lower_inverse(): factor = jnp.linalg.cholesky(block)  27.2 us
    another operation x4, other arithmetic, lower_inverse(): return jax.scipy.linalg.solve_triangular(factor, eye, lower=True)  24.1 us
    dot_general x13, matrix products, dot_t(): lax.dot_general(left, right, (((1,), (1,)), ((), ())), precision=exact_mo...  22.2 us
    all_to_all x1, blocking collectives, to_all(): lax.all_to_all(jnp.broadcast_to(x[None], (peers, *x.shape)), axis, 0, 0,...  17.8 us
    all_to_all x2, starting transfers between devices, summed(): return lax.all_to_all(pieces, axis, 0, 0, tiled=True).sum(axis=0)  10.7 us
    all_to_all x1, starting transfers between devices, to_all(): lax.all_to_all(jnp.broadcast_to(x[None], (peers, *x.shape)), axis, 0, 0,...  6.93 us
    all_to_all x2, waiting for transfers between devices, summed(): return lax.all_to_all(pieces, axis, 0, 0, tiled=True).sum(axis=0)  5.5 us
  transfers between devices with their start and end apart: 5, of which 2 were waited for; matrix products, arithmetic and copies ran while one was open for 48% of the time, Pallas kernels for 0%

profile of v1, /device:TPU:1, one launch (start us, length us, event | category | flops | bytes accessed | tf_op | source)
XLA Modules:
  0.0 183.4 jit_solution(11026743906289882199)
XLA Ops:
  0.7 0.8 compare_and_fusion.3
  1.5 0.6 copy-done
  2.1 1.1 gather_fusion
  3.4 17.8 %all_to_all.20 = f32[8,8,768]{2,1,0:T(8,128)S(1)} all-to-all(f32[8,8,768]{2,1,0:T(8,128)S(1)} %broadcast_in_dim.65), channel_id=1, replica_groups=mesh['rows_0'=4,'rows_1'=4,'rows_2'=8,'cols'=2] {'rows_2'}, dimensions={0} | all-to-all | bytes 393216 | tf_op jit(solution)/shard_map/all_to_all | solution.py:17
  21.2 2.0 %broadcast_in_dim.66 = f32[16,8,8,768]{3,2,1,0:T(8,128)} broadcast(f32[8,8,768]{2,1,0:T(8,128)S(1)} %all_to_all.20), dimensions={1,2,3} | broadcast | bytes 3342336 | tf_op jit(solution)/shard_map/broadcast_in_dim | solution.py:17
  23.2 6.9 %all-to-all-start.1 = ((f32[16,8,8,768]{3,2,1,0:T(8,128)}), f32[16,8,8,768]{3,2,1,0:T(8,128)}, u32[]{:S(2)}, u32[]{:S(2)}) async-start(f32[16,8,8,768]{3,2,1,0:T(8,128)} %broadcast_in_dim.66), calls=%async_computation.1 | async-start | bytes 6291456 | tf_op jit(solution)/shard_map/all_to_all | solution.py:17
  30.2 2.8 %collective-permute-start = (f32[256,256]{1,0:T(8,128)S(1)}, f32[256,256]{1,0:T(8,128)S(1)}, u32[]{:S(2)}, u32[]{:S(2)}) collective-permute-start(f32[256,256]{1,0:T(8,128)S(1)} %copy-done.6), channel_id=1, source_target_pairs={{0,1},{1,0},{2,3},{3,2},{4,5},{5,4},{6,7},{7,6},{8,9},{9,8},{10,11... | collective-permute-start | bytes 786440 | tf_op jit(solution)/shard_map/ppermute | solution.py:57
  33.0 0.6 iota_add_fusion
  34.3 0.9 broadcast_select_fusion.4
  35.2 36.2 %all-to-all-done.1 = f32[16,8,8,768]{3,2,1,0:T(8,128)} async-done(((f32[16,8,8,768]{3,2,1,0:T(8,128)}), f32[16,8,8,768]{3,2,1,0:T(8,128)}, u32[]{:S(2)}, u32[]{:S(2)}) %all-to-all-start.1) | async-done | bytes 3145760 | tf_op jit(solution)/shard_map/all_to_all | solution.py:17
  71.3 1.8 slice.53
  73.1 3.8 %collective-permute-start.1 = (f32[128,768]{1,0:T(8,128)}, f32[128,768]{1,0:T(8,128)}, u32[]{:S(2)}, u32[]{:S(2)}) collective-permute-start(f32[128,768]{1,0:T(8,128)} %bitcast.3), channel_id=1, source_target_pairs={{0,1},{1,0},{2,3},{3,2},{4,5},{5,4},{6,7},{7,6},{8,9},{9,8},{10,11... | collective-permute-start | bytes 1179656 | tf_op jit(solution)/shard_map/ppermute | solution.py:81
  76.9 2.2 %multiply_reduce_fusion = f32[16,8,8]{2,1,0:T(8,128)S(1)} fusion(f32[16,8,8,768]{3,2,1,0:T(8,128)} %all-to-all-done.1), kind=kLoop, calls=%fused_computation.1 | loop fusion | flops 1571840 | bytes 3149824 | tf_op jit(solution)/shard_map/reduce_sum | solution.py:38
  79.2 4.9 %fusion.9 = f32[256,1024]{1,0:T(8,128)S(1)} fusion(f32[256,768]{1,0:T(8,128)S(1)} %get-tuple-element.18, f32[1024,768]{1,0:T(8,128)} %bitcast, f32[]{:T(128)} %bitcast.40, s32[256]{0:T(256)S(1)} %fusion.75, f32[1024]{0:T(1024)S(1)} %add.239, f32[256]{0:T(256)S(1)} %get-tuple-element.17, pred[256]{0:T(512)(128)(4,1)S(1)} %compare_and_fusion.2), kind=kOutput, calls=%fused_computation.21 | convolution fusion | flops 2418278400 | bytes 4987140 | tf_op jit(solution)/shard_map/dot_general | solution.py:27
  84.2 3.2 %fusion.32 = f32[512,1024]{1,0:T(8,128)} fusion(f32[256,1024]{1,0:T(8,128)S(1)} %fusion.9, f32[256,256]{1,0:T(8,128)S(1)} %copy-done.4, f32[256,256]{1,0:T(8,128)S(1)} %copy-done.3), kind=kOutput, calls=%fused_computation.55 | convolution fusion | flops 1610743808 | bytes 3670016 | tf_op jit(solution)/shard_map/dot_general | solution.py:75
  87.4 4.6 %all-to-all-start.2 = ((f32[16,32,1024]{2,1,0:T(8,128)}), f32[16,32,1024]{2,1,0:T(8,128)}, u32[]{:S(2)}, u32[]{:S(2)}) async-start(f32[16,32,1024]{2,1,0:T(8,128)} %bitcast.44), calls=%async_computation.2 | async-start | bytes 4194304 | tf_op jit(solution)/shard_map/all_to_all | solution.py:23
  92.0 1.2 broadcast_select_fusion.2
  93.4 0.5 copy-done.1
  94.0 0.9 fusion.19
  94.9 0.7 copy-done.5
  95.7 0.9 fusion.60
  96.5 11.7 %cholesky.44 = f32[128,128]{1,0:T(8,128)S(1)} custom-call(f32[128,128]{1,0:T(8,128)S(1)} %fusion.60), custom_call_target="Cholesky" | custom-call | tf_op jit(solution)/shard_map/jit(cholesky)/cholesky | solution.py:42
  108.3 0.7 compare_reduce_fusion.1
  109.0 0.6 fusion.53
  109.6 9.8 %custom-call.6 = f32[1,128,128]{1,2,0:T(8,128)S(1)} custom-call(f32[1,128,128]{2,1,0:T(8,128)S(1)} %fusion.53), custom_call_target="InvertDiagBlocksLowerTriangular" | custom-call | tf_op jit(solution)/shard_map/jit(_solve_triangular)/triangular_solve | solution.py:44
  119.5 0.3 fusion.51
  119.7 1.1 fusion.55
  120.9 1.7 slice_subtract_fusion.4
  122.6 1.6 copy.32
  124.2 1.5 fusion.58
  125.7 13.2 %cholesky.55 = f32[128,128]{1,0:T(8,128)} custom-call(f32[128,128]{1,0:T(8,128)} %fusion.58), custom_call_target="Cholesky" | custom-call | tf_op jit(solution)/shard_map/jit(cholesky)/cholesky | solution.py:42
  138.9 0.9 select_reduce_fusion
  139.7 0.7 compare_reduce_fusion
  140.4 2.2 %fusion.54 = f32[1,128,128]{2,1,0:T(8,128)} fusion(f32[128,128]{1,0:T(8,128)} %cholesky.55, pred[]{:T(512)} %compare_reduce_fusion), kind=kLoop, calls=%fused_computation.91 | loop fusion | flops 65536 | bytes 131073 | tf_op jit(solution)/shard_map/jit(_solve_triangular)/triangular_solve | solution.py:44
  142.6 11.4 %custom-call.7 = f32[1,128,128]{1,2,0:T(8,128)} custom-call(f32[1,128,128]{2,1,0:T(8,128)} %fusion.54), custom_call_target="InvertDiagBlocksLowerTriangular" | custom-call | tf_op jit(solution)/shard_map/jit(_solve_triangular)/triangular_solve | solution.py:44
  154.1 2.1 %fusion.15 = f32[256,256]{0,1:T(8,128)S(1)} fusion(f32[256,768]{1,0:T(8,128)S(1)} %get-tuple-element.18, f32[128,768]{1,0:T(8,128)} %copy-done.2, f32[128,768]{1,0:T(8,128)} %copy-done.1, f32[]{:T(128)} %bitcast.41, s32[256]{0:T(256)} %iota_add_fusion, f32[256]{0:T(256)S(1)} %multiply_reduce_fusion.1, f32[256]{0:T(256)S(1)} %get-tuple-element.17, ...), kind=kOutput, calls=%fused_computation.30 | convolution fusion | flops 606339072 | bytes 1842692 | tf_op jit(solution)/shard_map/dot_general | solution.py:27
  156.4 0.3 fusion.49
  157.3 0.8 copy.33
  158.1 4.8 %fusion.4 = f32[1024,256]{1,0:T(8,128)S(1)} fusion(f32[1024,768]{1,0:T(8,128)} %bitcast, f32[]{:T(128)} %bitcast.42, s32[1024]{0:T(1024)S(1)} %fusion.69, s32[256]{0:T(256)} %copy-done.8, s32[256]{0:T(256)} %copy-done.11, s32[256]{0:T(256)} %copy-done.9, s32[256]{0:T(256)} %copy-done.10, f32[256]{0:T(256)S(1)} %multiply_reduce_fusion.1, ...), kind=kOutput, calls=%fused_computation.15 | convolution fusion | flops 2424766464 | bytes 4994564 | tf_op jit(solution)/shard_map/dot_general | solution.py:27
  162.9 0.6 fusion.37
  163.5 0.9 fusion.83
  164.4 1.4 fusion.36
  165.8 1.7 reduce_sum.47
  167.6 0.7 reshape.114
  168.2 6.1 %all-to-all-start.3 = ((f32[8,4,1024]{2,1,0:T(4,128)}), f32[8,4,1024]{2,1,0:T(4,128)S(1)}, u32[]{:S(2)}, u32[]{:S(2)}) async-start(f32[8,4,1024]{2,1,0:T(4,128)} %reshape.114), calls=%async_computation.3 | async-start | bytes 262144 | tf_op jit(solution)/shard_map/all_to_all | solution.py:23
  174.3 3.0 %convolution_subtract_fusion = f32[256,896]{1,0:T(8,128)} fusion(f32[256,1024]{1,0:T(8,128)S(1)} %fusion.9, f32[896,128]{0,1:T(8,128)} %fusion.36, f32[896,128]{0,1:T(8,128)S(1)} %fusion.37, f32[256,128]{0,1:T(8,128)S(1)} %fusion.46, f32[256,128]{0,1:T(8,128)S(1)} %fusion.47), kind=kOutput, calls=%fused_computation.22 | convolution fusion | flops 705167360 | bytes 3014656 | tf_op jit(solution)/shard_map/dot_general | solution.py:27
  177.3 5.5 %all-to-all-done.3 = f32[8,4,1024]{2,1,0:T(4,128)S(1)} async-done(((f32[8,4,1024]{2,1,0:T(4,128)}), f32[8,4,1024]{2,1,0:T(4,128)S(1)}, u32[]{:S(2)}, u32[]{:S(2)}) %all-to-all-start.3) | async-done | bytes 131104 | tf_op jit(solution)/shard_map/all_to_all | solution.py:23
  182.8 0.6 reduce_sum.48
  (48 shorter events, 1.6 us)
Async XLA Ops:
  0.6 1.4 copy-start
  23.2 6.9 %copy-start.6 = (f32[256,256]{1,0:T(8,128)S(1)}, f32[256,256]{1,0:T(8,128)}, u32[]{:S(2)}) copy-start(f32[256,256]{1,0:T(8,128)} %param.9) | copy-start | bytes 786436
  23.2 48.1 %all-to-all-start.1 = ((f32[16,8,8,768]{3,2,1,0:T(8,128)}), f32[16,8,8,768]{3,2,1,0:T(8,128)}, u32[]{:S(2)}, u32[]{:S(2)}) async-start(f32[16,8,8,768]{3,2,1,0:T(8,128)} %broadcast_in_dim.66), calls=%async_computation.1 | async-start | bytes 6291456 | tf_op jit(solution)/shard_map/all_to_all | solution.py:17
  30.2 4.1 %collective-permute-start = (f32[256,256]{1,0:T(8,128)S(1)}, f32[256,256]{1,0:T(8,128)S(1)}, u32[]{:S(2)}, u32[]{:S(2)}) collective-permute-start(f32[256,256]{1,0:T(8,128)S(1)} %copy-done.6), channel_id=1, source_target_pairs={{0,1},{1,0},{2,3},{3,2},{4,5},{5,4},{6,7},{7,6},{8,9},{9,8},{10,11... | collective-permute-start | bytes 786440 | tf_op jit(solution)/shard_map/ppermute | solution.py:57
  33.0 60.4 %copy-start.12 = (pred[256]{0:T(512)(128)(4,1)}, pred[256]{0:T(512)(128)(4,1)S(1)}, u32[]{:S(2)}) copy-start(pred[256]{0:T(512)(128)(4,1)S(1)} %get-tuple-element.27) | copy-start | bytes 772
  33.0 60.4 %copy-start.13 = (pred[256]{0:T(512)(128)(4,1)}, pred[256]{0:T(512)(128)(4,1)S(1)}, u32[]{:S(2)}) copy-start(pred[256]{0:T(512)(128)(4,1)S(1)} %get-tuple-element.28) | copy-start | bytes 772
  33.6 59.8 %copy-start.8 = (s32[256]{0:T(256)}, s32[256]{0:T(256)S(1)}, u32[]{:S(2)}) copy-start(s32[256]{0:T(256)S(1)} %get-tuple-element.25) | copy-start | bytes 3076
  33.6 59.8 %copy-start.9 = (s32[256]{0:T(256)}, s32[256]{0:T(256)S(1)}, u32[]{:S(2)}) copy-start(s32[256]{0:T(256)S(1)} %get-tuple-element.26) | copy-start | bytes 3076
  34.3 59.2 %copy-start.10 = (s32[256]{0:T(256)}, s32[256]{0:T(256)S(1)}, u32[]{:S(2)}) copy-start(s32[256]{0:T(256)S(1)} %get-tuple-element.29) | copy-start | bytes 3076
  34.3 59.2 %copy-start.11 = (s32[256]{0:T(256)}, s32[256]{0:T(256)S(1)}, u32[]{:S(2)}) copy-start(s32[256]{0:T(256)S(1)} %get-tuple-element.30) | copy-start | bytes 3076
  73.1 18.9 %collective-permute-start.1 = (f32[128,768]{1,0:T(8,128)}, f32[128,768]{1,0:T(8,128)}, u32[]{:S(2)}, u32[]{:S(2)}) collective-permute-start(f32[128,768]{1,0:T(8,128)} %bitcast.3), channel_id=1, source_target_pairs={{0,1},{1,0},{2,3},{3,2},{4,5},{5,4},{6,7},{7,6},{8,9},{9,8},{10,11... | collective-permute-start | bytes 1179656 | tf_op jit(solution)/shard_map/ppermute | solution.py:81
  79.2 5.0 %copy-start.3 = (f32[256,256]{1,0:T(8,128)S(1)}, f32[256,256]{1,0:T(8,128)}, u32[]{:S(2)}) copy-start(f32[256,256]{1,0:T(8,128)} %get-tuple-element.23) | copy-start | bytes 786436
  79.2 5.0 %copy-start.4 = (f32[256,256]{1,0:T(8,128)S(1)}, f32[256,256]{1,0:T(8,128)}, u32[]{:S(2)}) copy-start(f32[256,256]{1,0:T(8,128)} %get-tuple-element.24) | copy-start | bytes 786436
  87.4 78.4 %all-to-all-start.2 = ((f32[16,32,1024]{2,1,0:T(8,128)}), f32[16,32,1024]{2,1,0:T(8,128)}, u32[]{:S(2)}, u32[]{:S(2)}) async-start(f32[16,32,1024]{2,1,0:T(8,128)} %bitcast.44), calls=%async_computation.2 | async-start | bytes 4194304 | tf_op jit(solution)/shard_map/all_to_all | solution.py:23
  93.2 0.7 copy-start.1
  93.2 1.6 copy-start.2
  94.9 0.7 copy-start.5
  154.1 2.3 %copy-start.7 = (f32[1,128,128]{1,2,0:T(8,128)S(1)}, f32[1,128,128]{1,2,0:T(8,128)}, u32[]{:S(2)}) copy-start(f32[1,128,128]{1,2,0:T(8,128)} %custom-call.7) | copy-start | bytes 196612
  168.2 14.6 %all-to-all-start.3 = ((f32[8,4,1024]{2,1,0:T(4,128)}), f32[8,4,1024]{2,1,0:T(4,128)S(1)}, u32[]{:S(2)}, u32[]{:S(2)}) async-start(f32[8,4,1024]{2,1,0:T(4,128)} %reshape.114), calls=%async_computation.3 | async-start | bytes 262144 | tf_op jit(solution)/shard_map/all_to_all | solution.py:23

commit v2 on v1

--- a/solution.py
+++ b/solution.py
@@ -1,6 +1,7 @@
 import jax
 import jax.numpy as jnp
 from jax import lax
+from jax.experimental import pallas as pl
 from jax.sharding import Mesh
 from jax.sharding import PartitionSpec as P
 
@@ -8,6 +9,7 @@
 PW = 128
 ROWS = ("rows_0", "rows_1", "rows_2")
 PLANE = ("rows_0", "rows_1")
+SUB = 8
 
 exact_mode = lax.Precision.HIGHEST
 
@@ -38,10 +40,58 @@
     return jnp.sum(x * x, axis=1)
 
 
-def lower_inverse(block):
-    factor = jnp.linalg.cholesky(block)
-    eye = jnp.eye(PW, dtype=jnp.float32)
-    return jax.scipy.linalg.solve_triangular(factor, eye, lower=True)
+def inverse_factor(rows):
+    groups = len(rows)
+    ids = lax.broadcasted_iota(jnp.int32, (SUB, PW), 0)
+    lanes = lax.broadcasted_iota(jnp.int32, (SUB, PW), 1)
+    inv = [jnp.where(lanes == ids + SUB * g, 1.0, 0.0).astype(jnp.float32) for g in range(groups)]
+    for b in range(groups):
+        cols = [
+            [jnp.broadcast_to(rows[i][:, SUB * b + j : SUB * b + j + 1], (SUB, PW)) for i in range(b, groups)]
+            for j in range(SUB)
+        ]
+        head, inv_head = rows[b], inv[b]
+        steps = []
+        for k in range(SUB):
+            spread = [jnp.broadcast_to(cols[k][0][j : j + 1], (SUB, PW)) for j in range(k, SUB)]
+            scale = lax.rsqrt(spread[0])
+            row = jnp.broadcast_to(head[k : k + 1], (SUB, PW)) * scale
+            inv_row = jnp.broadcast_to(inv_head[k : k + 1], (SUB, PW)) * scale
+            mult = [c * scale for c in cols[k]]
+            mult[0] = jnp.where(ids > k, mult[0], 0.0)
+            for j in range(k + 1, SUB):
+                there = spread[j - k] * scale
+                cols[j] = [c - m * there for c, m in zip(cols[j], mult)]
+            head = head - mult[0] * row
+            inv_head = jnp.where(ids == k, inv_row, inv_head - mult[0] * inv_row)
+            steps.append((row, inv_row, mult))
+        inv[b] = inv_head
+        for i in range(b + 1, groups):
+            for row, inv_row, mult in steps:
+                rows[i] = rows[i] - mult[i - b] * row
+                inv[i] = inv[i] - mult[i - b] * inv_row
+    return inv
+
+
+def factor_kernel(block_ref, first_ref, corner_ref, second_ref):
+    def factor_into(block, out_ref):
+        inv = inverse_factor([block[SUB * g : SUB * g + SUB] for g in range(PW // SUB)])
+        for g, rows in enumerate(inv):
+            out_ref[SUB * g : SUB * g + SUB, :] = rows
+
+    factor_into(block_ref[:PW, :PW], first_ref)
+    corner = dot_t(block_ref[PW:, :PW], first_ref[...])
+    corner_ref[...] = corner
+    factor_into(block_ref[PW:, PW:] - dot_t(corner, corner), second_ref)
+
+
+def factors(block):
+    shape = jax.ShapeDtypeStruct((PW, PW), jnp.float32)
+    return pl.pallas_call(
+        factor_kernel,
+        out_shape=(shape,) * 3,
+        cost_estimate=pl.CostEstimate(flops=20_000_000, bytes_accessed=500_000, transcendentals=256),
+    )(block)
 
 
 def per_device(points, landmark_index, targets, ridge_shift):
@@ -100,9 +150,7 @@
     rows_column = at_heads(column_emb, col_sq, there)
     block = at_heads(heads, heads_sq, head_place)
 
-    inv_0 = lower_inverse(block[:PW, :PW])
-    corner = dot_t(block[PW:, :PW], inv_0)
-    inv_1 = lower_inverse(block[PW:, PW:] - dot_t(corner, corner))
+    inv_0, corner, inv_1 = factors(block)
 
     def panels_of(rows):
         left = dot_t(rows[:, :PW], inv_0)

time: 184 us -> 143 us (0.78)
  other arithmetic: 62 us -> 8.36 us
  Pallas kernels: 0 us -> 10.3 us
  waiting for transfers between devices: 41.7 us -> 48.8 us
  matrix products: 26 us -> 23.6 us
  local copies, waits for them, and re-layouts: 10 us -> 7.8 us
    another operation x10 -> x0, other arithmetic: 51.3 us -> none  [the longest x6 27.2 us: lower_inverse(): factor = jnp.linalg.cholesky(block)]
    pallas_call x0 -> x1, Pallas kernels: none -> 10.3 us  [factors(): pl.pallas_call(factor_kernel, out_shape=(shape,) * 3, cost_estimate=pl.Co...]
    all_to_all x2, waiting for transfers between devices: 5.5 us -> 12.7 us  [summed(): return lax.all_to_all(pieces, axis, 0, 0, tiled=True).sum(axis=0)]
    div x2 -> x0, other arithmetic: 2.36 us -> none  [lower_inverse(): factor = jnp.linalg.cholesky(block)]
    dot_general x13 -> x11, matrix products: 22.2 us -> 20.4 us  [dot_t(): lax.dot_general(left, right, (((1,), (1,)), ((), ())), precision=exact_mo...]
  transfers between devices with their start and end apart: 5 -> 5, of which waited for: 2 -> 3; matrix products, arithmetic and copies ran while one was open for 48% -> 21% of each run, Pallas kernels for 0% -> 7%
where the time goes in v2:
time: 143 us
  waiting for transfers between devices  48.8 us (34%)
  starting transfers between devices  24.3 us (17%)
  matrix products  23.6 us (17%)
  blocking collectives  17.8 us (12%)
  Pallas kernels  10.3 us (7%)
  other arithmetic  8.36 us (6%)
  local copies, waits for them, and re-layouts  7.8 us (5%)
  between operations  1.64 us (1%)
    all_to_all x1, waiting for transfers between devices, to_all(): lax.all_to_all(jnp.broadcast_to(x[None], (peers, *x.shape)), axis, 0, 0,...  36.2 us
    dot_general x11, matrix products, dot_t(): lax.dot_general(left, right, (((1,), (1,)), ((), ())), precision=exact_mo...  20.4 us
    all_to_all x1, blocking collectives, to_all(): lax.all_to_all(jnp.broadcast_to(x[None], (peers, *x.shape)), axis, 0, 0,...  17.8 us
    all_to_all x2, waiting for transfers between devices, summed(): return lax.all_to_all(pieces, axis, 0, 0, tiled=True).sum(axis=0)  12.7 us
    all_to_all x2, starting transfers between devices, summed(): return lax.all_to_all(pieces, axis, 0, 0, tiled=True).sum(axis=0)  10.7 us
    pallas_call x1, Pallas kernels, factors(): pl.pallas_call(factor_kernel, out_shape=(shape,) * 3, cost_estimate=pl.Co...  10.3 us
    all_to_all x1, starting transfers between devices, to_all(): lax.all_to_all(jnp.broadcast_to(x[None], (peers, *x.shape)), axis, 0, 0,...  6.93 us
    ppermute x1, starting transfers between devices, per_device(): peer_heads = lax.ppermute(own_heads, 'cols', [(0, 1), (1, 0)])  3.82 us
  transfers between devices with their start and end apart: 5, of which 3 were waited for; matrix products, arithmetic and copies ran while one was open for 21% of the time, Pallas kernels for 7%

profile of v2, /device:TPU:1, one launch (start us, length us, event | category | flops | bytes accessed | tf_op | source)
XLA Modules:
  0.0 142.6 jit_solution(10062041513238230626)
XLA Ops:
  0.6 0.0 copy-start
  0.7 0.8 compare_and_fusion.3
  1.5 0.6 copy-done
  2.1 1.1 gather_fusion
  3.2 0.2 multiply_reduce_fusion.2
  3.4 17.8 %all_to_all.20 = f32[8,8,768]{2,1,0:T(8,128)S(1)} all-to-all(f32[8,8,768]{2,1,0:T(8,128)S(1)} %broadcast_in_dim.64), channel_id=1, replica_groups=mesh['rows_0'=4,'rows_1'=4,'rows_2'=8,'cols'=2] {'rows_2'}, dimensions={0} | all-to-all | bytes 393216 | tf_op jit(solution)/shard_map/all_to_all | solution.py:19
  21.2 2.0 %broadcast_in_dim.65 = f32[16,8,8,768]{3,2,1,0:T(8,128)} broadcast(f32[8,8,768]{2,1,0:T(8,128)S(1)} %all_to_all.20), dimensions={1,2,3} | broadcast | bytes 3342336 | tf_op jit(solution)/shard_map/broadcast_in_dim | solution.py:19
  23.2 6.9 %all-to-all-start.1 = ((f32[16,8,8,768]{3,2,1,0:T(8,128)}), f32[16,8,8,768]{3,2,1,0:T(8,128)}, u32[]{:S(2)}, u32[]{:S(2)}) async-start(f32[16,8,8,768]{3,2,1,0:T(8,128)} %broadcast_in_dim.65), calls=%async_computation.1 | async-start | bytes 6291456 | tf_op jit(solution)/shard_map/all_to_all | solution.py:19
  30.2 2.8 %collective-permute-start = (f32[256,256]{1,0:T(8,128)S(1)}, f32[256,256]{1,0:T(8,128)S(1)}, u32[]{:S(2)}, u32[]{:S(2)}) collective-permute-start(f32[256,256]{1,0:T(8,128)S(1)} %copy-done.6), channel_id=1, source_target_pairs={{0,1},{1,0},{2,3},{3,2},{4,5},{5,4},{6,7},{7,6},{8,9},{9,8},{10,11... | collective-permute-start | bytes 786440 | tf_op jit(solution)/shard_map/ppermute | solution.py:107
  33.0 0.0 copy-start.15
  33.0 0.6 iota_add_fusion
  34.3 0.0 collective-permute-done
  34.3 0.9 broadcast_select_fusion.4
  35.2 36.2 %all-to-all-done.1 = f32[16,8,8,768]{3,2,1,0:T(8,128)} async-done(((f32[16,8,8,768]{3,2,1,0:T(8,128)}), f32[16,8,8,768]{3,2,1,0:T(8,128)}, u32[]{:S(2)}, u32[]{:S(2)}) %all-to-all-start.1) | async-done | bytes 3145760 | tf_op jit(solution)/shard_map/all_to_all | solution.py:19
  71.3 1.8 %slice.33 = f32[2,8,8,768]{3,2,1,0:T(8,128)} slice(f32[16,8,8,768]{3,2,1,0:T(8,128)} %all-to-all-done.1), slice={[0:2], [0:8], [0:8], [0:768]} | slice | bytes 786432 | tf_op jit(solution)/shard_map/slice | solution.py:130
  73.1 3.8 %collective-permute-start.1 = (f32[128,768]{1,0:T(8,128)}, f32[128,768]{1,0:T(8,128)}, u32[]{:S(2)}, u32[]{:S(2)}) collective-permute-start(f32[128,768]{1,0:T(8,128)} %bitcast.3), channel_id=1, source_target_pairs={{0,1},{1,0},{2,3},{3,2},{4,5},{5,4},{6,7},{7,6},{8,9},{9,8},{10,11... | collective-permute-start | bytes 1179656 | tf_op jit(solution)/shard_map/ppermute | solution.py:131
  76.9 2.2 %multiply_reduce_fusion = f32[16,8,8]{2,1,0:T(8,128)S(1)} fusion(f32[16,8,8,768]{3,2,1,0:T(8,128)} %all-to-all-done.1), kind=kLoop, calls=%fused_computation.1 | loop fusion | flops 1571840 | bytes 3149824 | tf_op jit(solution)/shard_map/reduce_sum | solution.py:40
  79.1 0.1 add.230
  79.2 0.0 copy-start.3
  79.2 4.9 %fusion.9 = f32[256,1024]{1,0:T(8,128)S(1)} fusion(f32[256,768]{1,0:T(8,128)S(1)} %get-tuple-element.22, f32[1024,768]{1,0:T(8,128)} %bitcast, f32[]{:T(128)} %bitcast.19, s32[256]{0:T(256)S(1)} %fusion.63, f32[1024]{0:T(1024)S(1)} %add.230, f32[256]{0:T(256)S(1)} %get-tuple-element.21, pred[256]{0:T(512)(128)(4,1)S(1)} %compare_and_fusion.2), kind=kOutput, calls=%fused_computation.21 | convolution fusion | flops 2418278400 | bytes 4987140 | tf_op jit(solution)/shard_map/dot_general | solution.py:29
  84.2 3.2 %fusion.32 = f32[512,1024]{1,0:T(8,128)} fusion(f32[256,1024]{1,0:T(8,128)S(1)} %fusion.9, f32[256,256]{1,0:T(8,128)S(1)} %copy-done.4, f32[256,256]{1,0:T(8,128)S(1)} %copy-done.3), kind=kOutput, calls=%fused_computation.55 | convolution fusion | flops 1610743808 | bytes 3670016 | tf_op jit(solution)/shard_map/dot_general | solution.py:125
  87.4 4.6 %all-to-all-start.2 = ((f32[16,32,1024]{2,1,0:T(8,128)}), f32[16,32,1024]{2,1,0:T(8,128)}, u32[]{:S(2)}, u32[]{:S(2)}) async-start(f32[16,32,1024]{2,1,0:T(8,128)} %bitcast.23), calls=%async_computation.2 | async-start | bytes 4194304 | tf_op jit(solution)/shard_map/all_to_all | solution.py:25
  92.1 0.0 collective-permute-done.1
  92.1 1.2 broadcast_select_fusion.2
  93.2 0.0 copy-start.2
  93.3 0.1 multiply_reduce_fusion.1
  93.4 0.0 copy-done.15
  93.4 0.0 copy-done.10
  93.5 0.5 copy-done.1
  94.0 0.1 copy-done.2
  94.1 1.6 %fusion.19.block_ref = f32[256,256]{1,0:T(8,128)} fusion(f32[128,768]{1,0:T(8,128)S(1)} %get-tuple-element.26, f32[128,768]{1,0:T(8,128)S(1)} %get-tuple-element.25, s32[256]{0:T(256)S(1)} %fusion.62, f32[256]{0:T(256)S(1)} %multiply_reduce_fusion.1, f32[]{:T(128)} %bitcast.22, s32[256]{0:T(256)S(1)} %get-tuple-element.29, s32[256]{0:T(256)S(1)} %get-tuple-element.34, ...), kind=kOutput, calls=%fused_computation.34 | convolution fusion | flops 606339072 | bytes 1055236 | tf_op jit(solution)/shard_map/dot_general | solution.py:29
  95.7 10.3 %shard_map.67 = (f32[128,128]{1,0:T(8,128)}, f32[128,128]{1,0:T(8,128)}, f32[128,128]{1,0:T(8,128)}) custom-call(f32[256,256]{1,0:T(8,128)} %fusion.19.block_ref), custom_call_target="tpu_custom_call" | custom-call | flops 20000000 | bytes 500000 | tf_op jit(solution)/shard_map/pallas_call | solution.py:90
  105.9 2.0 %fusion.15 = f32[256,256]{1,0:T(8,128)S(1)} fusion(f32[256,768]{1,0:T(8,128)S(1)} %get-tuple-element.22, f32[128,768]{1,0:T(8,128)} %copy-done.2, f32[128,768]{1,0:T(8,128)} %copy-done.1, f32[]{:T(128)} %bitcast.20, s32[256]{0:T(256)} %iota_add_fusion, f32[256]{0:T(256)S(1)} %multiply_reduce_fusion.1, f32[256]{0:T(256)S(1)} %get-tuple-element.21, ...), kind=kOutput, calls=%fused_computation.30 | convolution fusion | flops 606339072 | bytes 1842692 | tf_op jit(solution)/shard_map/dot_general | solution.py:29
  108.0 0.3 fusion.47
  108.3 0.4 fusion.70
  108.7 0.3 fusion.46
  109.0 0.8 copy.11
  109.8 5.0 %fusion.4 = f32[1024,256]{1,0:T(8,128)S(1)} fusion(f32[1024,768]{1,0:T(8,128)} %bitcast, f32[]{:T(128)} %bitcast.21, s32[1024]{0:T(1024)S(1)} %fusion.57, s32[256]{0:T(256)} %copy-done.10, s32[256]{0:T(256)} %copy-done.13, s32[256]{0:T(256)} %copy-done.11, s32[256]{0:T(256)} %copy-done.12, f32[256]{0:T(256)S(1)} %multiply_reduce_fusion.1, ...), kind=kOutput, calls=%fused_computation.15 | convolution fusion | flops 2424766464 | bytes 4994564 | tf_op jit(solution)/shard_map/dot_general | solution.py:29
  114.9 0.6 fusion.37
  115.5 0.9 fusion.71
  116.4 1.4 fusion.36
  117.8 7.8 %all-to-all-done.2 = f32[16,32,1024]{2,1,0:T(8,128)} async-done(((f32[16,32,1024]{2,1,0:T(8,128)}), f32[16,32,1024]{2,1,0:T(8,128)}, u32[]{:S(2)}, u32[]{:S(2)}) %all-to-all-start.2) | async-done | bytes 2097184 | tf_op jit(solution)/shard_map/all_to_all | solution.py:25
  125.6 1.7 %reduce_sum.47 = f32[32,1024]{1,0:T(8,128)S(1)} reduce(f32[16,32,1024]{2,1,0:T(8,128)} %all-to-all-done.2, f32[]{:T(128)} %constant.194.clone.1), dimensions={0}, to_apply=%region_2.3 | reduce | flops 491520 | bytes 2228228 | tf_op jit(solution)/shard_map/reduce_sum | solution.py:25
  127.3 0.7 reshape.106
  128.0 6.1 %all-to-all-start.3 = ((f32[8,4,1024]{2,1,0:T(4,128)}), f32[8,4,1024]{2,1,0:T(4,128)S(1)}, u32[]{:S(2)}, u32[]{:S(2)}) async-start(f32[8,4,1024]{2,1,0:T(4,128)} %reshape.106), calls=%async_computation.3 | async-start | bytes 262144 | tf_op jit(solution)/shard_map/all_to_all | solution.py:25
  134.1 3.0 %convolution_subtract_fusion = f32[256,896]{1,0:T(8,128)} fusion(f32[256,1024]{1,0:T(8,128)S(1)} %fusion.9, f32[896,128]{0,1:T(8,128)} %fusion.36, f32[896,128]{0,1:T(8,128)S(1)} %fusion.37, f32[256,128]{0,1:T(8,128)S(1)} %fusion.46, f32[256,128]{0,1:T(8,128)S(1)} %fusion.47), kind=kOutput, calls=%fused_computation.22 | convolution fusion | flops 705167360 | bytes 3014656 | tf_op jit(solution)/shard_map/dot_general | solution.py:29
  137.1 4.9 %all-to-all-done.3 = f32[8,4,1024]{2,1,0:T(4,128)S(1)} async-done(((f32[8,4,1024]{2,1,0:T(4,128)}), f32[8,4,1024]{2,1,0:T(4,128)S(1)}, u32[]{:S(2)}, u32[]{:S(2)}) %all-to-all-start.3) | async-done | bytes 131104 | tf_op jit(solution)/shard_map/all_to_all | solution.py:25
  142.0 0.6 reduce_sum.48
  (34 shorter events, 0.1 us)
Async XLA Ops:
  0.6 1.4 %copy-start = (f32[512,768]{1,0:T(8,128)S(1)}, f32[512,768]{1,0:T(8,128)}, u32[]{:S(2)}) copy-start(f32[512,768]{1,0:T(8,128)} %param.4) | copy-start | bytes 4718596
  23.2 6.9 %copy-start.6 = (f32[256,256]{1,0:T(8,128)S(1)}, f32[256,256]{1,0:T(8,128)}, u32[]{:S(2)}) copy-start(f32[256,256]{1,0:T(8,128)} %param.6) | copy-start | bytes 786436
  23.2 48.1 %all-to-all-start.1 = ((f32[16,8,8,768]{3,2,1,0:T(8,128)}), f32[16,8,8,768]{3,2,1,0:T(8,128)}, u32[]{:S(2)}, u32[]{:S(2)}) async-start(f32[16,8,8,768]{3,2,1,0:T(8,128)} %broadcast_in_dim.65), calls=%async_computation.1 | async-start | bytes 6291456 | tf_op jit(solution)/shard_map/all_to_all | solution.py:19
  30.2 4.1 %collective-permute-start = (f32[256,256]{1,0:T(8,128)S(1)}, f32[256,256]{1,0:T(8,128)S(1)}, u32[]{:S(2)}, u32[]{:S(2)}) collective-permute-start(f32[256,256]{1,0:T(8,128)S(1)} %copy-done.6), channel_id=1, source_target_pairs={{0,1},{1,0},{2,3},{3,2},{4,5},{5,4},{6,7},{7,6},{8,9},{9,8},{10,11... | collective-permute-start | bytes 786440 | tf_op jit(solution)/shard_map/ppermute | solution.py:107
  33.0 60.4 %copy-start.14 = (pred[256]{0:T(512)(128)(4,1)}, pred[256]{0:T(512)(128)(4,1)S(1)}, u32[]{:S(2)}) copy-start(pred[256]{0:T(512)(128)(4,1)S(1)} %get-tuple-element.31) | copy-start | bytes 772
  33.0 60.4 %copy-start.15 = (pred[256]{0:T(512)(128)(4,1)}, pred[256]{0:T(512)(128)(4,1)S(1)}, u32[]{:S(2)}) copy-start(pred[256]{0:T(512)(128)(4,1)S(1)} %get-tuple-element.32) | copy-start | bytes 772
  33.6 59.8 %copy-start.10 = (s32[256]{0:T(256)}, s32[256]{0:T(256)S(1)}, u32[]{:S(2)}) copy-start(s32[256]{0:T(256)S(1)} %get-tuple-element.29) | copy-start | bytes 3076
  33.6 59.8 %copy-start.11 = (s32[256]{0:T(256)}, s32[256]{0:T(256)S(1)}, u32[]{:S(2)}) copy-start(s32[256]{0:T(256)S(1)} %get-tuple-element.30) | copy-start | bytes 3076
  34.3 59.2 %copy-start.12 = (s32[256]{0:T(256)}, s32[256]{0:T(256)S(1)}, u32[]{:S(2)}) copy-start(s32[256]{0:T(256)S(1)} %get-tuple-element.33) | copy-start | bytes 3076
  34.3 59.2 %copy-start.13 = (s32[256]{0:T(256)}, s32[256]{0:T(256)S(1)}, u32[]{:S(2)}) copy-start(s32[256]{0:T(256)S(1)} %get-tuple-element.34) | copy-start | bytes 3076
  73.1 19.0 %collective-permute-start.1 = (f32[128,768]{1,0:T(8,128)}, f32[128,768]{1,0:T(8,128)}, u32[]{:S(2)}, u32[]{:S(2)}) collective-permute-start(f32[128,768]{1,0:T(8,128)} %bitcast.3), channel_id=1, source_target_pairs={{0,1},{1,0},{2,3},{3,2},{4,5},{5,4},{6,7},{7,6},{8,9},{9,8},{10,11... | collective-permute-start | bytes 1179656 | tf_op jit(solution)/shard_map/ppermute | solution.py:131
  79.2 5.0 %copy-start.3 = (f32[256,256]{1,0:T(8,128)S(1)}, f32[256,256]{1,0:T(8,128)}, u32[]{:S(2)}) copy-start(f32[256,256]{1,0:T(8,128)} %get-tuple-element.27) | copy-start | bytes 786436
  79.2 5.0 %copy-start.4 = (f32[256,256]{1,0:T(8,128)S(1)}, f32[256,256]{1,0:T(8,128)}, u32[]{:S(2)}) copy-start(f32[256,256]{1,0:T(8,128)} %get-tuple-element.28) | copy-start | bytes 786436
  87.4 38.2 %all-to-all-start.2 = ((f32[16,32,1024]{2,1,0:T(8,128)}), f32[16,32,1024]{2,1,0:T(8,128)}, u32[]{:S(2)}, u32[]{:S(2)}) async-start(f32[16,32,1024]{2,1,0:T(8,128)} %bitcast.23), calls=%async_computation.2 | async-start | bytes 4194304 | tf_op jit(solution)/shard_map/all_to_all | solution.py:25
  93.2 0.7 copy-start.1
  93.2 0.9 copy-start.2
  105.9 2.0 %copy-start.8 = (f32[128,128]{1,0:T(8,128)S(1)}, f32[128,128]{1,0:T(8,128)}, u32[]{:S(2)}) copy-start(f32[128,128]{1,0:T(8,128)} %get-tuple-element.6) | copy-start | bytes 196612
  105.9 2.3 %copy-start.7 = (f32[128,128]{1,0:T(8,128)S(1)}, f32[128,128]{1,0:T(8,128)}, u32[]{:S(2)}) copy-start(f32[128,128]{1,0:T(8,128)} %get-tuple-element.7) | copy-start | bytes 196612
  105.9 2.7 %copy-start.5 = (f32[128,128]{1,0:T(8,128)S(1)}, f32[128,128]{1,0:T(8,128)}, u32[]{:S(2)}) copy-start(f32[128,128]{1,0:T(8,128)} %get-tuple-element.8) | copy-start | bytes 196612
  109.8 5.0 %copy-start.9 = (f32[128,128]{1,0:T(8,128)S(1)}, f32[128,128]{1,0:T(8,128)}, u32[]{:S(2)}) copy-start(f32[128,128]{1,0:T(8,128)} %get-tuple-element.6) | copy-start | bytes 196612
  128.0 14.0 %all-to-all-start.3 = ((f32[8,4,1024]{2,1,0:T(4,128)}), f32[8,4,1024]{2,1,0:T(4,128)S(1)}, u32[]{:S(2)}, u32[]{:S(2)}) async-start(f32[8,4,1024]{2,1,0:T(4,128)} %reshape.106), calls=%async_computation.3 | async-start | bytes 262144 | tf_op jit(solution)/shard_map/all_to_all | solution.py:25

commit v3 on v2

v3 whole, which is shorter than its diff:
```python
import jax
import jax.numpy as jnp
from jax import lax
from jax.experimental import pallas as pl
from jax.experimental.pallas import tpu as pltpu
from jax.sharding import Mesh
from jax.sharding import PartitionSpec as P


C = 2048
PW = 128
Y = ("half", "near")
PLANE = ("half", "near", "x")
NEAR = ("near", "x")
ROWS = ("half", "near", "x", "z")
SUB = 8

exact_mode = lax.Precision.HIGHEST


def to_all(x, axis):
    peers = lax.axis_size(axis)
    return lax.all_to_all(jnp.broadcast_to(x[None], (peers, *x.shape)), axis, 0, 0, tiled=True)


def dot_t(left, right):
    return lax.dot_general(
        left, right, (((1,), (1,)), ((), ())), precision=exact_mode, preferred_element_type=jnp.float32
    )


def gaussian(left, left_sq, right, right_sq):
    cross = dot_t(left, right)
    return jnp.exp(-(left_sq[:, None] + right_sq[None, :] - 2.0 * cross) / (2.0 * left.shape[1]))


def squares(x):
    return jnp.sum(x * x, axis=1)


def inverse_factor(rows):
    groups = len(rows)
    ids = lax.broadcasted_iota(jnp.int32, (SUB, PW), 0)
    lanes = lax.broadcasted_iota(jnp.int32, (SUB, PW), 1)
    inv = [jnp.where(lanes == ids + SUB * g, 1.0, 0.0).astype(jnp.float32) for g in range(groups)]
    for b in range(groups):
        cols = [
            [jnp.broadcast_to(rows[i][:, SUB * b + j : SUB * b + j + 1], (SUB, PW)) for i in range(b, groups)]
            for j in range(SUB)
        ]
        head, inv_head = rows[b], inv[b]
        steps = []
        for k in range(SUB):
            spread = [jnp.broadcast_to(cols[k][0][j : j + 1], (SUB, PW)) for j in range(k, SUB)]
            scale = lax.rsqrt(spread[0])
            row = jnp.broadcast_to(head[k : k + 1], (SUB, PW)) * scale
            inv_row = jnp.broadcast_to(inv_head[k : k + 1], (SUB, PW)) * scale
            mult = [c * scale for c in cols[k]]
            mult[0] = jnp.where(ids > k, mult[0], 0.0)
            for j in range(k + 1, SUB):
                there = spread[j - k] * scale
                cols[j] = [c - m * there for c, m in zip(cols[j], mult)]
            head = head - mult[0] * row
            inv_head = jnp.where(ids == k, inv_row, inv_head - mult[0] * inv_row)
            steps.append((row, inv_row, mult))
        inv[b] = inv_head
        for i in range(b + 1, groups):
            for row, inv_row, mult in steps:
                rows[i] = rows[i] - mult[i - b] * row
                inv[i] = inv[i] - mult[i - b] * inv_row
    return inv


def update_kernel(block_ref, rows_ref, cols_ref, tile_ref, panel_ref, mine_ref, given_ref, first_ref, second_ref):
    def factor_into(block, out_ref):
        inv = inverse_factor([block[SUB * g : SUB * g + SUB] for g in range(PW // SUB)])
        for g, rows in enumerate(inv):
            out_ref[SUB * g : SUB * g + SUB, :] = rows

    factor_into(block_ref[:PW, :PW], first_ref)
    corner = dot_t(block_ref[PW:, :PW], first_ref[...])
    factor_into(block_ref[PW:, PW:] - dot_t(corner, corner), second_ref)

    def panels_of(ref):
        left = dot_t(ref[:, :PW], first_ref[...])
        return left, dot_t(ref[:, PW:] - dot_t(left, corner), second_ref[...])

    row_left, row_right = panels_of(rows_ref)
    col_left, col_right = panels_of(cols_ref)
    kept = panel_ref.shape[0]
    panel_ref[:, :PW] = row_left[:kept]
    panel_ref[:, PW:] = row_right[:kept]
    for out_ref, start in ((given_ref, kept), (mine_ref, 0)):
        part = slice(start, start + kept)
        out_ref[...] = (
            tile_ref[part, :] - dot_t(row_left[part], col_left) - dot_t(row_right[part], col_right)
        )


def updated(block, rows, cols, tile):
    kept = rows.shape[0] // 2
    wide = jax.ShapeDtypeStruct((kept, tile.shape[1]), jnp.float32)
    return pl.pallas_call(
        update_kernel,
        out_shape=(jax.ShapeDtypeStruct((kept, 2 * PW), jnp.float32), wide, wide),
        scratch_shapes=[pltpu.VMEM((PW, PW), jnp.float32)] * 2,
        cost_estimate=pl.CostEstimate(flops=400_000_000, bytes_accessed=4_000_000, transcendentals=256),
    )(block, rows, cols, tile)


def per_device(points, landmark_index, targets, ridge_shift):
    rows_here = landmark_index.shape[0]
    block_points = points.shape[0]
    row_pos = lax.axis_index(ROWS)
    col_pos = lax.axis_index("cols")
    y_pos = lax.axis_index(Y)
    n_rows = lax.axis_size(ROWS)
    n_y = lax.axis_size(Y)
    per_y = n_rows // n_y
    quarter = C // 2 // n_rows
    half = C // 4
    half_pos = lax.axis_index("half")
    upper = half_pos == 1
    ridge = ridge_shift[0]
    across = [(y, n_y - 1 - y) for y in range(n_y)]
    swap = [(0, 1), (1, 0)]

    def ordered(flag, mine, other, axis):
        return jnp.concatenate([jnp.where(flag, other, mine), jnp.where(flag, mine, other)], axis=axis)

    embedded = jnp.take(points, landmark_index - row_pos * block_points, axis=0)
    own = lax.dynamic_slice_in_dim(embedded, col_pos * quarter, quarter, 0)
    peer_embedded = lax.ppermute(embedded, Y, across)
    own_line = to_all(own, "z")
    column_emb = to_all(own_line, NEAR).reshape(half, -1)
    own_targets = jnp.concatenate([targets, lax.ppermute(targets, Y, across)], axis=0)
    pair_targets = ordered(col_pos == 1, own_targets, lax.ppermute(own_targets, "cols", swap), 1)
    rows_emb = jnp.concatenate([embedded, peer_embedded], axis=0)

    rows_sq = squares(rows_emb)
    col_sq = squares(column_emb)
    peer_pos = row_pos + (n_y - 1 - 2 * y_pos) * per_y
    local = lax.iota(jnp.int32, rows_here)
    row_place = jnp.concatenate([row_pos * rows_here + local, peer_pos * rows_here + local])
    column = half_pos * half + lax.iota(jnp.int32, half)
    col_place = column // quarter * rows_here + col_pos * quarter + column % quarter

    tile = gaussian(rows_emb, rows_sq, column_emb, col_sq)
    tile = tile + jnp.where(row_place[:, None] == col_place[None, :], ridge, 0.0)
    partial = lax.dot_general(
        pair_targets, tile, (((0,), (0,)), ((), ())), precision=exact_mode, preferred_element_type=jnp.float32
    )
    n_plane = lax.axis_size(PLANE)
    n_z = lax.axis_size("z")
    arrived = lax.all_to_all(partial.reshape(n_plane, -1, half), PLANE, 0, 0, tiled=True)
    nearer = arrived.reshape(2, n_plane // 2, -1, half).sum(axis=1)
    nearer = nearer.reshape(2, n_z, -1, half).swapaxes(0, 1)
    projected = lax.all_to_all(nearer, "z", 0, 0, tiled=True).sum(axis=0)
    projected = jnp.concatenate([projected[0], projected[1]], axis=1)

    sent_heads = lax.ppermute(column_emb[:PW], Y, [(y, n_y - 1 - y) for y in range(n_y // 2)])
    own_heads = jnp.where(upper, sent_heads, column_emb[:PW])
    heads = ordered(col_pos == 1, own_heads, lax.ppermute(own_heads, "cols", swap), 0)
    heads_sq = squares(heads)
    head = lax.iota(jnp.int32, 2 * PW)
    head_place = head % PW // quarter * rows_here + head // PW * quarter + head % quarter

    def at_heads(emb, emb_sq, place):
        base = gaussian(emb, emb_sq, heads, heads_sq)
        return base + jnp.where(place[:, None] == head_place[None, :], ridge, 0.0)

    operands = (
        at_heads(heads, heads_sq, head_place),
        at_heads(rows_emb, rows_sq, row_place),
        at_heads(column_emb, col_sq, col_place),
        tile,
    )
    panels, mine, given = updated(*operands)
    taken = lax.ppermute(given, Y, across)
    remainder = jnp.concatenate(
        [jnp.where(upper, taken, mine)[:, PW:], jnp.where(upper, mine, taken)], axis=1
    )
    return projected, panels, remainder


def solution(mesh):
    split = Mesh(
        mesh.devices.reshape(2, 2, 4, 8, mesh.shape["cols"]), ("half", "near", "x", "z", "cols")
    )
    placed = (P(ROWS, None), P(ROWS), P(ROWS, "cols"), P())
    return jax.shard_map(
        per_device,
        mesh=split,
        in_specs=placed,
        out_specs=(P(ROWS, "cols"), P(ROWS, None), P(ROWS, "cols")),
        check_vma=False,
    )
```

time: 143 us -> 143 us (level)
  starting transfers between devices: 24.3 us -> 33.8 us
  matrix products: 23.6 us -> 14.5 us
  waiting for transfers between devices: 48.8 us -> 41.4 us
  Pallas kernels: 10.3 us -> 14.6 us
  other arithmetic: 8.36 us -> 11.6 us
  local copies, waits for them, and re-layouts: 7.8 us -> 6.19 us
    all_to_all x1, waiting for transfers between devices: 36.2 us -> 0.01 us  [to_all(): lax.all_to_all(jnp.broadcast_to(x[None], (peers, *x.shape)), axis, 0, 0,...]
    ppermute x2 -> x6, waiting for transfers between devices: 0.01 us -> 31.3 us  [the longest x1 15.2 us: per_device(): peer_embedded = lax.ppermute(embedded, Y, across)]
    ppermute x2 -> x6, starting transfers between devices: 6.62 us -> 17 us  [the longest x1 5.09 us: per_device(): lax.ppermute(column_emb[:PW], Y, [(y, n_y - 1 - y) for y in range(n_y //...]
    dot_general x11 -> x4, matrix products: 20.4 us -> 11.7 us  [dot_t(): lax.dot_general(left, right, (((1,), (1,)), ((), ())), precision=exact_mo...]
    pallas_call x1, Pallas kernels: 10.3 us -> 14.6 us  [updated(): pl.pallas_call(update_kernel, out_shape=(jax.ShapeDtypeStruct((kept, 2 *...]
    select_n x2 -> x6, other arithmetic: 2.03 us -> 5.59 us  [the longest x2 3.56 us: ordered(): jnp.where(flag, other, mine)]
    all_to_all x2, waiting for transfers between devices: 12.7 us -> 10.2 us  [the longest x1 10.2 us: per_device(): lax.all_to_all(partial.reshape(n_plane, -1, half), PLANE, 0, 0, tiled=True)]
    all_to_all x1, starting transfers between devices: 6.93 us -> 5.16 us  [to_all(): lax.all_to_all(jnp.broadcast_to(x[None], (peers, *x.shape)), axis, 0, 0,...]
  transfers between devices with their start and end apart: 5 -> 9, of which waited for: 3 -> 5; matrix products, arithmetic and copies ran while one was open for 21% -> 16% of each run, Pallas kernels for 7% -> 10%
where the time goes in v3:
time: 143 us; the launch traced here: 142 us
  waiting for transfers between devices  41.4 us (29%)
  starting transfers between devices  33.8 us (24%)
  blocking collectives  17.8 us (12%)
  Pallas kernels  14.6 us (10%)
  matrix products  14.5 us (10%)
  other arithmetic  11.6 us (8%)
  local copies, waits for them, and re-layouts  6.19 us (4%)
  between operations  1.59 us (1%)
    all_to_all x1, blocking collectives, to_all(): lax.all_to_all(jnp.broadcast_to(x[None], (peers, *x.shape)), axis, 0, 0,...  17.8 us
    ppermute x1, waiting for transfers between devices, per_device(): peer_embedded = lax.ppermute(embedded, Y, across)  15.2 us
    pallas_call x1, Pallas kernels, updated(): pl.pallas_call(update_kernel, out_shape=(jax.ShapeDtypeStruct((kept, 2 *...  14.6 us
    ppermute x1, waiting for transfers between devices, per_device(): taken = lax.ppermute(given, Y, across)  12.3 us
    dot_general x4, matrix products, dot_t(): lax.dot_general(left, right, (((1,), (1,)), ((), ())), precision=exact_mo...  11.7 us
    all_to_all x1, waiting for transfers between devices, per_device(): lax.all_to_all(partial.reshape(n_plane, -1, half), PLANE, 0, 0, tiled=True)  10.2 us
    all_to_all x1, starting transfers between devices, per_device(): lax.all_to_all(partial.reshape(n_plane, -1, half), PLANE, 0, 0, tiled=True)  8.34 us
    all_to_all x1, starting transfers between devices, to_all(): lax.all_to_all(jnp.broadcast_to(x[None], (peers, *x.shape)), axis, 0, 0,...  5.16 us
  transfers between devices with their start and end apart: 9, of which 5 were waited for; matrix products, arithmetic and copies ran while one was open for 16% of the time, Pallas kernels for 10%

profile of v3, /device:TPU:1, one launch (start us, length us, event | category | flops | bytes accessed | tf_op | source)
XLA Modules:
  0.0 141.6 jit_solution(16992685360909754755)
XLA Ops:
  0.6 0.0 copy-start
  0.7 0.8 compare_and_fusion
  1.5 0.6 copy-done
  2.1 1.1 gather_fusion
  3.2 0.1 broadcast_select_fusion
  3.3 0.0 copy-start.4
  3.3 17.8 %all_to_all.20 = f32[8,8,768]{2,1,0:T(8,128)S(1)} all-to-all(f32[8,8,768]{2,1,0:T(8,128)S(1)} %broadcast_in_dim.69), channel_id=1, replica_groups=mesh['half'=2,'near'=2,'x'=4,'z'=8,'cols'=2] {'z'}, dimensions={0} | all-to-all | bytes 393216 | tf_op jit(solution)/shard_map/all_to_all | solution.py:23
  21.1 1.3 broadcast_in_dim.70
  22.4 5.2 %all-to-all-start.1 = ((f32[8,8,8,768]{3,2,1,0:T(8,128)}), f32[8,8,8,768]{3,2,1,0:T(8,128)S(1)}, u32[]{:S(2)}, u32[]{:S(2)}) async-start(f32[8,8,8,768]{3,2,1,0:T(8,128)} %broadcast_in_dim.70), calls=%async_computation.1 | async-start | bytes 3145728 | tf_op jit(solution)/shard_map/all_to_all | solution.py:23
  27.6 2.9 %collective-permute-start = (f32[256,256]{1,0:T(8,128)S(1)}, f32[256,256]{1,0:T(8,128)S(1)}, u32[]{:S(2)}, u32[]{:S(2)}) collective-permute-start(f32[256,256]{1,0:T(8,128)S(1)} %copy-done.10), channel_id=1, source_target_pairs={{0,192},{64,128},{128,64},{192,0},{1,193},{65,129},{129,65},{193,1... | collective-permute-start | bytes 786440 | tf_op jit(solution)/shard_map/ppermute | solution.py:136
  30.5 0.7 constant_dynamic-update-slice_fusion.1
  31.2 3.1 %collective-permute-done = f32[256,256]{1,0:T(8,128)S(1)} collective-permute-done((f32[256,256]{1,0:T(8,128)S(1)}, f32[256,256]{1,0:T(8,128)S(1)}, u32[]{:S(2)}, u32[]{:S(2)}) %collective-permute-start) | collective-permute-done | bytes 262176 | tf_op jit(solution)/shard_map/ppermute | solution.py:136
  34.3 0.7 constant_dynamic-update-slice_fusion
  35.0 3.9 %collective-permute-start.1 = (f32[512,256]{1,0:T(8,128)}, f32[512,256]{1,0:T(8,128)}, u32[]{:S(2)}, u32[]{:S(2)}) collective-permute-start(f32[512,256]{1,0:T(8,128)} %constant_dynamic-update-slice_fusion), channel_id=1, source_target_pairs={{0,1},{1,0},{2,3},{3,2},{4,5},{5,4},{6,7},{7,6},{8,9},{9,8},{10,11... | collective-permute-start | bytes 1572872 | tf_op jit(solution)/shard_map/ppermute | solution.py:137
  38.9 3.0 %collective-permute-start.2 = (f32[256,768]{1,0:T(8,128)}, f32[256,768]{1,0:T(8,128)}, u32[]{:S(2)}, u32[]{:S(2)}) collective-permute-start(f32[256,768]{1,0:T(8,128)} %copy-done.4), channel_id=1, source_target_pairs={{0,192},{64,128},{128,64},{192,0},{1,193},{65,129},{129,65},{193,1... | collective-permute-start | bytes 2359304 | tf_op jit(solution)/shard_map/ppermute | solution.py:133
  42.5 0.0 copy-start.11
  42.6 2.3 %broadcast_select_fusion.3 = (f32[512,256]{1,0:T(8,128)}, f32[512,256]{1,0:T(8,128)}) fusion(f32[512,256]{1,0:T(8,128)} %collective-permute-done.1, f32[512,256]{1,0:T(8,128)} %constant_dynamic-update-slice_fusion, pred[]{:T(512)S(6)} %eq.33), kind=kLoop, calls=%fused_computation.32 | loop fusion | flops 262144 | bytes 2097153 | tf_op jit(solution)/shard_map/jit(_where)/select_n | solution.py:129
  44.9 15.2 %collective-permute-done.2 = f32[256,768]{1,0:T(8,128)} collective-permute-done((f32[256,768]{1,0:T(8,128)}, f32[256,768]{1,0:T(8,128)}, u32[]{:S(2)}, u32[]{:S(2)}) %collective-permute-start.2) | collective-permute-done | bytes 786464 | tf_op jit(solution)/shard_map/ppermute | solution.py:133
  60.0 1.3 multiply_reduce_fusion.1
  61.4 5.1 %collective-permute-start.3 = (f32[128,768]{1,0:T(8,128)S(1)}, f32[128,768]{1,0:T(8,128)}, u32[]{:S(2)}, u32[]{:S(2)}) collective-permute-start(f32[128,768]{1,0:T(8,128)S(1)} %bitcast.24), channel_id=1, source_target_pairs={{0,192},{64,128},{1,193},{65,129},{2,194},{66,130},{3,195},{67,131... | collective-permute-start | bytes 1179656 | tf_op jit(solution)/shard_map/ppermute | solution.py:161
  66.5 0.8 multiply_reduce_fusion
  67.3 0.8 add.253
  68.1 4.4 %select_add_fusion.tile_ref = f32[512,512]{1,0:T(8,128)S(1)} fusion(f32[512,768]{1,0:T(8,128)S(1)} %bitcast.21, f32[256,768]{1,0:T(8,128)} %collective-permute-done.2, f32[256,768]{1,0:T(8,128)} %copy-done.4, f32[]{:T(128)} %bitcast.17, s32[512]{0:T(512)S(1)} %fusion.16, f32[512]{0:T(512)S(1)} %add.253, f32[512]{0:T(512)S(1)} %multiply_reduce_fusion.1, ...), kind=kOutput, calls=%fused_computation.23 | convolution fusion | flops 2418409472 | bytes 4202500 | tf_op jit(solution)/shard_map/dot_general | solution.py:27
  72.5 0.8 collective-permute-done.3
  73.3 0.8 broadcast_select_fusion.4
  74.1 1.7 %collective-permute-start.4 = (f32[128,768]{1,0:T(8,128)}, f32[128,768]{1,0:T(8,128)}, u32[]{:S(2)}, u32[]{:S(2)}) collective-permute-start(f32[128,768]{1,0:T(8,128)} %broadcast_select_fusion.4), channel_id=1, source_target_pairs={{0,1},{1,0},{2,3},{3,2},{4,5},{5,4},{6,7},{7,6},{8,9},{9,8},{10,11... | collective-permute-start | bytes 1179656 | tf_op jit(solution)/shard_map/ppermute | solution.py:163
  75.8 2.9 %fusion.10 = f32[512,512]{1,0:T(8,128)} fusion(f32[512,512]{1,0:T(8,128)S(1)} %select_add_fusion.tile_ref, f32[512,256]{1,0:T(8,128)S(1)} %copy-done.8, f32[512,256]{1,0:T(8,128)S(1)} %copy-done.7), kind=kOutput, calls=%fused_computation.18 | convolution fusion | flops 1610874880 | bytes 3145728 | tf_op jit(solution)/shard_map/dot_general | solution.py:150
  78.7 8.3 %all-to-all-start.2 = ((f32[16,32,512]{2,1,0:T(8,128)}), f32[16,32,512]{2,1,0:T(8,128)}, u32[]{:S(2)}, u32[]{:S(2)}) async-start(f32[16,32,512]{2,1,0:T(8,128)} %bitcast.23), calls=%async_computation.2 | async-start | bytes 2097152 | tf_op jit(solution)/shard_map/all_to_all | solution.py:155
  87.0 0.0 copy-start.6
  87.1 0.0 copy-start.12
  87.1 0.0 copy-start.13
  87.1 1.2 broadcast_select_fusion.6
  88.3 0.1 multiply_reduce_fusion.2
  88.5 3.4 %select_add_fusion.1.rows_ref = f32[512,256]{1,0:T(8,128)} fusion(f32[128,768]{1,0:T(8,128)S(1)} %get-tuple-element.14, f32[128,768]{1,0:T(8,128)S(1)} %get-tuple-element.13, f32[256,768]{1,0:T(8,128)} %collective-permute-done.2, f32[256,768]{1,0:T(8,128)S(1)} %copy-done.6, f32[]{:T(128)} %bitcast.19, s32[256]{0:T(256)S(1)} %fusion.21, ...), kind=kOutput, calls=%fused_computation.27 | convolution fusion | flops 1209597952 | bytes 2889732 | tf_op jit(solution)/shard_map/dot_general | solution.py:27
  92.0 2.3 %fusion.4.cols_ref = f32[512,256]{1,0:T(8,128)} fusion(f32[512,768]{1,0:T(8,128)S(1)} %bitcast.22, f32[128,768]{1,0:T(8,128)S(1)} %get-tuple-element.14, f32[128,768]{1,0:T(8,128)S(1)} %get-tuple-element.13, f32[512]{0:T(512)S(1)} %add.253, f32[]{:T(128)} %bitcast.20, s32[256]{0:T(256)S(1)} %fusion.21, f32[256]{0:T(256)S(1)} %multiply_reduce_fusion.2, ...), kind=kOutput, calls=%fused_computation.10 | convolution fusion | flops 1209204736 | bytes 2889732 | tf_op jit(solution)/shard_map/dot_general | solution.py:27
  94.3 10.2 %all-to-all-done.2 = f32[16,32,512]{2,1,0:T(8,128)} async-done(((f32[16,32,512]{2,1,0:T(8,128)}), f32[16,32,512]{2,1,0:T(8,128)}, u32[]{:S(2)}, u32[]{:S(2)}) %all-to-all-start.2) | async-done | bytes 1048608 | tf_op jit(solution)/shard_map/all_to_all | solution.py:155
  104.4 1.3 bitcast_reduce_fusion
  105.7 0.1 copy.10
  105.8 0.7 copy.11
  106.5 3.4 %all-to-all-start.3 = ((f32[8,2,4,512]{3,2,1,0:T(4,128)}), f32[8,2,4,512]{3,2,1,0:T(4,128)S(1)}, u32[]{:S(2)}, u32[]{:S(2)}) async-start(f32[8,2,4,512]{3,2,1,0:T(4,128)} %copy.11), calls=%async_computation.3 | async-start | bytes 262144 | tf_op jit(solution)/shard_map/all_to_all | solution.py:158
  109.9 1.6 %fusion.9.block_ref = f32[256,256]{1,0:T(8,128)} fusion(f32[128,768]{1,0:T(8,128)S(1)} %copy-done.3, f32[128,768]{1,0:T(8,128)S(1)} %get-tuple-element.13, f32[]{:T(128)} %bitcast.18, s32[256]{0:T(256)S(1)} %copy-done.14, f32[256]{0:T(256)S(1)} %multiply_reduce_fusion.2), kind=kOutput, calls=%fused_computation.17 | convolution fusion | flops 604700672 | bytes 1050628 | tf_op jit(solution)/shard_map/dot_general | solution.py:27
  111.5 14.6 %shard_map.67 = (f32[256,256]{1,0:T(8,128)}, f32[256,512]{1,0:T(8,128)}, f32[256,512]{1,0:T(8,128)}) custom-call(f32[256,256]{1,0:T(8,128)} %fusion.9.block_ref, f32[512,256]{1,0:T(8,128)} %select_add_fusion.1.rows_ref, f32[512,256]{1,0:T(8,128)} %fusion.4.cols_ref, f32[512,512]{1,0:T(8,128)} %copy-done.1), custom_call_target="tpu_custom_call" | custom-call | flops 400000000 | bytes 4000000 | tf_op jit(solution)/shard_map/pallas_call | solution.py:103
  126.1 0.4 collective-permute-start.5
  126.6 0.6 pad_maximum_fusion.14
  127.2 12.3 %collective-permute-done.5 = f32[256,512]{1,0:T(8,128)S(1)} collective-permute-done((f32[256,512]{1,0:T(8,128)}, f32[256,512]{1,0:T(8,128)S(1)}, u32[]{:S(2)}, u32[]{:S(2)}) %collective-permute-start.5) | collective-permute-done | bytes 524320 | tf_op jit(solution)/shard_map/ppermute | solution.py:179
  139.5 1.0 slice_select_fusion
  140.5 0.1 broadcast_select_fusion.1
  140.6 1.0 pad_maximum_fusion.5
  (37 shorter events, 0.2 us)
Async XLA Ops:
  0.6 1.4 %copy-start = (f32[512,768]{1,0:T(8,128)S(1)}, f32[512,768]{1,0:T(8,128)}, u32[]{:S(2)}) copy-start(f32[512,768]{1,0:T(8,128)} %param.4) | copy-start | bytes 4718596
  3.3 19.2 %copy-start.4 = (f32[256,768]{1,0:T(8,128)}, f32[256,768]{1,0:T(8,128)S(1)}, u32[]{:S(2)}) copy-start(f32[256,768]{1,0:T(8,128)S(1)} %broadcast_select_fusion) | copy-start | bytes 2359300
  22.4 5.2 %copy-start.10 = (f32[256,256]{1,0:T(8,128)S(1)}, f32[256,256]{1,0:T(8,128)}, u32[]{:S(2)}) copy-start(f32[256,256]{1,0:T(8,128)} %param.6) | copy-start | bytes 786436
  22.4 38.9 %all-to-all-start.1 = ((f32[8,8,8,768]{3,2,1,0:T(8,128)}), f32[8,8,8,768]{3,2,1,0:T(8,128)S(1)}, u32[]{:S(2)}, u32[]{:S(2)}) async-start(f32[8,8,8,768]{3,2,1,0:T(8,128)} %broadcast_in_dim.70), calls=%async_computation.1 | async-start | bytes 3145728 | tf_op jit(solution)/shard_map/all_to_all | solution.py:23
  27.6 6.7 %collective-permute-start = (f32[256,256]{1,0:T(8,128)S(1)}, f32[256,256]{1,0:T(8,128)S(1)}, u32[]{:S(2)}, u32[]{:S(2)}) collective-permute-start(f32[256,256]{1,0:T(8,128)S(1)} %copy-done.10), channel_id=1, source_target_pairs={{0,192},{64,128},{128,64},{192,0},{1,193},{65,129},{129,65},{193,1... | collective-permute-start | bytes 786440 | tf_op jit(solution)/shard_map/ppermute | solution.py:136
  35.0 7.6 %collective-permute-start.1 = (f32[512,256]{1,0:T(8,128)}, f32[512,256]{1,0:T(8,128)}, u32[]{:S(2)}, u32[]{:S(2)}) collective-permute-start(f32[512,256]{1,0:T(8,128)} %constant_dynamic-update-slice_fusion), channel_id=1, source_target_pairs={{0,1},{1,0},{2,3},{3,2},{4,5},{5,4},{6,7},{7,6},{8,9},{9,8},{10,11... | collective-permute-start | bytes 1572872 | tf_op jit(solution)/shard_map/ppermute | solution.py:137
  38.9 21.2 %collective-permute-start.2 = (f32[256,768]{1,0:T(8,128)}, f32[256,768]{1,0:T(8,128)}, u32[]{:S(2)}, u32[]{:S(2)}) collective-permute-start(f32[256,768]{1,0:T(8,128)} %copy-done.4), channel_id=1, source_target_pairs={{0,192},{64,128},{128,64},{192,0},{1,193},{65,129},{129,65},{193,1... | collective-permute-start | bytes 2359304 | tf_op jit(solution)/shard_map/ppermute | solution.py:133
  42.5 17.6 %copy-start.5 = (f32[256,768]{1,0:T(8,128)S(1)}, f32[256,768]{1,0:T(8,128)}, u32[]{:S(2)}) copy-start(f32[256,768]{1,0:T(8,128)} %copy-done.4) | copy-start | bytes 2359300
  42.5 25.6 %copy-start.11 = (s32[512]{0:T(512)}, s32[512]{0:T(512)S(1)}, u32[]{:S(2)}) copy-start(s32[512]{0:T(512)S(1)} %pad_add_fusion) | copy-start | bytes 6148
  61.4 11.9 %collective-permute-start.3 = (f32[128,768]{1,0:T(8,128)S(1)}, f32[128,768]{1,0:T(8,128)}, u32[]{:S(2)}, u32[]{:S(2)}) collective-permute-start(f32[128,768]{1,0:T(8,128)S(1)} %bitcast.24), channel_id=1, source_target_pairs={{0,192},{64,128},{1,193},{65,129},{2,194},{66,130},{3,195},{67,131... | collective-permute-start | bytes 1179656 | tf_op jit(solution)/shard_map/ppermute | solution.py:161
  68.1 7.7 %copy-start.7 = (f32[512,256]{1,0:T(8,128)S(1)}, f32[512,256]{1,0:T(8,128)}, u32[]{:S(2)}) copy-start(f32[512,256]{1,0:T(8,128)} %get-tuple-element.11) | copy-start | bytes 1572868
  68.1 7.7 %copy-start.8 = (f32[512,256]{1,0:T(8,128)S(1)}, f32[512,256]{1,0:T(8,128)}, u32[]{:S(2)}) copy-start(f32[512,256]{1,0:T(8,128)} %get-tuple-element.12) | copy-start | bytes 1572868
  72.5 6.2 %copy-start.1 = (f32[512,512]{1,0:T(8,128)}, f32[512,512]{1,0:T(8,128)S(1)}, u32[]{:S(2)}) copy-start(f32[512,512]{1,0:T(8,128)S(1)} %select_add_fusion.tile_ref) | copy-start | bytes 3145732
  74.1 13.0 %collective-permute-start.4 = (f32[128,768]{1,0:T(8,128)}, f32[128,768]{1,0:T(8,128)}, u32[]{:S(2)}, u32[]{:S(2)}) collective-permute-start(f32[128,768]{1,0:T(8,128)} %broadcast_select_fusion.4), channel_id=1, source_target_pairs={{0,1},{1,0},{2,3},{3,2},{4,5},{5,4},{6,7},{7,6},{8,9},{9,8},{10,11... | collective-permute-start | bytes 1179656 | tf_op jit(solution)/shard_map/ppermute | solution.py:163
  78.7 25.7 %all-to-all-start.2 = ((f32[16,32,512]{2,1,0:T(8,128)}), f32[16,32,512]{2,1,0:T(8,128)}, u32[]{:S(2)}, u32[]{:S(2)}) async-start(f32[16,32,512]{2,1,0:T(8,128)} %bitcast.23), calls=%async_computation.2 | async-start | bytes 2097152 | tf_op jit(solution)/shard_map/all_to_all | solution.py:155
  87.0 1.5 %copy-start.6 = (f32[256,768]{1,0:T(8,128)S(1)}, f32[256,768]{1,0:T(8,128)}, u32[]{:S(2)}) copy-start(f32[256,768]{1,0:T(8,128)} %copy-done.4) | copy-start | bytes 2359300
  87.1 1.5 %copy-start.12 = (s32[512]{0:T(512)S(1)}, s32[512]{0:T(512)}, u32[]{:S(2)}) copy-start(s32[512]{0:T(512)} %copy-done.11) | copy-start | bytes 6148
  87.1 4.9 %copy-start.13 = (s32[256]{0:T(256)}, s32[256]{0:T(256)S(1)}, u32[]{:S(2)}) copy-start(s32[256]{0:T(256)S(1)} %fusion.21) | copy-start | bytes 3076
  88.3 3.6 %copy-start.2 = (f32[128,768]{1,0:T(8,128)}, f32[128,768]{1,0:T(8,128)S(1)}, u32[]{:S(2)}) copy-start(f32[128,768]{1,0:T(8,128)S(1)} %get-tuple-element.14) | copy-start | bytes 1179652
  94.3 15.7 %copy-start.3 = (f32[128,768]{1,0:T(8,128)S(1)}, f32[128,768]{1,0:T(8,128)}, u32[]{:S(2)}) copy-start(f32[128,768]{1,0:T(8,128)} %copy-done.2) | copy-start | bytes 1179652
  94.3 15.7 %copy-start.14 = (s32[256]{0:T(256)S(1)}, s32[256]{0:T(256)}, u32[]{:S(2)}) copy-start(s32[256]{0:T(256)} %copy-done.13) | copy-start | bytes 3076
  106.5 20.0 %all-to-all-start.3 = ((f32[8,2,4,512]{3,2,1,0:T(4,128)}), f32[8,2,4,512]{3,2,1,0:T(4,128)S(1)}, u32[]{:S(2)}, u32[]{:S(2)}) async-start(f32[8,2,4,512]{3,2,1,0:T(4,128)} %copy.11), calls=%async_computation.3 | async-start | bytes 262144 | tf_op jit(solution)/shard_map/all_to_all | solution.py:158
  126.1 14.4 %copy-start.9 = (f32[256,512]{1,0:T(8,128)S(1)}, f32[256,512]{1,0:T(8,128)}, u32[]{:S(2)}) copy-start(f32[256,512]{1,0:T(8,128)} %get-tuple-element.8) | copy-start | bytes 1572868
  126.1 13.4 %collective-permute-start.5 = (f32[256,512]{1,0:T(8,128)}, f32[256,512]{1,0:T(8,128)S(1)}, u32[]{:S(2)}, u32[]{:S(2)}) collective-permute-start(f32[256,512]{1,0:T(8,128)} %get-tuple-element.7), channel_id=1, source_target_pairs={{0,192},{64,128},{128,64},{192,0},{1,193},{65,129},{129,65},{193,1... | collective-permute-start | bytes 1572872 | tf_op jit(solution)/shard_map/ppermute | solution.py:179

commit v4 on v3

--- a/solution.py
+++ b/solution.py
@@ -27,6 +27,18 @@
     return lax.dot_general(
         left, right, (((1,), (1,)), ((), ())), precision=exact_mode, preferred_element_type=jnp.float32
     )
+
+
+def in_two(x):
+    high = x.astype(jnp.bfloat16)
+    return high, (x - high.astype(jnp.float32)).astype(jnp.bfloat16)
+
+
+def split_dot_t(left, right):
+    def part(a, b):
+        return lax.dot_general(a, b, (((1,), (1,)), ((), ())), preferred_element_type=jnp.float32)
+
+    return part(left[0], right[1]) + part(left[1], right[0]) + part(left[0], right[0])
 
 
 def gaussian(left, left_sq, right, right_sq):
@@ -81,19 +93,29 @@
     corner = dot_t(block_ref[PW:, :PW], first_ref[...])
     factor_into(block_ref[PW:, PW:] - dot_t(corner, corner), second_ref)
 
+    first, second, below = in_two(first_ref[...]), in_two(second_ref[...]), in_two(corner)
+
     def panels_of(ref):
-        left = dot_t(ref[:, :PW], first_ref[...])
-        return left, dot_t(ref[:, PW:] - dot_t(left, corner), second_ref[...])
-
-    row_left, row_right = panels_of(rows_ref)
-    col_left, col_right = panels_of(cols_ref)
+        left = split_dot_t(in_two(ref[:, :PW]), first)
+        left_two = in_two(left)
+        right = split_dot_t(in_two(ref[:, PW:] - split_dot_t(left_two, below)), second)
+        return left, right, left_two, in_two(right)
+
+    row_left, row_right, row_left_two, row_right_two = panels_of(rows_ref)
+    _, _, col_left_two, col_right_two = panels_of(cols_ref)
     kept = panel_ref.shape[0]
     panel_ref[:, :PW] = row_left[:kept]
     panel_ref[:, PW:] = row_right[:kept]
+
+    def rows_of(two, part):
+        return two[0][part], two[1][part]
+
     for out_ref, start in ((given_ref, kept), (mine_ref, 0)):
         part = slice(start, start + kept)
         out_ref[...] = (
-            tile_ref[part, :] - dot_t(row_left[part], col_left) - dot_t(row_right[part], col_right)
+            tile_ref[part, :]
+            - split_dot_t(rows_of(row_left_two, part), col_left_two)
+            - split_dot_t(rows_of(row_right_two, part), col_right_two)
         )
 
 
@@ -128,14 +150,16 @@
     def ordered(flag, mine, other, axis):
         return jnp.concatenate([jnp.where(flag, other, mine), jnp.where(flag, mine, other)], axis=axis)
 
-    embedded = jnp.take(points, landmark_index - row_pos * block_points, axis=0)
+    local_index = landmark_index - row_pos * block_points
+    embedded = points.at[local_index].get(mode="promise_in_bounds")
     own = lax.dynamic_slice_in_dim(embedded, col_pos * quarter, quarter, 0)
     peer_embedded = lax.ppermute(embedded, Y, across)
     own_line = to_all(own, "z")
-    column_emb = to_all(own_line, NEAR).reshape(half, -1)
+    column_emb = lax.optimization_barrier(to_all(own_line, NEAR).reshape(half, -1))
     own_targets = jnp.concatenate([targets, lax.ppermute(targets, Y, across)], axis=0)
-    pair_targets = ordered(col_pos == 1, own_targets, lax.ppermute(own_targets, "cols", swap), 1)
-    rows_emb = jnp.concatenate([embedded, peer_embedded], axis=0)
+    peer_targets = lax.ppermute(own_targets, "cols", swap)
+    pair_targets = lax.optimization_barrier(ordered(col_pos == 1, own_targets, peer_targets, 1))
+    rows_emb = lax.optimization_barrier(jnp.concatenate([embedded, peer_embedded], axis=0))
 
     rows_sq = squares(rows_emb)
     col_sq = squares(column_emb)
@@ -148,7 +172,7 @@
     tile = gaussian(rows_emb, rows_sq, column_emb, col_sq)
     tile = tile + jnp.where(row_place[:, None] == col_place[None, :], ridge, 0.0)
     partial = lax.dot_general(
-        pair_targets, tile, (((0,), (0,)), ((), ())), precision=exact_mode, preferred_element_type=jnp.float32
+        pair_targets, tile, (((0,), (0,)), ((), ())), precision=lax.Precision.HIGH, preferred_element_type=jnp.float32
     )
     n_plane = lax.axis_size(PLANE)
     n_z = lax.axis_size("z")

time: 143 us -> 134 us (0.937)
  blocking collectives: 17.8 us -> 0 us
  waiting for transfers between devices: 41.4 us -> 48.6 us
  starting transfers between devices: 33.8 us -> 40.1 us
  matrix products: 14.5 us -> 11.1 us
  local copies, waits for them, and re-layouts: 6.19 us -> 8.19 us
  Pallas kernels: 14.6 us -> 13.1 us
    all_to_all x1 -> x0, blocking collectives: 17.8 us -> none  [to_all(): lax.all_to_all(jnp.broadcast_to(x[None], (peers, *x.shape)), axis, 0, 0,...]
    all_to_all x1 -> x2, starting transfers between devices: 5.16 us -> 14 us  [to_all(): lax.all_to_all(jnp.broadcast_to(x[None], (peers, *x.shape)), axis, 0, 0,...]
    all_to_all x1 -> x2, waiting for transfers between devices: 0.01 us -> 5.45 us  [to_all(): lax.all_to_all(jnp.broadcast_to(x[None], (peers, *x.shape)), axis, 0, 0,...]
    ppermute x1, waiting for transfers between devices: 0.78 us -> 4.46 us  [per_device(): lax.ppermute(column_emb[:PW], Y, [(y, n_y - 1 - y) for y in range(n_y //...]
    ppermute x1, waiting for transfers between devices: 3.05 us -> 0.01 us  [per_device(): lax.ppermute(targets, Y, across)]
    dot_general x4, matrix products: 11.7 us -> 9.08 us  [dot_t(): lax.dot_general(left, right, (((1,), (1,)), ((), ())), precision=exact_mo...]
    concatenate x0 -> x2, other arithmetic: none -> 2.37 us  [the longest x1 1.24 us: per_device(): jnp.concatenate([embedded, peer_embedded], axis=0)]
    reduce_sum x3, other arithmetic: 2.24 us -> 0.49 us  [squares(): return jnp.sum(x * x, axis=1)]
  transfers between devices with their start and end apart: 9 -> 10, of which waited for: 5 -> 5; matrix products, arithmetic and copies ran while one was open for 16% -> 16% of each run, Pallas kernels for 10% -> 10%
where the time goes in v4:
time: 134 us; the launch traced here: 133 us
  waiting for transfers between devices  48.6 us (36%)
  starting transfers between devices  40.1 us (30%)
  Pallas kernels  13.1 us (10%)
  matrix products  11.1 us (8%)
  other arithmetic  10.3 us (8%)
  local copies, waits for them, and re-layouts  8.19 us (6%)
  between operations  1.6 us (1%)
    ppermute x1, waiting for transfers between devices, per_device(): peer_embedded = lax.ppermute(embedded, Y, across)  15.1 us
    all_to_all x2, starting transfers between devices, to_all(): lax.all_to_all(jnp.broadcast_to(x[None], (peers, *x.shape)), axis, 0, 0,...  14 us
    pallas_call x1, Pallas kernels, updated(): pl.pallas_call(update_kernel, out_shape=(jax.ShapeDtypeStruct((kept, 2 *...  13.1 us
    ppermute x1, waiting for transfers between devices, per_device(): taken = lax.ppermute(given, Y, across)  12.2 us
    all_to_all x1, waiting for transfers between devices, per_device(): lax.all_to_all(partial.reshape(n_plane, -1, half), PLANE, 0, 0, tiled=True)  11.3 us
    dot_general x4, matrix products, dot_t(): lax.dot_general(left, right, (((1,), (1,)), ((), ())), precision=exact_mo...  9.08 us
    all_to_all x1, starting transfers between devices, per_device(): lax.all_to_all(partial.reshape(n_plane, -1, half), PLANE, 0, 0, tiled=True)  7.26 us
    all_to_all x2, waiting for transfers between devices, to_all(): lax.all_to_all(jnp.broadcast_to(x[None], (peers, *x.shape)), axis, 0, 0,...  5.45 us
  transfers between devices with their start and end apart: 10, of which 5 were waited for; matrix products, arithmetic and copies ran while one was open for 16% of the time, Pallas kernels for 10%

profile of v4, /device:TPU:1, one launch (start us, length us, event | category | flops | bytes accessed | tf_op | source)
XLA Modules:
  0.0 132.9 jit_solution(2069616359659917746)
XLA Ops:
  0.6 0.0 copy-start
  0.7 0.8 compare_select_fusion
  1.5 0.6 copy-done
  2.1 1.1 gather_fusion
  3.2 0.8 broadcast_in_dim.33
  4.0 9.0 %all-to-all-start = ((f32[8,8,768]{2,1,0:T(8,128)}), f32[8,8,768]{2,1,0:T(8,128)S(1)}, u32[]{:S(2)}, u32[]{:S(2)}) async-start(f32[8,8,768]{2,1,0:T(8,128)} %broadcast_in_dim.33), calls=%async_computation | async-start | bytes 393216 | tf_op jit(solution)/shard_map/all_to_all | solution.py:23
  13.0 2.8 %collective-permute-start = (f32[256,256]{1,0:T(8,128)S(1)}, f32[256,256]{1,0:T(8,128)}, u32[]{:S(2)}, u32[]{:S(2)}) collective-permute-start(f32[256,256]{1,0:T(8,128)S(1)} %copy-done.12), channel_id=1, source_target_pairs={{0,192},{64,128},{128,64},{192,0},{1,193},{65,129},{129,65},{193,1... | collective-permute-start | bytes 786440 | tf_op jit(solution)/shard_map/ppermute | solution.py:159
  15.8 0.7 constant_dynamic-update-slice_fusion.1
  16.5 5.4 %all-to-all-done = f32[8,8,768]{2,1,0:T(8,128)S(1)} async-done(((f32[8,8,768]{2,1,0:T(8,128)}), f32[8,8,768]{2,1,0:T(8,128)S(1)}, u32[]{:S(2)}, u32[]{:S(2)}) %all-to-all-start) | async-done | bytes 196640 | tf_op jit(solution)/shard_map/all_to_all | solution.py:23
  22.0 1.3 broadcast_in_dim.34
  23.3 5.0 %all-to-all-start.1 = ((f32[8,8,8,768]{3,2,1,0:T(8,128)}), f32[8,8,8,768]{3,2,1,0:T(8,128)S(1)}, u32[]{:S(2)}, u32[]{:S(2)}) async-start(f32[8,8,8,768]{3,2,1,0:T(8,128)} %broadcast_in_dim.34), calls=%async_computation.1 | async-start | bytes 3145728 | tf_op jit(solution)/shard_map/all_to_all | solution.py:23
  28.3 1.7 %constant_dynamic-update-slice_fusion = f32[512,256]{1,0:T(8,128)} fusion(f32[512,256]{1,0:T(8,128)} %constant_dynamic-update-slice_fusion.1, f32[256,256]{1,0:T(8,128)} %collective-permute-done), kind=kLoop, calls=%fused_computation.36 | loop fusion | bytes 524288 | tf_op jit(solution)/shard_map/concatenate | solution.py:159
  30.0 2.7 %collective-permute-start.1 = (f32[512,256]{1,0:T(8,128)}, f32[512,256]{1,0:T(8,128)}, u32[]{:S(2)}, u32[]{:S(2)}) collective-permute-start(f32[512,256]{1,0:T(8,128)} %constant_dynamic-update-slice_fusion), channel_id=1, source_target_pairs={{0,1},{1,0},{2,3},{3,2},{4,5},{5,4},{6,7},{7,6},{8,9},{9,8},{10,11... | collective-permute-start | bytes 1572872 | tf_op jit(solution)/shard_map/ppermute | solution.py:160
  32.7 3.2 %collective-permute-start.2 = (f32[256,768]{1,0:T(8,128)}, f32[256,768]{1,0:T(8,128)}, u32[]{:S(2)}, u32[]{:S(2)}) collective-permute-start(f32[256,768]{1,0:T(8,128)} %copy-done.8), channel_id=1, source_target_pairs={{0,192},{64,128},{128,64},{192,0},{1,193},{65,129},{129,65},{193,1... | collective-permute-start | bytes 2359304 | tf_op jit(solution)/shard_map/ppermute | solution.py:156
  36.6 1.3 broadcast_select_fusion.2
  37.9 0.0 copy-start.9
  37.9 1.1 pad_maximum_fusion.1
  39.0 15.1 %collective-permute-done.2 = f32[256,768]{1,0:T(8,128)} collective-permute-done((f32[256,768]{1,0:T(8,128)}, f32[256,768]{1,0:T(8,128)}, u32[]{:S(2)}, u32[]{:S(2)}) %collective-permute-start.2) | collective-permute-done | bytes 786464 | tf_op jit(solution)/shard_map/ppermute | solution.py:156
  54.1 1.2 pad_maximum_fusion
  55.4 1.1 copy-done.1
  56.5 0.2 multiply_reduce_fusion.1
  56.7 4.5 %collective-permute-start.3 = (f32[128,768]{1,0:T(8,128)S(1)}, f32[128,768]{1,0:T(8,128)S(1)}, u32[]{:S(2)}, u32[]{:S(2)}) collective-permute-start(f32[128,768]{1,0:T(8,128)S(1)} %slice.21), channel_id=1, source_target_pairs={{0,192},{64,128},{1,193},{65,129},{2,194},{66,130},{3,195},{67,131... | collective-permute-start | bytes 1179656 | tf_op jit(solution)/shard_map/ppermute | solution.py:185
  61.2 0.2 multiply_reduce_fusion
  61.4 2.9 %select_add_fusion.tile_ref = f32[512,512]{1,0:T(8,128)S(1)} fusion(f32[]{:T(128)} %bitcast.18, s32[512]{0:T(512)S(1)} %fusion.12, f32[512,768]{1,0:T(8,128)S(1)} %copy-done.2, f32[512,768]{1,0:T(8,128)S(1)} %bitcast.24, f32[512]{0:T(512)S(1)} %multiply_reduce_fusion, f32[512]{0:T(512)S(1)} %multiply_reduce_fusion.1, s32[512]{0:T(512)S(1)} %pad_add_fusion), kind=kOutput, calls=%fused_computation.20 | convolution fusion | flops 2418016256 | bytes 4202500 | tf_op jit(solution)/shard_map/dot_general | solution.py:27
  64.3 4.5 %collective-permute-done.3 = f32[128,768]{1,0:T(8,128)S(1)} collective-permute-done((f32[128,768]{1,0:T(8,128)S(1)}, f32[128,768]{1,0:T(8,128)S(1)}, u32[]{:S(2)}, u32[]{:S(2)}) %collective-permute-start.3) | collective-permute-done | bytes 393248 | tf_op jit(solution)/shard_map/ppermute | solution.py:185
  68.7 0.1 broadcast_select_fusion.3
  68.8 0.0 copy-start.11
  68.8 1.8 %collective-permute-start.4 = (f32[128,768]{1,0:T(8,128)S(1)}, f32[128,768]{1,0:T(8,128)}, u32[]{:S(2)}, u32[]{:S(2)}) collective-permute-start(f32[128,768]{1,0:T(8,128)S(1)} %broadcast_select_fusion.3), channel_id=1, source_target_pairs={{0,1},{1,0},{2,3},{3,2},{4,5},{5,4},{6,7},{7,6},{8,9},{9,8},{10,11... | collective-permute-start | bytes 1179656 | tf_op jit(solution)/shard_map/ppermute | solution.py:187
  70.6 2.0 %fusion.23 = f32[512,512]{1,0:T(8,128)} fusion(f32[512,512]{1,0:T(8,128)S(1)} %copy-done.7, f32[512,512]{1,0:T(8,128)S(1)} %select_add_fusion.tile_ref), kind=kOutput, calls=%fused_computation.74 | convolution fusion | flops 805306368 | bytes 3145728 | tf_op jit(solution)/shard_map/dot_general | solution.py:174
  72.7 7.3 %all-to-all-start.2 = ((f32[16,32,512]{2,1,0:T(8,128)}), f32[16,32,512]{2,1,0:T(8,128)}, u32[]{:S(2)}, u32[]{:S(2)}) async-start(f32[16,32,512]{2,1,0:T(8,128)} %bitcast.27), calls=%async_computation.2 | async-start | bytes 2097152 | tf_op jit(solution)/shard_map/all_to_all | solution.py:179
  79.9 0.0 copy-start.15
  80.0 1.2 broadcast_select_fusion.5
  81.1 0.1 multiply_reduce_fusion.2
  81.3 2.3 %fusion.4.cols_ref = f32[512,256]{1,0:T(8,128)} fusion(f32[512,768]{1,0:T(8,128)S(1)} %bitcast.26, f32[128,768]{1,0:T(8,128)S(1)} %get-tuple-element.12, f32[128,768]{1,0:T(8,128)S(1)} %get-tuple-element.11, f32[512]{0:T(512)S(1)} %multiply_reduce_fusion, f32[]{:T(128)} %bitcast.21, s32[256]{0:T(256)S(1)} %fusion.17, f32[256]{0:T(256)S(1)} %multiply_reduce_fusion.2, ...), kind=kOutput, calls=%fused_computation.10 | convolution fusion | flops 1209204736 | bytes 2889732 | tf_op jit(solution)/shard_map/dot_general | solution.py:27
  83.6 2.3 %select_add_fusion.1.rows_ref = f32[512,256]{1,0:T(8,128)} fusion(f32[512,768]{1,0:T(8,128)S(1)} %copy-done.3, f32[128,768]{1,0:T(8,128)S(1)} %get-tuple-element.12, f32[128,768]{1,0:T(8,128)S(1)} %get-tuple-element.11, f32[]{:T(128)} %bitcast.20, s32[256]{0:T(256)S(1)} %fusion.17, f32[256]{0:T(256)S(1)} %multiply_reduce_fusion.2, ...), kind=kOutput, calls=%fused_computation.24 | convolution fusion | flops 1209204736 | bytes 2889732 | tf_op jit(solution)/shard_map/dot_general | solution.py:27
  85.9 11.3 %all-to-all-done.2 = f32[16,32,512]{2,1,0:T(8,128)} async-done(((f32[16,32,512]{2,1,0:T(8,128)}), f32[16,32,512]{2,1,0:T(8,128)}, u32[]{:S(2)}, u32[]{:S(2)}) %all-to-all-start.2) | async-done | bytes 1048608 | tf_op jit(solution)/shard_map/all_to_all | solution.py:179
  97.3 1.3 bitcast_reduce_fusion
  98.6 0.1 copy.10
  98.7 0.7 copy.11
  99.4 3.4 %all-to-all-start.3 = ((f32[8,2,4,512]{3,2,1,0:T(4,128)}), f32[8,2,4,512]{3,2,1,0:T(4,128)S(1)}, u32[]{:S(2)}, u32[]{:S(2)}) async-start(f32[8,2,4,512]{3,2,1,0:T(4,128)} %copy.11), calls=%async_computation.3 | async-start | bytes 262144 | tf_op jit(solution)/shard_map/all_to_all | solution.py:182
  102.8 1.6 %fusion.9.block_ref = f32[256,256]{1,0:T(8,128)} fusion(f32[128,768]{1,0:T(8,128)S(1)} %copy-done.6, f32[128,768]{1,0:T(8,128)S(1)} %get-tuple-element.11, f32[]{:T(128)} %bitcast.19, s32[256]{0:T(256)S(1)} %copy-done.16, f32[256]{0:T(256)S(1)} %copy-done.14), kind=kOutput, calls=%fused_computation.17 | convolution fusion | flops 604700672 | bytes 1050628 | tf_op jit(solution)/shard_map/dot_general | solution.py:27
  104.3 13.1 %shard_map.67 = (f32[256,256]{1,0:T(8,128)}, f32[256,512]{1,0:T(8,128)}, f32[256,512]{1,0:T(8,128)}) custom-call(f32[256,256]{1,0:T(8,128)} %fusion.9.block_ref, f32[512,256]{1,0:T(8,128)} %select_add_fusion.1.rows_ref, f32[512,256]{1,0:T(8,128)} %fusion.4.cols_ref, f32[512,512]{1,0:T(8,128)} %copy-done.4), custom_call_target="tpu_custom_call" | custom-call | flops 400000000 | bytes 4000000 | tf_op jit(solution)/shard_map/pallas_call | solution.py:125
  117.5 0.4 collective-permute-start.5
  118.0 0.6 pad_maximum_fusion.9
  118.6 12.2 %collective-permute-done.5 = f32[256,512]{1,0:T(8,128)S(1)} collective-permute-done((f32[256,512]{1,0:T(8,128)}, f32[256,512]{1,0:T(8,128)S(1)}, u32[]{:S(2)}, u32[]{:S(2)}) %collective-permute-start.5) | collective-permute-done | bytes 524320 | tf_op jit(solution)/shard_map/ppermute | solution.py:203
  130.8 1.0 slice_select_fusion
  131.9 0.1 broadcast_select_fusion
  132.0 1.0 pad_maximum_fusion.2
  (42 shorter events, 0.2 us)
Async XLA Ops:
  0.6 1.4 %copy-start = (f32[512,768]{1,0:T(8,128)S(1)}, f32[512,768]{1,0:T(8,128)}, u32[]{:S(2)}) copy-start(f32[512,768]{1,0:T(8,128)} %param.4) | copy-start | bytes 4718596
  2.1 10.9 %copy-start.12 = (f32[256,256]{1,0:T(8,128)S(1)}, f32[256,256]{1,0:T(8,128)}, u32[]{:S(2)}) copy-start(f32[256,256]{1,0:T(8,128)} %param.6) | copy-start | bytes 786436
  3.2 20.1 %copy-start.8 = (f32[256,768]{1,0:T(8,128)}, f32[256,768]{1,0:T(8,128)S(1)}, u32[]{:S(2)}) copy-start(f32[256,768]{1,0:T(8,128)S(1)} %gather_fusion) | copy-start | bytes 2359300
  4.0 18.0 %all-to-all-start = ((f32[8,8,768]{2,1,0:T(8,128)}), f32[8,8,768]{2,1,0:T(8,128)S(1)}, u32[]{:S(2)}, u32[]{:S(2)}) async-start(f32[8,8,768]{2,1,0:T(8,128)} %broadcast_in_dim.33), calls=%async_computation | async-start | bytes 393216 | tf_op jit(solution)/shard_map/all_to_all | solution.py:23
  13.0 15.3 %collective-permute-start = (f32[256,256]{1,0:T(8,128)S(1)}, f32[256,256]{1,0:T(8,128)}, u32[]{:S(2)}, u32[]{:S(2)}) collective-permute-start(f32[256,256]{1,0:T(8,128)S(1)} %copy-done.12), channel_id=1, source_target_pairs={{0,192},{64,128},{128,64},{192,0},{1,193},{65,129},{129,65},{193,1... | collective-permute-start | bytes 786440 | tf_op jit(solution)/shard_map/ppermute | solution.py:159
  23.3 33.4 %all-to-all-start.1 = ((f32[8,8,8,768]{3,2,1,0:T(8,128)}), f32[8,8,8,768]{3,2,1,0:T(8,128)S(1)}, u32[]{:S(2)}, u32[]{:S(2)}) async-start(f32[8,8,8,768]{3,2,1,0:T(8,128)} %broadcast_in_dim.34), calls=%async_computation.1 | async-start | bytes 3145728 | tf_op jit(solution)/shard_map/all_to_all | solution.py:23
  30.0 6.6 %collective-permute-start.1 = (f32[512,256]{1,0:T(8,128)}, f32[512,256]{1,0:T(8,128)}, u32[]{:S(2)}, u32[]{:S(2)}) collective-permute-start(f32[512,256]{1,0:T(8,128)} %constant_dynamic-update-slice_fusion), channel_id=1, source_target_pairs={{0,1},{1,0},{2,3},{3,2},{4,5},{5,4},{6,7},{7,6},{8,9},{9,8},{10,11... | collective-permute-start | bytes 1572872 | tf_op jit(solution)/shard_map/ppermute | solution.py:160
  32.7 21.4 %collective-permute-start.2 = (f32[256,768]{1,0:T(8,128)}, f32[256,768]{1,0:T(8,128)}, u32[]{:S(2)}, u32[]{:S(2)}) collective-permute-start(f32[256,768]{1,0:T(8,128)} %copy-done.8), channel_id=1, source_target_pairs={{0,192},{64,128},{128,64},{192,0},{1,193},{65,129},{129,65},{193,1... | collective-permute-start | bytes 2359304 | tf_op jit(solution)/shard_map/ppermute | solution.py:156
  37.9 16.2 %copy-start.9 = (f32[256,768]{1,0:T(8,128)S(1)}, f32[256,768]{1,0:T(8,128)}, u32[]{:S(2)}) copy-start(f32[256,768]{1,0:T(8,128)} %copy-done.8) | copy-start | bytes 2359300
  55.3 1.1 copy-start.1
  56.7 4.7 %copy-start.2 = (f32[512,768]{1,0:T(8,128)S(1)}, f32[512,768]{1,0:T(8,128)}, u32[]{:S(2)}) copy-start(f32[512,768]{1,0:T(8,128)} %copy-done.1) | copy-start | bytes 4718596
  56.7 12.0 %collective-permute-start.3 = (f32[128,768]{1,0:T(8,128)S(1)}, f32[128,768]{1,0:T(8,128)S(1)}, u32[]{:S(2)}, u32[]{:S(2)}) collective-permute-start(f32[128,768]{1,0:T(8,128)S(1)} %slice.21), channel_id=1, source_target_pairs={{0,192},{64,128},{1,193},{65,129},{2,194},{66,130},{3,195},{67,131... | collective-permute-start | bytes 1179656 | tf_op jit(solution)/shard_map/ppermute | solution.py:185
  64.3 8.4 %copy-start.4 = (f32[512,512]{1,0:T(8,128)}, f32[512,512]{1,0:T(8,128)S(1)}, u32[]{:S(2)}) copy-start(f32[512,512]{1,0:T(8,128)S(1)} %select_add_fusion.tile_ref) | copy-start | bytes 3145732
  64.3 6.3 %copy-start.7 = (f32[512,512]{1,0:T(8,128)S(1)}, f32[512,512]{1,0:T(8,128)}, u32[]{:S(2)}) copy-start(f32[512,512]{1,0:T(8,128)} %pad_maximum_fusion.1) | copy-start | bytes 3145732
  68.8 3.9 %copy-start.11 = (f32[128,768]{1,0:T(8,128)}, f32[128,768]{1,0:T(8,128)S(1)}, u32[]{:S(2)}) copy-start(f32[128,768]{1,0:T(8,128)S(1)} %broadcast_select_fusion.3) | copy-start | bytes 1179652
  68.8 11.2 %collective-permute-start.4 = (f32[128,768]{1,0:T(8,128)S(1)}, f32[128,768]{1,0:T(8,128)}, u32[]{:S(2)}, u32[]{:S(2)}) collective-permute-start(f32[128,768]{1,0:T(8,128)S(1)} %broadcast_select_fusion.3), channel_id=1, source_target_pairs={{0,1},{1,0},{2,3},{3,2},{4,5},{5,4},{6,7},{7,6},{8,9},{9,8},{10,11... | collective-permute-start | bytes 1179656 | tf_op jit(solution)/shard_map/ppermute | solution.py:187
  72.7 24.6 %all-to-all-start.2 = ((f32[16,32,512]{2,1,0:T(8,128)}), f32[16,32,512]{2,1,0:T(8,128)}, u32[]{:S(2)}, u32[]{:S(2)}) async-start(f32[16,32,512]{2,1,0:T(8,128)} %bitcast.27), calls=%async_computation.2 | async-start | bytes 2097152 | tf_op jit(solution)/shard_map/all_to_all | solution.py:179
  79.9 3.7 %copy-start.15 = (s32[256]{0:T(256)}, s32[256]{0:T(256)S(1)}, u32[]{:S(2)}) copy-start(s32[256]{0:T(256)S(1)} %fusion.17) | copy-start | bytes 3076
  81.1 2.5 %copy-start.5 = (f32[128,768]{1,0:T(8,128)}, f32[128,768]{1,0:T(8,128)S(1)}, u32[]{:S(2)}) copy-start(f32[128,768]{1,0:T(8,128)S(1)} %get-tuple-element.12) | copy-start | bytes 1179652
  81.3 2.3 %copy-start.13 = (f32[256]{0:T(256)}, f32[256]{0:T(256)S(1)}, u32[]{:S(2)}) copy-start(f32[256]{0:T(256)S(1)} %multiply_reduce_fusion.2) | copy-start | bytes 3076
  81.3 2.3 %copy-start.3 = (f32[512,768]{1,0:T(8,128)S(1)}, f32[512,768]{1,0:T(8,128)}, u32[]{:S(2)}) copy-start(f32[512,768]{1,0:T(8,128)} %copy-done.1) | copy-start | bytes 4718596
  85.9 16.8 %copy-start.6 = (f32[128,768]{1,0:T(8,128)S(1)}, f32[128,768]{1,0:T(8,128)}, u32[]{:S(2)}) copy-start(f32[128,768]{1,0:T(8,128)} %copy-done.5) | copy-start | bytes 1179652
  85.9 16.8 %copy-start.14 = (f32[256]{0:T(256)S(1)}, f32[256]{0:T(256)}, u32[]{:S(2)}) copy-start(f32[256]{0:T(256)} %copy-done.13) | copy-start | bytes 3076
  85.9 16.8 %copy-start.16 = (s32[256]{0:T(256)S(1)}, s32[256]{0:T(256)}, u32[]{:S(2)}) copy-start(s32[256]{0:T(256)} %copy-done.15) | copy-start | bytes 3076
  99.4 18.6 %all-to-all-start.3 = ((f32[8,2,4,512]{3,2,1,0:T(4,128)}), f32[8,2,4,512]{3,2,1,0:T(4,128)S(1)}, u32[]{:S(2)}, u32[]{:S(2)}) async-start(f32[8,2,4,512]{3,2,1,0:T(4,128)} %copy.11), calls=%async_computation.3 | async-start | bytes 262144 | tf_op jit(solution)/shard_map/all_to_all | solution.py:182
  117.5 14.4 %copy-start.10 = (f32[256,512]{1,0:T(8,128)S(1)}, f32[256,512]{1,0:T(8,128)}, u32[]{:S(2)}) copy-start(f32[256,512]{1,0:T(8,128)} %get-tuple-element.8) | copy-start | bytes 1572868
  117.5 13.3 %collective-permute-start.5 = (f32[256,512]{1,0:T(8,128)}, f32[256,512]{1,0:T(8,128)S(1)}, u32[]{:S(2)}, u32[]{:S(2)}) collective-permute-start(f32[256,512]{1,0:T(8,128)} %get-tuple-element.7), channel_id=1, source_target_pairs={{0,192},{64,128},{128,64},{192,0},{1,193},{65,129},{129,65},{193,1... | collective-permute-start | bytes 1572872 | tf_op jit(solution)/shard_map/ppermute | solution.py:203

commit v5 on v4

--- a/solution.py
+++ b/solution.py
@@ -14,6 +14,7 @@
 NEAR = ("near", "x")
 ROWS = ("half", "near", "x", "z")
 SUB = 8
+CHUNK = 128
 
 exact_mode = lax.Precision.HIGHEST
 
@@ -50,7 +51,7 @@
     return jnp.sum(x * x, axis=1)
 
 
-def inverse_factor(rows):
+def inverse_factor(rows, between):
     groups = len(rows)
     ids = lax.broadcasted_iota(jnp.int32, (SUB, PW), 0)
     lanes = lax.broadcasted_iota(jnp.int32, (SUB, PW), 1)
@@ -80,18 +81,75 @@
             for row, inv_row, mult in steps:
                 rows[i] = rows[i] - mult[i - b] * row
                 inv[i] = inv[i] - mult[i - b] * inv_row
+        between(b)
     return inv
 
 
-def update_kernel(block_ref, rows_ref, cols_ref, tile_ref, panel_ref, mine_ref, given_ref, first_ref, second_ref):
-    def factor_into(block, out_ref):
-        inv = inverse_factor([block[SUB * g : SUB * g + SUB] for g in range(PW // SUB)])
+def in_three(x):
+    high, rest = x.astype(jnp.bfloat16), x
+    rest = rest - high.astype(jnp.float32)
+    middle = rest.astype(jnp.bfloat16)
+    return high, middle, (rest - middle.astype(jnp.float32)).astype(jnp.bfloat16)
+
+
+def full_dot_t(left, right):
+    total = None
+    for i, j in ((2, 0), (0, 2), (1, 1), (1, 0), (0, 1), (0, 0)):
+        part = lax.dot_general(
+            left[i], right[j], (((1,), (1,)), ((), ())), preferred_element_type=jnp.float32
+        )
+        total = part if total is None else total + part
+    return total
+
+
+def update_kernel(
+    place_ref, ridge_ref, block_ref, heads_ref, head_sq_ref, rows_emb_ref, cols_emb_ref, tile_ref,
+    panel_ref, mine_ref, given_ref, first_ref, second_ref, rows_ref, cols_ref,
+):
+    heads = in_three(heads_ref[...])
+    head_sq = head_sq_ref[...]
+    n_heads, width = heads_ref.shape
+    kept = panel_ref.shape[0]
+    head = lax.broadcasted_iota(jnp.int32, (CHUNK, n_heads), 1)
+    head_place = (head % PW >> 3) * kept + (head // PW) * SUB + (head & (SUB - 1))
+    local = lax.broadcasted_iota(jnp.int32, (CHUNK, n_heads), 0)
+
+    def chunk(step):
+        emb_ref, out_ref, start = (
+            (rows_emb_ref, rows_ref, step * CHUNK)
+            if step < rows_ref.shape[0] // CHUNK
+            else (cols_emb_ref, cols_ref, step * CHUNK - rows_ref.shape[0])
+        )
+        emb = emb_ref[start : start + CHUNK, :]
+        if emb_ref is rows_emb_ref:
+            place = place_ref[start // kept] + start % kept + local
+        else:
+            column = place_ref[2] + start + local
+            place = (column >> 3) * kept + place_ref[3] + (column & (SUB - 1))
+        cross = full_dot_t(in_three(emb), heads)
+        square = jnp.sum(emb * emb, axis=1, keepdims=True)
+        base = jnp.exp(-(square + head_sq - 2.0 * cross) / (2.0 * width))
+        out_ref[start : start + CHUNK, :] = base + jnp.where(place == head_place, ridge_ref[0], 0.0)
+
+    chunks = (rows_ref.shape[0] + cols_ref.shape[0]) // CHUNK
+    groups = PW // SUB
+
+    def between(panel):
+        def run(b):
+            done = panel * groups + b
+            for step in range(done * chunks // (2 * groups), (done + 1) * chunks // (2 * groups)):
+                chunk(step)
+
+        return run
+
+    def factor_into(block, out_ref, run):
+        inv = inverse_factor([block[SUB * g : SUB * g + SUB] for g in range(groups)], run)
         for g, rows in enumerate(inv):
             out_ref[SUB * g : SUB * g + SUB, :] = rows
 
-    factor_into(block_ref[:PW, :PW], first_ref)
+    factor_into(block_ref[:PW, :PW], first_ref, between(0))
     corner = dot_t(block_ref[PW:, :PW], first_ref[...])
-    factor_into(block_ref[PW:, PW:] - dot_t(corner, corner), second_ref)
+    factor_into(block_ref[PW:, PW:] - dot_t(corner, corner), second_ref, between(1))
 
     first, second, below = in_two(first_ref[...]), in_two(second_ref[...]), in_two(corner)
 
@@ -103,7 +161,6 @@
 
     row_left, row_right, row_left_two, row_right_two = panels_of(rows_ref)
     _, _, col_left_two, col_right_two = panels_of(cols_ref)
-    kept = panel_ref.shape[0]
     panel_ref[:, :PW] = row_left[:kept]
     panel_ref[:, PW:] = row_right[:kept]
 
@@ -119,15 +176,18 @@
         )
 
 
-def updated(block, rows, cols, tile):
-    kept = rows.shape[0] // 2
+def updated(place, ridge, block, heads, head_sq, rows_emb, cols_emb, tile):
+    kept = rows_emb.shape[0] // 2
     wide = jax.ShapeDtypeStruct((kept, tile.shape[1]), jnp.float32)
+    scalar = pl.BlockSpec(memory_space=pltpu.SMEM)
     return pl.pallas_call(
         update_kernel,
         out_shape=(jax.ShapeDtypeStruct((kept, 2 * PW), jnp.float32), wide, wide),
-        scratch_shapes=[pltpu.VMEM((PW, PW), jnp.float32)] * 2,
-        cost_estimate=pl.CostEstimate(flops=400_000_000, bytes_accessed=4_000_000, transcendentals=256),
-    )(block, rows, cols, tile)
+        in_specs=[scalar, scalar] + [pl.BlockSpec(memory_space=pltpu.VMEM)] * 6,
+        scratch_shapes=[pltpu.VMEM((PW, PW), jnp.float32)] * 2
+        + [pltpu.VMEM((emb.shape[0], 2 * PW), jnp.float32) for emb in (rows_emb, cols_emb)],
+        cost_estimate=pl.CostEstimate(flops=900_000_000, bytes_accessed=8_000_000, transcendentals=256),
+    )(place, ridge, block, heads, head_sq, rows_emb, cols_emb, tile)
 
 
 def per_device(points, landmark_index, targets, ridge_shift):
@@ -170,7 +230,9 @@
     col_place = column // quarter * rows_here + col_pos * quarter + column % quarter
 
     tile = gaussian(rows_emb, rows_sq, column_emb, col_sq)
-    tile = tile + jnp.where(row_place[:, None] == col_place[None, :], ridge, 0.0)
+    tile = lax.optimization_barrier(
+        tile + jnp.where(row_place[:, None] == col_place[None, :], ridge, 0.0)
+    )
     partial = lax.dot_general(
         pair_targets, tile, (((0,), (0,)), ((), ())), precision=lax.Precision.HIGH, preferred_element_type=jnp.float32
     )
@@ -193,10 +255,17 @@
         base = gaussian(emb, emb_sq, heads, heads_sq)
         return base + jnp.where(place[:, None] == head_place[None, :], ridge, 0.0)
 
+    places = jnp.stack(
+        [row_pos * rows_here, peer_pos * rows_here, half_pos * half, col_pos * quarter]
+    ).astype(jnp.int32)
     operands = (
+        places,
+        ridge_shift,
         at_heads(heads, heads_sq, head_place),
-        at_heads(rows_emb, rows_sq, row_place),
-        at_heads(column_emb, col_sq, col_place),
+        heads,
+        heads_sq[None, :],
+        rows_emb,
+        column_emb,
         tile,
     )
     panels, mine, given = updated(*operands)

time: 134 us -> 134 us (level)
  matrix products: 11.1 us -> 6.53 us
  Pallas kernels: 13.1 us -> 16.1 us
  waiting for transfers between devices: 48.6 us -> 50.3 us
    dot_general x4 -> x2, matrix products: 9.08 us -> 4.48 us  [dot_t(): lax.dot_general(left, right, (((1,), (1,)), ((), ())), precision=exact_mo...]
    pallas_call x1, Pallas kernels: 13.1 us -> 16.1 us  [updated(): pl.pallas_call(update_kernel, out_shape=(jax.ShapeDtypeStruct((kept, 2 *...]
    all_to_all x1, waiting for transfers between devices: 11.3 us -> 13 us  [per_device(): lax.all_to_all(partial.reshape(n_plane, -1, half), PLANE, 0, 0, tiled=True)]
  transfers between devices with their start and end apart: 10 -> 10, of which waited for: 5 -> 5; matrix products, arithmetic and copies ran while one was open for 16% -> 13% of each run, Pallas kernels for 10% -> 12%
where the time goes in v5:
time: 134 us; the launch traced here: 133 us
  waiting for transfers between devices  50.3 us (38%)
  starting transfers between devices  40.3 us (30%)
  Pallas kernels  16.1 us (12%)
  other arithmetic  10.4 us (8%)
  local copies, waits for them, and re-layouts  8.19 us (6%)
  matrix products  6.53 us (5%)
  between operations  1.53 us (1%)
    pallas_call x1, Pallas kernels, updated(): pl.pallas_call(update_kernel, out_shape=(jax.ShapeDtypeStruct((kept, 2 *...  16.1 us
    ppermute x1, waiting for transfers between devices, per_device(): peer_embedded = lax.ppermute(embedded, Y, across)  15.1 us
    all_to_all x2, starting transfers between devices, to_all(): lax.all_to_all(jnp.broadcast_to(x[None], (peers, *x.shape)), axis, 0, 0,...  14 us
    all_to_all x1, waiting for transfers between devices, per_device(): lax.all_to_all(partial.reshape(n_plane, -1, half), PLANE, 0, 0, tiled=True)  13 us
    ppermute x1, waiting for transfers between devices, per_device(): taken = lax.ppermute(given, Y, across)  12.2 us
    all_to_all x1, starting transfers between devices, per_device(): lax.all_to_all(partial.reshape(n_plane, -1, half), PLANE, 0, 0, tiled=True)  7.2 us
    all_to_all x2, waiting for transfers between devices, to_all(): lax.all_to_all(jnp.broadcast_to(x[None], (peers, *x.shape)), axis, 0, 0,...  5.44 us
    ppermute x1, starting transfers between devices, per_device(): lax.ppermute(column_emb[:PW], Y, [(y, n_y - 1 - y) for y in range(n_y //...  4.59 us
  transfers between devices with their start and end apart: 10, of which 5 were waited for; matrix products, arithmetic and copies ran while one was open for 13% of the time, Pallas kernels for 12%

profile of v5, /device:TPU:1, one launch (start us, length us, event | category | flops | bytes accessed | tf_op | source)
XLA Modules:
  0.0 133.3 jit_solution(8006926043535578247)
XLA Ops:
  0.6 0.0 copy-start
  0.7 0.8 compare_select_fusion
  1.5 0.6 copy-done
  2.1 1.1 gather_fusion
  3.2 0.0 copy-start.6
  3.2 0.8 broadcast_in_dim.25
  4.0 9.0 %all-to-all-start = ((f32[8,8,768]{2,1,0:T(8,128)}), f32[8,8,768]{2,1,0:T(8,128)S(1)}, u32[]{:S(2)}, u32[]{:S(2)}) async-start(f32[8,8,768]{2,1,0:T(8,128)} %broadcast_in_dim.25), calls=%async_computation | async-start | bytes 393216 | tf_op jit(solution)/shard_map/all_to_all | solution.py:24
  13.0 2.8 %collective-permute-start = (f32[256,256]{1,0:T(8,128)S(1)}, f32[256,256]{1,0:T(8,128)}, u32[]{:S(2)}, u32[]{:S(2)}) collective-permute-start(f32[256,256]{1,0:T(8,128)S(1)} %copy-done.9), channel_id=1, source_target_pairs={{0,192},{64,128},{128,64},{192,0},{1,193},{65,129},{129,65},{193,1... | collective-permute-start | bytes 786440 | tf_op jit(solution)/shard_map/ppermute | solution.py:219
  15.8 0.7 constant_dynamic-update-slice_fusion.1
  16.5 5.4 %all-to-all-done = f32[8,8,768]{2,1,0:T(8,128)S(1)} async-done(((f32[8,8,768]{2,1,0:T(8,128)}), f32[8,8,768]{2,1,0:T(8,128)S(1)}, u32[]{:S(2)}, u32[]{:S(2)}) %all-to-all-start) | async-done | bytes 196640 | tf_op jit(solution)/shard_map/all_to_all | solution.py:24
  22.0 1.3 broadcast_in_dim.44
  23.2 5.0 %all-to-all-start.1 = ((f32[8,8,8,768]{3,2,1,0:T(8,128)}), f32[8,8,8,768]{3,2,1,0:T(8,128)S(1)}, u32[]{:S(2)}, u32[]{:S(2)}) async-start(f32[8,8,8,768]{3,2,1,0:T(8,128)} %broadcast_in_dim.44), calls=%async_computation.1 | async-start | bytes 3145728 | tf_op jit(solution)/shard_map/all_to_all | solution.py:24
  28.3 0.0 collective-permute-done
  28.3 1.7 %constant_dynamic-update-slice_fusion = f32[512,256]{1,0:T(8,128)} fusion(f32[512,256]{1,0:T(8,128)} %constant_dynamic-update-slice_fusion.1, f32[256,256]{1,0:T(8,128)} %collective-permute-done), kind=kLoop, calls=%fused_computation.28 | loop fusion | bytes 524288 | tf_op jit(solution)/shard_map/concatenate | solution.py:219
  30.0 2.7 %collective-permute-start.1 = (f32[512,256]{1,0:T(8,128)}, f32[512,256]{1,0:T(8,128)}, u32[]{:S(2)}, u32[]{:S(2)}) collective-permute-start(f32[512,256]{1,0:T(8,128)} %constant_dynamic-update-slice_fusion), channel_id=1, source_target_pairs={{0,1},{1,0},{2,3},{3,2},{4,5},{5,4},{6,7},{7,6},{8,9},{9,8},{10,11... | collective-permute-start | bytes 1572872 | tf_op jit(solution)/shard_map/ppermute | solution.py:220
  32.7 3.2 %collective-permute-start.2 = (f32[256,768]{1,0:T(8,128)}, f32[256,768]{1,0:T(8,128)}, u32[]{:S(2)}, u32[]{:S(2)}) collective-permute-start(f32[256,768]{1,0:T(8,128)} %copy-done.6), channel_id=1, source_target_pairs={{0,192},{64,128},{128,64},{192,0},{1,193},{65,129},{129,65},{193,1... | collective-permute-start | bytes 2359304 | tf_op jit(solution)/shard_map/ppermute | solution.py:216
  36.6 0.0 collective-permute-done.1
  36.6 1.3 broadcast_select_fusion.2
  37.8 0.0 copy-start.7
  37.9 1.1 pad_maximum_fusion.1
  39.0 15.1 %collective-permute-done.2 = f32[256,768]{1,0:T(8,128)} collective-permute-done((f32[256,768]{1,0:T(8,128)}, f32[256,768]{1,0:T(8,128)}, u32[]{:S(2)}, u32[]{:S(2)}) %collective-permute-start.2) | collective-permute-done | bytes 786464 | tf_op jit(solution)/shard_map/ppermute | solution.py:216
  54.1 1.2 pad_maximum_fusion.rows_emb_ref
  55.3 1.2 copy-done.2
  56.5 0.2 multiply_reduce_fusion.1
  56.7 4.6 %collective-permute-start.3 = (f32[128,768]{1,0:T(8,128)S(1)}, f32[128,768]{1,0:T(8,128)S(1)}, u32[]{:S(2)}, u32[]{:S(2)}) collective-permute-start(f32[128,768]{1,0:T(8,128)S(1)} %slice.21), channel_id=1, source_target_pairs={{0,192},{64,128},{1,193},{65,129},{2,194},{66,130},{3,195},{67,131... | collective-permute-start | bytes 1179656 | tf_op jit(solution)/shard_map/ppermute | solution.py:247
  61.3 0.2 multiply_reduce_fusion
  61.5 2.9 %select_add_fusion.tile_ref = f32[512,512]{1,0:T(8,128)S(1)} fusion(f32[]{:T(128)} %bitcast.21, s32[512]{0:T(512)S(1)} %fusion.7, f32[512,768]{1,0:T(8,128)S(1)} %copy-done.3, f32[512,768]{1,0:T(8,128)S(1)} %bitcast.25, f32[512]{0:T(512)S(1)} %multiply_reduce_fusion, f32[512]{0:T(512)S(1)} %multiply_reduce_fusion.1, s32[512]{0:T(512)S(1)} %pad_add_fusion), kind=kOutput, calls=%fused_computation.13 | convolution fusion | flops 2418016256 | bytes 4202500 | tf_op jit(solution)/shard_map/dot_general | solution.py:28
  64.4 4.5 %collective-permute-done.3 = f32[128,768]{1,0:T(8,128)S(1)} collective-permute-done((f32[128,768]{1,0:T(8,128)S(1)}, f32[128,768]{1,0:T(8,128)S(1)}, u32[]{:S(2)}, u32[]{:S(2)}) %collective-permute-start.3) | collective-permute-done | bytes 393248 | tf_op jit(solution)/shard_map/ppermute | solution.py:247
  68.9 0.1 broadcast_select_fusion.3
  69.0 1.8 %collective-permute-start.4 = (f32[128,768]{1,0:T(8,128)S(1)}, f32[128,768]{1,0:T(8,128)}, u32[]{:S(2)}, u32[]{:S(2)}) collective-permute-start(f32[128,768]{1,0:T(8,128)S(1)} %broadcast_select_fusion.3), channel_id=1, source_target_pairs={{0,1},{1,0},{2,3},{3,2},{4,5},{5,4},{6,7},{7,6},{8,9},{9,8},{10,11... | collective-permute-start | bytes 1179656 | tf_op jit(solution)/shard_map/ppermute | solution.py:249
  70.8 2.0 %fusion.15 = f32[512,512]{1,0:T(8,128)} fusion(f32[512,512]{1,0:T(8,128)S(1)} %copy-done.5, f32[512,512]{1,0:T(8,128)S(1)} %select_add_fusion.tile_ref), kind=kOutput, calls=%fused_computation.64 | convolution fusion | flops 805306368 | bytes 3145728 | tf_op jit(solution)/shard_map/dot_general | solution.py:236
  72.8 7.2 %all-to-all-start.2 = ((f32[16,32,512]{2,1,0:T(8,128)}), f32[16,32,512]{2,1,0:T(8,128)S(1)}, u32[]{:S(2)}, u32[]{:S(2)}) async-start(f32[16,32,512]{2,1,0:T(8,128)} %bitcast.2), calls=%async_computation.2 | async-start | bytes 2097152 | tf_op jit(solution)/shard_map/all_to_all | solution.py:241
  80.0 0.7 pad_add_fusion.1.place_ref
  80.7 1.1 broadcast_select_fusion.5
  81.8 0.9 pad_maximum_fusion.3
  82.7 1.6 %fusion.4.block_ref = f32[256,256]{1,0:T(8,128)} fusion(f32[]{:T(128)} %bitcast.22, s32[256]{0:T(256)S(1)} %fusion.12, f32[256]{0:T(256)S(1)} %get-tuple-element.12, f32[128,768]{1,0:T(8,128)S(1)} %get-tuple-element.14, f32[128,768]{1,0:T(8,128)S(1)} %get-tuple-element.13), kind=kOutput, calls=%fused_computation.10 | convolution fusion | flops 604700672 | bytes 1050628 | tf_op jit(solution)/shard_map/dot_general | solution.py:28
  84.3 13.0 %all-to-all-done.2 = f32[16,32,512]{2,1,0:T(8,128)S(1)} async-done(((f32[16,32,512]{2,1,0:T(8,128)}), f32[16,32,512]{2,1,0:T(8,128)S(1)}, u32[]{:S(2)}, u32[]{:S(2)}) %all-to-all-start.2) | async-done | bytes 1048608 | tf_op jit(solution)/shard_map/all_to_all | solution.py:241
  97.3 0.1 bitcast_reduce_fusion
  97.4 0.1 copy.8
  97.5 0.7 copy.9
  98.2 3.6 %all-to-all-start.3 = ((f32[8,2,4,512]{3,2,1,0:T(4,128)}), f32[8,2,4,512]{3,2,1,0:T(4,128)S(1)}, u32[]{:S(2)}, u32[]{:S(2)}) async-start(f32[8,2,4,512]{3,2,1,0:T(4,128)} %copy.9), calls=%async_computation.3 | async-start | bytes 262144 | tf_op jit(solution)/shard_map/all_to_all | solution.py:244
  101.8 16.1 %shard_map.67 = (f32[256,256]{1,0:T(8,128)}, f32[256,512]{1,0:T(8,128)}, f32[256,512]{1,0:T(8,128)}) custom-call(s32[4]{0:T(128)} %pad_add_fusion.1.place_ref, f32[1]{0:T(128)} %copy.11.ridge_ref, f32[256,256]{1,0:T(8,128)} %fusion.4.block_ref, f32[256,768]{1,0:T(8,128)} %get-tuple-element.11.heads_ref, f32[1,256]{1,0:T(1,128)} %bitcast.29, ...), custom_call_target="tpu_custom_call" | custom-call | flops 900000000 | bytes 8000000 | tf_op jit(solution)/shard_map/pallas_call | solution.py:183
  117.8 0.4 collective-permute-start.5
  118.3 0.6 pad_maximum_fusion.4
  118.9 12.2 %collective-permute-done.5 = f32[256,512]{1,0:T(8,128)S(1)} collective-permute-done((f32[256,512]{1,0:T(8,128)}, f32[256,512]{1,0:T(8,128)S(1)}, u32[]{:S(2)}, u32[]{:S(2)}) %collective-permute-start.5) | collective-permute-done | bytes 524320 | tf_op jit(solution)/shard_map/ppermute | solution.py:272
  131.2 1.0 slice_select_fusion
  132.2 0.1 broadcast_select_fusion
  132.3 1.0 pad_maximum_fusion.2
  (29 shorter events, 0.2 us)
Async XLA Ops:
  0.6 1.4 %copy-start = (f32[512,768]{1,0:T(8,128)S(1)}, f32[512,768]{1,0:T(8,128)}, u32[]{:S(2)}) copy-start(f32[512,768]{1,0:T(8,128)} %param.4) | copy-start | bytes 4718596
  2.1 10.9 %copy-start.9 = (f32[256,256]{1,0:T(8,128)S(1)}, f32[256,256]{1,0:T(8,128)}, u32[]{:S(2)}) copy-start(f32[256,256]{1,0:T(8,128)} %param.6) | copy-start | bytes 786436
  3.2 20.1 %copy-start.6 = (f32[256,768]{1,0:T(8,128)}, f32[256,768]{1,0:T(8,128)S(1)}, u32[]{:S(2)}) copy-start(f32[256,768]{1,0:T(8,128)S(1)} %gather_fusion) | copy-start | bytes 2359300
  4.0 18.0 %all-to-all-start = ((f32[8,8,768]{2,1,0:T(8,128)}), f32[8,8,768]{2,1,0:T(8,128)S(1)}, u32[]{:S(2)}, u32[]{:S(2)}) async-start(f32[8,8,768]{2,1,0:T(8,128)} %broadcast_in_dim.25), calls=%async_computation | async-start | bytes 393216 | tf_op jit(solution)/shard_map/all_to_all | solution.py:24
  13.0 15.3 %collective-permute-start = (f32[256,256]{1,0:T(8,128)S(1)}, f32[256,256]{1,0:T(8,128)}, u32[]{:S(2)}, u32[]{:S(2)}) collective-permute-start(f32[256,256]{1,0:T(8,128)S(1)} %copy-done.9), channel_id=1, source_target_pairs={{0,192},{64,128},{128,64},{192,0},{1,193},{65,129},{129,65},{193,1... | collective-permute-start | bytes 786440 | tf_op jit(solution)/shard_map/ppermute | solution.py:219
  23.2 33.4 %all-to-all-start.1 = ((f32[8,8,8,768]{3,2,1,0:T(8,128)}), f32[8,8,8,768]{3,2,1,0:T(8,128)S(1)}, u32[]{:S(2)}, u32[]{:S(2)}) async-start(f32[8,8,8,768]{3,2,1,0:T(8,128)} %broadcast_in_dim.44), calls=%async_computation.1 | async-start | bytes 3145728 | tf_op jit(solution)/shard_map/all_to_all | solution.py:24
  30.0 6.6 %collective-permute-start.1 = (f32[512,256]{1,0:T(8,128)}, f32[512,256]{1,0:T(8,128)}, u32[]{:S(2)}, u32[]{:S(2)}) collective-permute-start(f32[512,256]{1,0:T(8,128)} %constant_dynamic-update-slice_fusion), channel_id=1, source_target_pairs={{0,1},{1,0},{2,3},{3,2},{4,5},{5,4},{6,7},{7,6},{8,9},{9,8},{10,11... | collective-permute-start | bytes 1572872 | tf_op jit(solution)/shard_map/ppermute | solution.py:220
  32.7 21.4 %collective-permute-start.2 = (f32[256,768]{1,0:T(8,128)}, f32[256,768]{1,0:T(8,128)}, u32[]{:S(2)}, u32[]{:S(2)}) collective-permute-start(f32[256,768]{1,0:T(8,128)} %copy-done.6), channel_id=1, source_target_pairs={{0,192},{64,128},{128,64},{192,0},{1,193},{65,129},{129,65},{193,1... | collective-permute-start | bytes 2359304 | tf_op jit(solution)/shard_map/ppermute | solution.py:216
  37.8 16.2 %copy-start.7 = (f32[256,768]{1,0:T(8,128)S(1)}, f32[256,768]{1,0:T(8,128)}, u32[]{:S(2)}) copy-start(f32[256,768]{1,0:T(8,128)} %copy-done.6) | copy-start | bytes 2359300
  55.3 1.2 copy-start.2
  56.7 12.2 %copy-start.1 = (f32[8,8,8,768]{3,2,1,0:T(8,128)}, f32[8,8,8,768]{3,2,1,0:T(8,128)S(1)}, u32[]{:S(2)}) copy-start(f32[8,8,8,768]{3,2,1,0:T(8,128)S(1)} %all-to-all-done.1) | copy-start | bytes 4718596
  56.7 4.8 %copy-start.3 = (f32[512,768]{1,0:T(8,128)S(1)}, f32[512,768]{1,0:T(8,128)}, u32[]{:S(2)}) copy-start(f32[512,768]{1,0:T(8,128)} %copy-done.2) | copy-start | bytes 4718596
  56.7 12.2 %collective-permute-start.3 = (f32[128,768]{1,0:T(8,128)S(1)}, f32[128,768]{1,0:T(8,128)S(1)}, u32[]{:S(2)}, u32[]{:S(2)}) collective-permute-start(f32[128,768]{1,0:T(8,128)S(1)} %slice.21), channel_id=1, source_target_pairs={{0,192},{64,128},{1,193},{65,129},{2,194},{66,130},{3,195},{67,131... | collective-permute-start | bytes 1179656 | tf_op jit(solution)/shard_map/ppermute | solution.py:247
  64.4 8.4 %copy-start.4 = (f32[512,512]{1,0:T(8,128)}, f32[512,512]{1,0:T(8,128)S(1)}, u32[]{:S(2)}) copy-start(f32[512,512]{1,0:T(8,128)S(1)} %select_add_fusion.tile_ref) | copy-start | bytes 3145732
  64.4 6.3 %copy-start.5 = (f32[512,512]{1,0:T(8,128)S(1)}, f32[512,512]{1,0:T(8,128)}, u32[]{:S(2)}) copy-start(f32[512,512]{1,0:T(8,128)} %pad_maximum_fusion.1) | copy-start | bytes 3145732
  69.0 11.8 %collective-permute-start.4 = (f32[128,768]{1,0:T(8,128)S(1)}, f32[128,768]{1,0:T(8,128)}, u32[]{:S(2)}, u32[]{:S(2)}) collective-permute-start(f32[128,768]{1,0:T(8,128)S(1)} %broadcast_select_fusion.3), channel_id=1, source_target_pairs={{0,1},{1,0},{2,3},{3,2},{4,5},{5,4},{6,7},{7,6},{8,9},{9,8},{10,11... | collective-permute-start | bytes 1179656 | tf_op jit(solution)/shard_map/ppermute | solution.py:249
  72.8 24.5 %all-to-all-start.2 = ((f32[16,32,512]{2,1,0:T(8,128)}), f32[16,32,512]{2,1,0:T(8,128)S(1)}, u32[]{:S(2)}, u32[]{:S(2)}) async-start(f32[16,32,512]{2,1,0:T(8,128)} %bitcast.2), calls=%async_computation.2 | async-start | bytes 2097152 | tf_op jit(solution)/shard_map/all_to_all | solution.py:241
  82.7 15.5 %copy-start.10 = (f32[256]{0:T(256)}, f32[256]{0:T(256)S(1)}, u32[]{:S(2)}) copy-start(f32[256]{0:T(256)S(1)} %get-tuple-element.12) | copy-start | bytes 3076
  98.2 20.1 %all-to-all-start.3 = ((f32[8,2,4,512]{3,2,1,0:T(4,128)}), f32[8,2,4,512]{3,2,1,0:T(4,128)S(1)}, u32[]{:S(2)}, u32[]{:S(2)}) async-start(f32[8,2,4,512]{3,2,1,0:T(4,128)} %copy.9), calls=%async_computation.3 | async-start | bytes 262144 | tf_op jit(solution)/shard_map/all_to_all | solution.py:244
  117.8 14.4 %copy-start.8 = (f32[256,512]{1,0:T(8,128)S(1)}, f32[256,512]{1,0:T(8,128)}, u32[]{:S(2)}) copy-start(f32[256,512]{1,0:T(8,128)} %get-tuple-element.8) | copy-start | bytes 1572868
  117.8 13.3 %collective-permute-start.5 = (f32[256,512]{1,0:T(8,128)}, f32[256,512]{1,0:T(8,128)S(1)}, u32[]{:S(2)}, u32[]{:S(2)}) collective-permute-start(f32[256,512]{1,0:T(8,128)} %get-tuple-element.7), channel_id=1, source_target_pairs={{0,192},{64,128},{128,64},{192,0},{1,193},{65,129},{129,65},{193,1... | collective-permute-start | bytes 1572872 | tf_op jit(solution)/shard_map/ppermute | solution.py:272

commit v6 on v5

--- a/solution.py
+++ b/solution.py
@@ -103,12 +103,26 @@
 
 
 def update_kernel(
-    place_ref, ridge_ref, block_ref, heads_ref, head_sq_ref, rows_emb_ref, cols_emb_ref, tile_ref,
+    place_ref, ridge_ref, head_0_ref, head_1_ref, rows_emb_ref, cols_emb_ref, tile_ref,
     panel_ref, mine_ref, given_ref, first_ref, second_ref, rows_ref, cols_ref,
 ):
-    heads = in_three(heads_ref[...])
-    head_sq = head_sq_ref[...]
-    n_heads, width = heads_ref.shape
+    head_emb = jnp.concatenate([head_0_ref[...], head_1_ref[...]], axis=0)
+    heads = in_three(head_emb)
+    n_heads, width = head_emb.shape
+    ones = jnp.ones((SUB, width), jnp.bfloat16)
+    head_sq = sum(
+        lax.dot_general(ones, part, (((1,), (1,)), ((), ())), preferred_element_type=jnp.float32)
+        for part in reversed(in_three(head_emb * head_emb))
+    )[:1]
+
+    def distances(emb, parts):
+        square = jnp.sum(emb * emb, axis=1, keepdims=True)
+        return jnp.exp(-(square + head_sq - 2.0 * full_dot_t(parts, heads)) / (2.0 * width))
+
+    same = lax.broadcasted_iota(jnp.int32, (n_heads, n_heads), 0) == lax.broadcasted_iota(
+        jnp.int32, (n_heads, n_heads), 1
+    )
+    block = distances(head_emb, heads) + jnp.where(same, ridge_ref[0], 0.0)
     kept = panel_ref.shape[0]
     head = lax.broadcasted_iota(jnp.int32, (CHUNK, n_heads), 1)
     head_place = (head % PW >> 3) * kept + (head // PW) * SUB + (head & (SUB - 1))
@@ -126,9 +140,7 @@
         else:
             column = place_ref[2] + start + local
             place = (column >> 3) * kept + place_ref[3] + (column & (SUB - 1))
-        cross = full_dot_t(in_three(emb), heads)
-        square = jnp.sum(emb * emb, axis=1, keepdims=True)
-        base = jnp.exp(-(square + head_sq - 2.0 * cross) / (2.0 * width))
+        base = distances(emb, in_three(emb))
         out_ref[start : start + CHUNK, :] = base + jnp.where(place == head_place, ridge_ref[0], 0.0)
 
     chunks = (rows_ref.shape[0] + cols_ref.shape[0]) // CHUNK
@@ -147,9 +159,9 @@
         for g, rows in enumerate(inv):
             out_ref[SUB * g : SUB * g + SUB, :] = rows
 
-    factor_into(block_ref[:PW, :PW], first_ref, between(0))
-    corner = dot_t(block_ref[PW:, :PW], first_ref[...])
-    factor_into(block_ref[PW:, PW:] - dot_t(corner, corner), second_ref, between(1))
+    factor_into(block[:PW, :PW], first_ref, between(0))
+    corner = dot_t(block[PW:, :PW], first_ref[...])
+    factor_into(block[PW:, PW:] - dot_t(corner, corner), second_ref, between(1))
 
     first, second, below = in_two(first_ref[...]), in_two(second_ref[...]), in_two(corner)
 
@@ -176,18 +188,54 @@
         )
 
 
-def updated(place, ridge, block, heads, head_sq, rows_emb, cols_emb, tile):
+def updated(place, ridge, head_0, head_1, rows_emb, cols_emb, tile):
     kept = rows_emb.shape[0] // 2
     wide = jax.ShapeDtypeStruct((kept, tile.shape[1]), jnp.float32)
     scalar = pl.BlockSpec(memory_space=pltpu.SMEM)
     return pl.pallas_call(
         update_kernel,
         out_shape=(jax.ShapeDtypeStruct((kept, 2 * PW), jnp.float32), wide, wide),
-        in_specs=[scalar, scalar] + [pl.BlockSpec(memory_space=pltpu.VMEM)] * 6,
+        in_specs=[scalar, scalar] + [pl.BlockSpec(memory_space=pltpu.VMEM)] * 5,
         scratch_shapes=[pltpu.VMEM((PW, PW), jnp.float32)] * 2
         + [pltpu.VMEM((emb.shape[0], 2 * PW), jnp.float32) for emb in (rows_emb, cols_emb)],
         cost_estimate=pl.CostEstimate(flops=900_000_000, bytes_accessed=8_000_000, transcendentals=256),
-    )(place, ridge, block, heads, head_sq, rows_emb, cols_emb, tile)
+    )(place, ridge, head_0, head_1, rows_emb, cols_emb, tile)
+
+
+def take_kernel(start_ref, index_ref, points_ref, emb_ref, own_ref):
+    point = lax.broadcasted_iota(jnp.int32, (points_ref.shape[0], index_ref.shape[1]), 0)
+    hot = jnp.where(point == index_ref[...] - start_ref[0], 1.0, 0.0).astype(jnp.bfloat16)
+    high, middle, low = (
+        lax.dot_general(hot, part, (((0,), (0,)), ((), ())), preferred_element_type=jnp.float32)
+        for part in in_three(points_ref[...])
+    )
+    emb_ref[...] = high + middle + low
+    own = emb_ref[pl.ds(pl.multiple_of(start_ref[1], SUB), SUB), :]
+    for peer in range(own_ref.shape[0]):
+        own_ref[peer] = own
+
+
+def taken_rows(start, index, points, peers):
+    width = points.shape[1]
+    vmem = pl.BlockSpec(memory_space=pltpu.VMEM)
+    return pl.pallas_call(
+        take_kernel,
+        out_shape=(
+            jax.ShapeDtypeStruct((index.shape[0], width), jnp.float32),
+            jax.ShapeDtypeStruct((peers, SUB, width), jnp.float32),
+        ),
+        in_specs=[pl.BlockSpec(memory_space=pltpu.SMEM), vmem, vmem],
+        compiler_params=pltpu.CompilerParams(vmem_limit_bytes=20 * 2**20),
+        cost_estimate=pl.CostEstimate(flops=600_000_000, bytes_accessed=3_000_000, transcendentals=0),
+    )(start, index[None, :], points)
+
+
+def chosen(*values):
+    slots = lax.iota(jnp.int32, len(values))
+    table = jnp.zeros(len(values), jnp.int32)
+    for slot, value in enumerate(values):
+        table = jnp.where(slots == slot, value, table)
+    return table
 
 
 def per_device(points, landmark_index, targets, ridge_shift):
@@ -210,20 +258,23 @@
     def ordered(flag, mine, other, axis):
         return jnp.concatenate([jnp.where(flag, other, mine), jnp.where(flag, mine, other)], axis=axis)
 
-    local_index = landmark_index - row_pos * block_points
-    embedded = points.at[local_index].get(mode="promise_in_bounds")
-    own = lax.dynamic_slice_in_dim(embedded, col_pos * quarter, quarter, 0)
+    n_z = lax.axis_size("z")
+    start = chosen(row_pos * block_points, col_pos * quarter, half_pos * half)
+    embedded, own_copies = taken_rows(start, landmark_index, points, n_z)
     peer_embedded = lax.ppermute(embedded, Y, across)
-    own_line = to_all(own, "z")
+    own_line = lax.all_to_all(own_copies, "z", 0, 0, tiled=True)
     column_emb = lax.optimization_barrier(to_all(own_line, NEAR).reshape(half, -1))
     own_targets = jnp.concatenate([targets, lax.ppermute(targets, Y, across)], axis=0)
     peer_targets = lax.ppermute(own_targets, "cols", swap)
     pair_targets = lax.optimization_barrier(ordered(col_pos == 1, own_targets, peer_targets, 1))
-    rows_emb = lax.optimization_barrier(jnp.concatenate([embedded, peer_embedded], axis=0))
+    peer_pos = row_pos + (n_y - 1 - 2 * y_pos) * per_y
+    places = chosen(row_pos * rows_here, peer_pos * rows_here, half_pos * half, col_pos * quarter)
+    rows_emb, places = lax.optimization_barrier(
+        (jnp.concatenate([embedded, peer_embedded], axis=0), places)
+    )
 
     rows_sq = squares(rows_emb)
     col_sq = squares(column_emb)
-    peer_pos = row_pos + (n_y - 1 - 2 * y_pos) * per_y
     local = lax.iota(jnp.int32, rows_here)
     row_place = jnp.concatenate([row_pos * rows_here + local, peer_pos * rows_here + local])
     column = half_pos * half + lax.iota(jnp.int32, half)
@@ -237,7 +288,6 @@
         pair_targets, tile, (((0,), (0,)), ((), ())), precision=lax.Precision.HIGH, preferred_element_type=jnp.float32
     )
     n_plane = lax.axis_size(PLANE)
-    n_z = lax.axis_size("z")
     arrived = lax.all_to_all(partial.reshape(n_plane, -1, half), PLANE, 0, 0, tiled=True)
     nearer = arrived.reshape(2, n_plane // 2, -1, half).sum(axis=1)
     nearer = nearer.reshape(2, n_z, -1, half).swapaxes(0, 1)
@@ -246,29 +296,14 @@
 
     sent_heads = lax.ppermute(column_emb[:PW], Y, [(y, n_y - 1 - y) for y in range(n_y // 2)])
     own_heads = jnp.where(upper, sent_heads, column_emb[:PW])
-    heads = ordered(col_pos == 1, own_heads, lax.ppermute(own_heads, "cols", swap), 0)
-    heads_sq = squares(heads)
-    head = lax.iota(jnp.int32, 2 * PW)
-    head_place = head % PW // quarter * rows_here + head // PW * quarter + head % quarter
-
-    def at_heads(emb, emb_sq, place):
-        base = gaussian(emb, emb_sq, heads, heads_sq)
-        return base + jnp.where(place[:, None] == head_place[None, :], ridge, 0.0)
-
-    places = jnp.stack(
-        [row_pos * rows_here, peer_pos * rows_here, half_pos * half, col_pos * quarter]
-    ).astype(jnp.int32)
-    operands = (
-        places,
-        ridge_shift,
-        at_heads(heads, heads_sq, head_place),
-        heads,
-        heads_sq[None, :],
-        rows_emb,
-        column_emb,
-        tile,
-    )
-    panels, mine, given = updated(*operands)
+    peer_heads = lax.ppermute(own_heads, "cols", swap)
+    swapped = col_pos == 1
+    head_0 = jnp.where(swapped, peer_heads, own_heads)
+    head_1 = jnp.where(swapped, own_heads, peer_heads)
+
+    panels, mine, given = updated(
+        places, ridge_shift, head_0, head_1, rows_emb, column_emb, tile
+    )
     taken = lax.ppermute(given, Y, across)
     remainder = jnp.concatenate(
         [jnp.where(upper, taken, mine)[:, PW:], jnp.where(upper, mine, taken)], axis=1

time: 134 us -> 125 us (0.933)
  the two profiles are of different devices: /device:TPU:1 before, /device:TPU:32 now
where the time goes in v6:
time: 125 us
  waiting for transfers between devices  49.9 us (40%)
  starting transfers between devices  36 us (29%)
  Pallas kernels  20.1 us (16%)
  other arithmetic  6.25 us (5%)
  local copies, waits for them, and re-layouts  6.15 us (5%)
  matrix products  4.95 us (4%)
  between operations  1.52 us (1%)
    pallas_call x1, Pallas kernels, updated(): pl.pallas_call(update_kernel, out_shape=(jax.ShapeDtypeStruct((kept, 2 *...  18 us
    ppermute x1, waiting for transfers between devices, per_device(): peer_embedded = lax.ppermute(embedded, Y, across)  16.7 us
    all_to_all x1, waiting for transfers between devices, per_device(): lax.all_to_all(partial.reshape(n_plane, -1, half), PLANE, 0, 0, tiled=True)  14.1 us
    ppermute x1, waiting for transfers between devices, per_device(): taken = lax.ppermute(given, Y, across)  11.3 us
    all_to_all x1, starting transfers between devices, per_device(): own_line = lax.all_to_all(own_copies, 'z', 0, 0, tiled=True)  8.57 us
    all_to_all x1, waiting for transfers between devices, per_device(): own_line = lax.all_to_all(own_copies, 'z', 0, 0, tiled=True)  5.98 us
    ppermute x1, starting transfers between devices, per_device(): lax.ppermute(column_emb[:PW], Y, [(y, n_y - 1 - y) for y in range(n_y //...  5.79 us
    all_to_all x1, starting transfers between devices, to_all(): lax.all_to_all(jnp.broadcast_to(x[None], (peers, *x.shape)), axis, 0, 0,...  5.31 us
  transfers between devices with their start and end apart: 10, of which 5 were waited for; matrix products, arithmetic and copies ran while one was open for 8% of the time, Pallas kernels for 14%

profile of v6, /device:TPU:32, one launch (start us, length us, event | category | flops | bytes accessed | tf_op | source)
XLA Modules:
  0.0 124.8 jit_solution(3577100498566389108)
XLA Ops:
  0.7 0.0 copy-start
  0.7 1.4 %copy-done = f32[512,768]{1,0:T(8,128)S(1)} copy-done((f32[512,768]{1,0:T(8,128)S(1)}, f32[512,768]{1,0:T(8,128)}, u32[]{:S(2)}) %copy-start) | copy-done | bytes 1572888
  2.1 0.7 copy-done.1
  2.8 2.1 %shard_map.67 = (f32[256,768]{1,0:T(8,128)S(1)}, f32[8,8,768]{2,1,0:T(8,128)}) custom-call(s32[3]{0:T(128)S(1)} %compare_select_fusion.6.start_ref, s32[1,256]{1,0:T(1,128)S(1)} %bitcast.18, f32[512,768]{1,0:T(8,128)S(1)} %copy-done), custom_call_target="tpu_custom_call" | custom-call | flops 600000000 | bytes 3000000 | tf_op jit(solution)/shard_map/pallas_call | solution.py:221
  4.9 8.6 %all-to-all-start = ((f32[8,8,768]{2,1,0:T(8,128)}), f32[8,8,768]{2,1,0:T(8,128)S(1)}, u32[]{:S(2)}, u32[]{:S(2)}) async-start(f32[8,8,768]{2,1,0:T(8,128)} %get-tuple-element.12), calls=%async_computation | async-start | bytes 393216 | tf_op jit(solution)/shard_map/all_to_all | solution.py:265
  13.4 0.0 copy-done.7
  13.4 3.0 %collective-permute-start = (f32[256,256]{1,0:T(8,128)S(1)}, f32[256,256]{1,0:T(8,128)S(1)}, u32[]{:S(2)}, u32[]{:S(2)}) collective-permute-start(f32[256,256]{1,0:T(8,128)S(1)} %copy-done.7), channel_id=1, source_target_pairs={{0,192},{64,128},{128,64},{192,0},{1,193},{65,129},{129,65},{193,1... | collective-permute-start | bytes 786440 | tf_op jit(solution)/shard_map/ppermute | solution.py:267
  16.5 6.0 %all-to-all-done = f32[8,8,768]{2,1,0:T(8,128)S(1)} async-done(((f32[8,8,768]{2,1,0:T(8,128)}), f32[8,8,768]{2,1,0:T(8,128)S(1)}, u32[]{:S(2)}, u32[]{:S(2)}) %all-to-all-start) | async-done | bytes 196640 | tf_op jit(solution)/shard_map/all_to_all | solution.py:265
  22.5 1.3 %broadcast_in_dim.52 = f32[8,8,8,768]{3,2,1,0:T(8,128)} broadcast(f32[8,8,768]{2,1,0:T(8,128)S(1)} %all-to-all-done), dimensions={1,2,3} | broadcast | bytes 1769472 | tf_op jit(solution)/shard_map/broadcast_in_dim | solution.py:24
  23.7 5.3 %all-to-all-start.1 = ((f32[8,8,8,768]{3,2,1,0:T(8,128)}), f32[8,8,8,768]{3,2,1,0:T(8,128)S(1)}, u32[]{:S(2)}, u32[]{:S(2)}) async-start(f32[8,8,8,768]{3,2,1,0:T(8,128)} %broadcast_in_dim.52), calls=%async_computation.1 | async-start | bytes 3145728 | tf_op jit(solution)/shard_map/all_to_all | solution.py:24
  29.0 0.0 collective-permute-done
  29.1 0.1 collective-permute-start.1
  29.2 3.5 %collective-permute-start.2 = (f32[256,768]{1,0:T(8,128)S(1)}, f32[256,768]{1,0:T(8,128)}, u32[]{:S(2)}, u32[]{:S(2)}) collective-permute-start(f32[256,768]{1,0:T(8,128)S(1)} %get-tuple-element.10), channel_id=1, source_target_pairs={{0,192},{64,128},{128,64},{192,0},{1,193},{65,129},{129,65},{193,1... | collective-permute-start | bytes 2359304 | tf_op jit(solution)/shard_map/ppermute | solution.py:264
  32.7 0.5 compare_select_fusion.3.place_ref
  34.0 0.0 collective-permute-done.1
  34.0 0.1 broadcast_select_fusion.2
  34.0 0.1 pad_maximum_fusion.1
  34.2 16.7 %collective-permute-done.2 = f32[256,768]{1,0:T(8,128)} collective-permute-done((f32[256,768]{1,0:T(8,128)S(1)}, f32[256,768]{1,0:T(8,128)}, u32[]{:S(2)}, u32[]{:S(2)}) %collective-permute-start.2) | collective-permute-done | bytes 786464 | tf_op jit(solution)/shard_map/ppermute | solution.py:264
  50.9 1.2 pad_maximum_fusion.rows_emb_ref
  52.2 0.0 copy-start.3
  52.2 1.2 copy-done.3
  53.4 0.2 multiply_reduce_fusion.1
  53.5 0.0 all-to-all-done.1
  53.5 0.0 copy-start.2
  53.6 0.8 slice.19
  54.3 0.2 multiply_reduce_fusion
  54.5 5.8 %collective-permute-start.3 = (f32[128,768]{1,0:T(8,128)}, f32[128,768]{1,0:T(8,128)}, u32[]{:S(2)}, u32[]{:S(2)}) collective-permute-start(f32[128,768]{1,0:T(8,128)} %slice.19), channel_id=1, source_target_pairs={{0,192},{64,128},{1,193},{65,129},{2,194},{66,130},{3,195},{67,131... | collective-permute-start | bytes 1179656 | tf_op jit(solution)/shard_map/ppermute | solution.py:297
  60.3 2.9 %fusion.4.tile_ref = f32[512,512]{1,0:T(8,128)S(1)} fusion(f32[512,768]{1,0:T(8,128)S(1)} %copy-done.4, f32[512,768]{1,0:T(8,128)S(1)} %bitcast.21, f32[]{:T(128)} %bitcast.17, s32[512]{0:T(512)S(1)} %fusion.7, f32[512]{0:T(512)S(1)} %multiply_reduce_fusion, f32[512]{0:T(512)S(1)} %multiply_reduce_fusion.1, s32[512]{0:T(512)S(1)} %pad_add_fusion), kind=kOutput, calls=%fused_computation.8 | convolution fusion | flops 2418016256 | bytes 4202500 | tf_op jit(solution)/shard_map/dot_general | solution.py:28
  63.2 2.1 %fusion.10 = f32[512,512]{1,0:T(8,128)} fusion(f32[512,512]{1,0:T(8,128)S(1)} %pad_maximum_fusion.1, f32[512,512]{1,0:T(8,128)S(1)} %fusion.4.tile_ref), kind=kOutput, calls=%fused_computation.46 | convolution fusion | flops 805306368 | bytes 3145728 | tf_op jit(solution)/shard_map/dot_general | solution.py:287
  65.3 4.3 %all-to-all-start.2 = ((f32[16,32,512]{2,1,0:T(8,128)}), f32[16,32,512]{2,1,0:T(8,128)S(1)}, u32[]{:S(2)}, u32[]{:S(2)}) async-start(f32[16,32,512]{2,1,0:T(8,128)} %bitcast.3), calls=%async_computation.2 | async-start | bytes 2097152 | tf_op jit(solution)/shard_map/all_to_all | solution.py:291
  69.6 0.0 collective-permute-done.3
  69.6 0.1 broadcast_select_fusion.3
  69.7 0.1 collective-permute-start.4
  69.8 1.7 %collective-permute-done.4 = f32[128,768]{1,0:T(8,128)S(1)} collective-permute-done((f32[128,768]{1,0:T(8,128)S(1)}, f32[128,768]{1,0:T(8,128)S(1)}, u32[]{:S(2)}, u32[]{:S(2)}) %collective-permute-start.4) | collective-permute-done | bytes 393248 | tf_op jit(solution)/shard_map/ppermute | solution.py:299
  71.5 1.0 broadcast_select_fusion.4
  72.5 14.1 %all-to-all-done.2 = f32[16,32,512]{2,1,0:T(8,128)S(1)} async-done(((f32[16,32,512]{2,1,0:T(8,128)}), f32[16,32,512]{2,1,0:T(8,128)S(1)}, u32[]{:S(2)}, u32[]{:S(2)}) %all-to-all-start.2) | async-done | bytes 1048608 | tf_op jit(solution)/shard_map/all_to_all | solution.py:291
  86.6 0.1 bitcast_reduce_fusion
  86.7 0.1 copy.8
  86.8 0.7 copy.9
  87.5 4.7 %all-to-all-start.3 = ((f32[8,2,4,512]{3,2,1,0:T(4,128)}), f32[8,2,4,512]{3,2,1,0:T(4,128)S(1)}, u32[]{:S(2)}, u32[]{:S(2)}) async-start(f32[8,2,4,512]{3,2,1,0:T(4,128)} %copy.9), calls=%async_computation.3 | async-start | bytes 262144 | tf_op jit(solution)/shard_map/all_to_all | solution.py:294
  92.2 18.0 %shard_map.68 = (f32[256,256]{1,0:T(8,128)}, f32[256,512]{1,0:T(8,128)}, f32[256,512]{1,0:T(8,128)}) custom-call(s32[4]{0:T(128)} %compare_select_fusion.3.place_ref, f32[1]{0:T(128)} %copy.11.ridge_ref, f32[128,768]{1,0:T(8,128)} %get-tuple-element.20.head_0_ref, f32[128,768]{1,0:T(8,128)} %get-tuple-element.19.head_1_ref, f32[512,768]{1,0:T(8,128)} %copy-done.3, ...), custom_call_target="tpu_custom_call" | custom-call | flops 900000000 | bytes 8000000 | tf_op jit(solution)/shard_map/pallas_call | solution.py:195
  110.2 0.5 collective-permute-start.5
  110.7 0.0 all-to-all-done.3
  110.8 0.6 pad_maximum_fusion.3
  111.4 11.3 %collective-permute-done.5 = f32[256,512]{1,0:T(8,128)S(1)} collective-permute-done((f32[256,512]{1,0:T(8,128)}, f32[256,512]{1,0:T(8,128)S(1)}, u32[]{:S(2)}, u32[]{:S(2)}) %collective-permute-start.5) | collective-permute-done | bytes 524320 | tf_op jit(solution)/shard_map/ppermute | solution.py:307
  122.7 1.0 slice_select_fusion
  123.8 0.1 broadcast_select_fusion
  123.9 1.0 pad_maximum_fusion.2
  (17 shorter events, 0.1 us)
Async XLA Ops:
  0.7 1.4 %copy-start = (f32[512,768]{1,0:T(8,128)S(1)}, f32[512,768]{1,0:T(8,128)}, u32[]{:S(2)}) copy-start(f32[512,768]{1,0:T(8,128)} %points_ref.1) | copy-start | bytes 4718596
  2.1 0.7 copy-start.1
  2.8 10.7 %copy-start.7 = (f32[256,256]{1,0:T(8,128)S(1)}, f32[256,256]{1,0:T(8,128)}, u32[]{:S(2)}) copy-start(f32[256,256]{1,0:T(8,128)} %param.6) | copy-start | bytes 786436
  4.9 17.6 %all-to-all-start = ((f32[8,8,768]{2,1,0:T(8,128)}), f32[8,8,768]{2,1,0:T(8,128)S(1)}, u32[]{:S(2)}, u32[]{:S(2)}) async-start(f32[8,8,768]{2,1,0:T(8,128)} %get-tuple-element.12), calls=%async_computation | async-start | bytes 393216 | tf_op jit(solution)/shard_map/all_to_all | solution.py:265
  13.4 15.6 %collective-permute-start = (f32[256,256]{1,0:T(8,128)S(1)}, f32[256,256]{1,0:T(8,128)S(1)}, u32[]{:S(2)}, u32[]{:S(2)}) collective-permute-start(f32[256,256]{1,0:T(8,128)S(1)} %copy-done.7), channel_id=1, source_target_pairs={{0,192},{64,128},{128,64},{192,0},{1,193},{65,129},{129,65},{193,1... | collective-permute-start | bytes 786440 | tf_op jit(solution)/shard_map/ppermute | solution.py:267
  23.7 29.8 %all-to-all-start.1 = ((f32[8,8,8,768]{3,2,1,0:T(8,128)}), f32[8,8,8,768]{3,2,1,0:T(8,128)S(1)}, u32[]{:S(2)}, u32[]{:S(2)}) async-start(f32[8,8,8,768]{3,2,1,0:T(8,128)} %broadcast_in_dim.52), calls=%async_computation.1 | async-start | bytes 3145728 | tf_op jit(solution)/shard_map/all_to_all | solution.py:24
  29.1 4.9 %collective-permute-start.1 = (f32[512,256]{1,0:T(8,128)S(1)}, f32[512,256]{1,0:T(8,128)S(1)}, u32[]{:S(2)}, u32[]{:S(2)}) collective-permute-start(f32[512,256]{1,0:T(8,128)S(1)} %constant_dynamic-update-slice_fusion), channel_id=1, source_target_pairs={{0,1},{1,0},{2,3},{3,2},{4,5},{5,4},{6,7},{7,6},{8,9},{9,8},{10,11... | collective-permute-start | bytes 1572872 | tf_op jit(solution)/shard_map/ppermute | solution.py:268
  29.2 21.8 %collective-permute-start.2 = (f32[256,768]{1,0:T(8,128)S(1)}, f32[256,768]{1,0:T(8,128)}, u32[]{:S(2)}, u32[]{:S(2)}) collective-permute-start(f32[256,768]{1,0:T(8,128)S(1)} %get-tuple-element.10), channel_id=1, source_target_pairs={{0,192},{64,128},{128,64},{192,0},{1,193},{65,129},{129,65},{193,1... | collective-permute-start | bytes 2359304 | tf_op jit(solution)/shard_map/ppermute | solution.py:264
  52.2 1.2 copy-start.3
  53.5 16.1 %copy-start.2 = (f32[8,8,8,768]{3,2,1,0:T(8,128)}, f32[8,8,8,768]{3,2,1,0:T(8,128)S(1)}, u32[]{:S(2)}) copy-start(f32[8,8,8,768]{3,2,1,0:T(8,128)S(1)} %all-to-all-done.1) | copy-start | bytes 4718596
  53.5 6.7 %copy-start.4 = (f32[512,768]{1,0:T(8,128)S(1)}, f32[512,768]{1,0:T(8,128)}, u32[]{:S(2)}) copy-start(f32[512,768]{1,0:T(8,128)} %copy-done.3) | copy-start | bytes 4718596
  54.5 15.1 %collective-permute-start.3 = (f32[128,768]{1,0:T(8,128)}, f32[128,768]{1,0:T(8,128)}, u32[]{:S(2)}, u32[]{:S(2)}) collective-permute-start(f32[128,768]{1,0:T(8,128)} %slice.19), channel_id=1, source_target_pairs={{0,192},{64,128},{1,193},{65,129},{2,194},{66,130},{3,195},{67,131... | collective-permute-start | bytes 1179656 | tf_op jit(solution)/shard_map/ppermute | solution.py:297
  63.2 2.1 %copy-start.5 = (f32[512,512]{1,0:T(8,128)}, f32[512,512]{1,0:T(8,128)S(1)}, u32[]{:S(2)}) copy-start(f32[512,512]{1,0:T(8,128)S(1)} %fusion.4.tile_ref) | copy-start | bytes 3145732
  65.3 21.3 %all-to-all-start.2 = ((f32[16,32,512]{2,1,0:T(8,128)}), f32[16,32,512]{2,1,0:T(8,128)S(1)}, u32[]{:S(2)}, u32[]{:S(2)}) async-start(f32[16,32,512]{2,1,0:T(8,128)} %bitcast.3), calls=%async_computation.2 | async-start | bytes 2097152 | tf_op jit(solution)/shard_map/all_to_all | solution.py:291
  69.7 1.8 %collective-permute-start.4 = (f32[128,768]{1,0:T(8,128)S(1)}, f32[128,768]{1,0:T(8,128)S(1)}, u32[]{:S(2)}, u32[]{:S(2)}) collective-permute-start(f32[128,768]{1,0:T(8,128)S(1)} %broadcast_select_fusion.3), channel_id=1, source_target_pairs={{0,1},{1,0},{2,3},{3,2},{4,5},{5,4},{6,7},{7,6},{8,9},{9,8},{10,11... | collective-permute-start | bytes 1179656 | tf_op jit(solution)/shard_map/ppermute | solution.py:299
  87.5 23.3 %all-to-all-start.3 = ((f32[8,2,4,512]{3,2,1,0:T(4,128)}), f32[8,2,4,512]{3,2,1,0:T(4,128)S(1)}, u32[]{:S(2)}, u32[]{:S(2)}) async-start(f32[8,2,4,512]{3,2,1,0:T(4,128)} %copy.9), calls=%async_computation.3 | async-start | bytes 262144 | tf_op jit(solution)/shard_map/all_to_all | solution.py:294
  110.2 13.5 %copy-start.6 = (f32[256,512]{1,0:T(8,128)S(1)}, f32[256,512]{1,0:T(8,128)}, u32[]{:S(2)}) copy-start(f32[256,512]{1,0:T(8,128)} %get-tuple-element.16) | copy-start | bytes 1572868
  110.2 12.5 %collective-permute-start.5 = (f32[256,512]{1,0:T(8,128)}, f32[256,512]{1,0:T(8,128)S(1)}, u32[]{:S(2)}, u32[]{:S(2)}) collective-permute-start(f32[256,512]{1,0:T(8,128)} %get-tuple-element.15), channel_id=1, source_target_pairs={{0,192},{64,128},{128,64},{192,0},{1,193},{65,129},{129,65},{193,1... | collective-permute-start | bytes 1572872 | tf_op jit(solution)/shard_map/ppermute | solution.py:307

commit v7 on v6

--- a/solution.py
+++ b/solution.py
@@ -198,6 +198,7 @@
         in_specs=[scalar, scalar] + [pl.BlockSpec(memory_space=pltpu.VMEM)] * 5,
         scratch_shapes=[pltpu.VMEM((PW, PW), jnp.float32)] * 2
         + [pltpu.VMEM((emb.shape[0], 2 * PW), jnp.float32) for emb in (rows_emb, cols_emb)],
+        compiler_params=pltpu.CompilerParams(vmem_limit_bytes=32 * 2**20),
         cost_estimate=pl.CostEstimate(flops=900_000_000, bytes_accessed=8_000_000, transcendentals=256),
     )(place, ridge, head_0, head_1, rows_emb, cols_emb, tile)
 
@@ -290,9 +291,8 @@
     n_plane = lax.axis_size(PLANE)
     arrived = lax.all_to_all(partial.reshape(n_plane, -1, half), PLANE, 0, 0, tiled=True)
     nearer = arrived.reshape(2, n_plane // 2, -1, half).sum(axis=1)
-    nearer = nearer.reshape(2, n_z, -1, half).swapaxes(0, 1)
-    projected = lax.all_to_all(nearer, "z", 0, 0, tiled=True).sum(axis=0)
-    projected = jnp.concatenate([projected[0], projected[1]], axis=1)
+    joined = jnp.concatenate([nearer[0], nearer[1]], axis=1).reshape(n_z, -1, 2 * half)
+    projected = lax.all_to_all(joined, "z", 0, 0, tiled=True).sum(axis=0)
 
     sent_heads = lax.ppermute(column_emb[:PW], Y, [(y, n_y - 1 - y) for y in range(n_y // 2)])
     own_heads = jnp.where(upper, sent_heads, column_emb[:PW])

time: 125 us -> 109 us (0.87)
  the two profiles are of different devices: /device:TPU:32 before, /device:TPU:1 now
where the time goes in v7:
time: 109 us; the launch traced here: 108 us
  starting transfers between devices  37.5 us (34%)
  waiting for transfers between devices  21.7 us (20%)
  Pallas kernels  17.7 us (16%)
  blocking collectives  10.2 us (9%)
  other arithmetic  7.27 us (7%)
  local copies, waits for them, and re-layouts  6.76 us (6%)
  matrix products  4.94 us (5%)
  between operations  1.5 us (1%)
    pallas_call x1, Pallas kernels, updated(): pl.pallas_call(update_kernel, out_shape=(jax.ShapeDtypeStruct((kept, 2 *...  15.6 us
    ppermute x1, waiting for transfers between devices, per_device(): peer_embedded = lax.ppermute(embedded, Y, across)  14.9 us
    all_to_all x1, blocking collectives, per_device(): projected = lax.all_to_all(joined, 'z', 0, 0, tiled=True).sum(axis=0)  10.2 us
    all_to_all x1, starting transfers between devices, per_device(): own_line = lax.all_to_all(own_copies, 'z', 0, 0, tiled=True)  9 us
    all_to_all x1, waiting for transfers between devices, per_device(): own_line = lax.all_to_all(own_copies, 'z', 0, 0, tiled=True)  5.44 us
    ppermute x1, starting transfers between devices, per_device(): lax.ppermute(column_emb[:PW], Y, [(y, n_y - 1 - y) for y in range(n_y //...  5.06 us
    all_to_all x1, starting transfers between devices, to_all(): lax.all_to_all(jnp.broadcast_to(x[None], (peers, *x.shape)), axis, 0, 0,...  5.03 us
    unnamed x21, local copies, waits for them, and re-layouts  4.61 us
  transfers between devices with their start and end apart: 9, of which 3 were waited for; matrix products, arithmetic and copies ran while one was open for 13% of the time, Pallas kernels for 14%

profile of v7, /device:TPU:1, one launch (start us, length us, event | category | flops | bytes accessed | tf_op | source)
XLA Modules:
  0.0 107.5 jit_solution(4594770579214905991)
XLA Ops:
  0.7 0.0 copy-start.6
  0.7 1.4 %copy-done.6 = f32[512,768]{1,0:T(8,128)S(1)} copy-done((f32[512,768]{1,0:T(8,128)S(1)}, f32[512,768]{1,0:T(8,128)}, u32[]{:S(2)}) %copy-start.6) | copy-done | bytes 1572888
  2.1 0.7 copy-done.7
  2.8 2.1 %shard_map.67 = (f32[256,768]{1,0:T(8,128)S(1)}, f32[8,8,768]{2,1,0:T(8,128)}) custom-call(s32[3]{0:T(128)S(1)} %compare_select_fusion.6.start_ref, s32[1,256]{1,0:T(1,128)S(1)} %bitcast.16, f32[512,768]{1,0:T(8,128)S(1)} %copy-done.6), custom_call_target="tpu_custom_call" | custom-call | flops 600000000 | bytes 3000000 | tf_op jit(solution)/shard_map/pallas_call | solution.py:222
  4.9 9.0 %all-to-all-start = ((f32[8,8,768]{2,1,0:T(8,128)}), f32[8,8,768]{2,1,0:T(8,128)S(1)}, u32[]{:S(2)}, u32[]{:S(2)}) async-start(f32[8,8,768]{2,1,0:T(8,128)} %get-tuple-element.12), calls=%async_computation | async-start | bytes 393216 | tf_op jit(solution)/shard_map/all_to_all | solution.py:266
  13.9 0.0 copy-done.9
  13.9 2.8 %collective-permute-start = (f32[256,256]{1,0:T(8,128)S(1)}, f32[256,256]{1,0:T(8,128)S(1)}, u32[]{:S(2)}, u32[]{:S(2)}) collective-permute-start(f32[256,256]{1,0:T(8,128)S(1)} %copy-done.9), channel_id=1, source_target_pairs={{0,192},{64,128},{128,64},{192,0},{1,193},{65,129},{129,65},{193,1... | collective-permute-start | bytes 786440 | tf_op jit(solution)/shard_map/ppermute | solution.py:268
  16.7 0.7 constant_dynamic-update-slice_fusion.1
  17.4 5.4 %all-to-all-done = f32[8,8,768]{2,1,0:T(8,128)S(1)} async-done(((f32[8,8,768]{2,1,0:T(8,128)}), f32[8,8,768]{2,1,0:T(8,128)S(1)}, u32[]{:S(2)}, u32[]{:S(2)}) %all-to-all-start) | async-done | bytes 196640 | tf_op jit(solution)/shard_map/all_to_all | solution.py:266
  22.9 1.3 %broadcast_in_dim.52 = f32[8,8,8,768]{3,2,1,0:T(8,128)} broadcast(f32[8,8,768]{2,1,0:T(8,128)S(1)} %all-to-all-done), dimensions={1,2,3} | broadcast | bytes 1769472 | tf_op jit(solution)/shard_map/broadcast_in_dim | solution.py:24
  24.2 5.0 %all-to-all-start.1 = ((f32[8,8,8,768]{3,2,1,0:T(8,128)}), f32[8,8,8,768]{3,2,1,0:T(8,128)S(1)}, u32[]{:S(2)}, u32[]{:S(2)}) async-start(f32[8,8,8,768]{3,2,1,0:T(8,128)} %broadcast_in_dim.52), calls=%async_computation.1 | async-start | bytes 3145728 | tf_op jit(solution)/shard_map/all_to_all | solution.py:24
  29.2 0.0 collective-permute-done
  29.2 0.8 constant_dynamic-update-slice_fusion
  30.0 2.7 %collective-permute-start.1 = (f32[512,256]{1,0:T(8,128)}, f32[512,256]{1,0:T(8,128)}, u32[]{:S(2)}, u32[]{:S(2)}) collective-permute-start(f32[512,256]{1,0:T(8,128)} %constant_dynamic-update-slice_fusion), channel_id=1, source_target_pairs={{0,1},{1,0},{2,3},{3,2},{4,5},{5,4},{6,7},{7,6},{8,9},{9,8},{10,11... | collective-permute-start | bytes 1572872 | tf_op jit(solution)/shard_map/ppermute | solution.py:269
  32.7 0.0 copy-done.4
  32.7 3.2 %collective-permute-start.2 = (f32[256,768]{1,0:T(8,128)S(1)}, f32[256,768]{1,0:T(8,128)}, u32[]{:S(2)}, u32[]{:S(2)}) collective-permute-start(f32[256,768]{1,0:T(8,128)S(1)} %get-tuple-element.10), channel_id=1, source_target_pairs={{0,192},{64,128},{128,64},{192,0},{1,193},{65,129},{129,65},{193,1... | collective-permute-start | bytes 2359304 | tf_op jit(solution)/shard_map/ppermute | solution.py:265
  36.6 0.0 collective-permute-done.1
  36.6 1.3 %broadcast_select_fusion.2 = (f32[512,256]{1,0:T(8,128)S(1)}, f32[512,256]{1,0:T(8,128)S(1)}) fusion(f32[512,256]{1,0:T(8,128)} %collective-permute-done.1, f32[512,256]{1,0:T(8,128)} %constant_dynamic-update-slice_fusion, pred[]{:T(512)S(6)} %eq.43), kind=kLoop, calls=%fused_computation.15 | loop fusion | flops 262144 | bytes 2097153 | tf_op jit(solution)/shard_map/jit(_where)/select_n | solution.py:260
  37.9 0.0 copy-start.5
  37.9 1.2 %pad_maximum_fusion.1 = f32[512,512]{1,0:T(8,128)} fusion(f32[512,256]{1,0:T(8,128)S(1)} %get-tuple-element.18, f32[512,256]{1,0:T(8,128)S(1)} %get-tuple-element.17), kind=kLoop, calls=%fused_computation.9 | loop fusion | flops 262144 | bytes 2097152 | tf_op jit(solution)/shard_map/concatenate | solution.py:260
  39.0 14.9 %collective-permute-done.2 = f32[256,768]{1,0:T(8,128)} collective-permute-done((f32[256,768]{1,0:T(8,128)S(1)}, f32[256,768]{1,0:T(8,128)}, u32[]{:S(2)}, u32[]{:S(2)}) %collective-permute-start.2) | collective-permute-done | bytes 786464 | tf_op jit(solution)/shard_map/ppermute | solution.py:265
  53.9 0.0 copy-done.5
  53.9 1.2 %pad_maximum_fusion.rows_emb_ref = f32[512,768]{1,0:T(8,128)S(1)} fusion(f32[256,768]{1,0:T(8,128)} %collective-permute-done.2, f32[256,768]{1,0:T(8,128)S(1)} %copy-done.5), kind=kLoop, calls=%fused_computation | loop fusion | flops 393216 | bytes 3145728 | tf_op jit(solution)/shard_map/concatenate | solution.py:274
  55.1 0.2 multiply_reduce_fusion.1
  55.3 0.0 all-to-all-done.1
  55.3 0.2 multiply_reduce_fusion
  55.5 5.1 %collective-permute-start.3 = (f32[128,768]{1,0:T(8,128)S(1)}, f32[128,768]{1,0:T(8,128)}, u32[]{:S(2)}, u32[]{:S(2)}) collective-permute-start(f32[128,768]{1,0:T(8,128)S(1)} %slice.19), channel_id=1, source_target_pairs={{0,192},{64,128},{1,193},{65,129},{2,194},{66,130},{3,195},{67,131... | collective-permute-start | bytes 1179656 | tf_op jit(solution)/shard_map/ppermute | solution.py:297
  60.6 2.9 %fusion.4.tile_ref = f32[512,512]{1,0:T(8,128)S(1)} fusion(f32[512,768]{1,0:T(8,128)S(1)} %pad_maximum_fusion.rows_emb_ref, f32[512,768]{1,0:T(8,128)S(1)} %bitcast.13, f32[]{:T(128)} %bitcast.10, s32[512]{0:T(512)S(1)} %fusion.7, f32[512]{0:T(512)S(1)} %multiply_reduce_fusion, f32[512]{0:T(512)S(1)} %multiply_reduce_fusion.1, s32[512]{0:T(512)S(1)} %pad_add_fusion), kind=kOutput, calls=%fused_computation.8 | convolution fusion | flops 2418016256 | bytes 4202500 | tf_op jit(solution)/shard_map/dot_general | solution.py:28
  63.5 0.0 copy-done.8
  63.5 2.0 %fusion.11 = f32[512,512]{1,0:T(8,128)} fusion(f32[512,512]{1,0:T(8,128)S(1)} %copy-done.8, f32[512,512]{1,0:T(8,128)S(1)} %fusion.4.tile_ref), kind=kOutput, calls=%fused_computation.45 | convolution fusion | flops 805306368 | bytes 3145728 | tf_op jit(solution)/shard_map/dot_general | solution.py:288
  65.5 1.0 copy-done
  66.5 4.3 %all-to-all-start.2 = ((f32[16,32,512]{2,1,0:T(8,128)}), f32[16,32,512]{2,1,0:T(8,128)}, u32[]{:S(2)}, u32[]{:S(2)}) async-start(f32[16,32,512]{2,1,0:T(8,128)} %bitcast.17), calls=%async_computation.2 | async-start | bytes 2097152 | tf_op jit(solution)/shard_map/all_to_all | solution.py:292
  70.9 0.0 collective-permute-done.3
  70.9 0.1 broadcast_select_fusion.3
  70.9 1.5 %collective-permute-start.4 = (f32[128,768]{1,0:T(8,128)S(1)}, f32[128,768]{1,0:T(8,128)S(1)}, u32[]{:S(2)}, u32[]{:S(2)}) collective-permute-start(f32[128,768]{1,0:T(8,128)S(1)} %broadcast_select_fusion.3), channel_id=1, source_target_pairs={{0,1},{1,0},{2,3},{3,2},{4,5},{5,4},{6,7},{7,6},{8,9},{9,8},{10,11... | collective-permute-start | bytes 1179656 | tf_op jit(solution)/shard_map/ppermute | solution.py:299
  72.4 1.3 %collective-permute-done.4 = f32[128,768]{1,0:T(8,128)S(1)} collective-permute-done((f32[128,768]{1,0:T(8,128)S(1)}, f32[128,768]{1,0:T(8,128)S(1)}, u32[]{:S(2)}, u32[]{:S(2)}) %collective-permute-start.4) | collective-permute-done | bytes 393248 | tf_op jit(solution)/shard_map/ppermute | solution.py:299
  73.7 0.1 broadcast_select_fusion.4
  73.8 15.6 %shard_map.68 = (f32[256,256]{1,0:T(8,128)}, f32[256,512]{1,0:T(8,128)S(1)}, f32[256,512]{1,0:T(8,128)}) custom-call(s32[4]{0:T(128)S(1)} %compare_select_fusion.3.place_ref, f32[1]{0:T(128)} %copy.10.ridge_ref, f32[128,768]{1,0:T(8,128)S(1)} %get-tuple-element.20.head_0_ref, f32[128,768]{1,0:T(8,128)S(1)} %get-tuple-element.19.head_1_ref, ...), custom_call_target="tpu_custom_call" | custom-call | flops 900000000 | bytes 8000000 | tf_op jit(solution)/shard_map/pallas_call | solution.py:195
  89.4 0.8 copy-done.2
  90.2 3.9 %collective-permute-start.5 = (f32[256,512]{1,0:T(8,128)}, f32[256,512]{1,0:T(8,128)S(1)}, u32[]{:S(2)}, u32[]{:S(2)}) collective-permute-start(f32[256,512]{1,0:T(8,128)} %get-tuple-element.15), channel_id=1, source_target_pairs={{0,192},{64,128},{128,64},{192,0},{1,193},{65,129},{129,65},{193,1... | collective-permute-start | bytes 1572872 | tf_op jit(solution)/shard_map/ppermute | solution.py:307
  94.1 0.0 all-to-all-done.2
  94.1 1.3 %bitcast_reduce_fusion = f32[2,32,512]{2,1,0:T(8,128)S(1)} fusion(f32[16,32,512]{2,1,0:T(8,128)} %all-to-all-done.2), kind=kLoop, calls=%fused_computation.10 | loop fusion | flops 229376 | bytes 1179648 | tf_op jit(solution)/shard_map/reduce_sum | solution.py:293
  95.5 10.2 %all_to_all.20 = f32[8,4,1024]{2,1,0:T(4,128)S(1)} all-to-all(f32[8,4,1024]{2,1,0:T(4,128)S(1)} %pad_maximum_fusion.3), channel_id=1, replica_groups=mesh['half'=2,'near'=2,'x'=4,'z'=8,'cols'=2] {'z'}, dimensions={0} | all-to-all | bytes 262144 | tf_op jit(solution)/shard_map/all_to_all | solution.py:295
  105.8 0.6 reduce_sum.39
  106.4 0.0 collective-permute-done.5
  106.4 0.1 slice_select_fusion
  106.5 0.1 broadcast_select_fusion
  106.6 1.0 pad_maximum_fusion.2
  (20 shorter events, 0.2 us)
Async XLA Ops:
  0.7 1.4 %copy-start.6 = (f32[512,768]{1,0:T(8,128)S(1)}, f32[512,768]{1,0:T(8,128)}, u32[]{:S(2)}) copy-start(f32[512,768]{1,0:T(8,128)} %points_ref.1) | copy-start | bytes 4718596
  2.1 0.7 copy-start.7
  2.8 11.1 %copy-start.9 = (f32[256,256]{1,0:T(8,128)S(1)}, f32[256,256]{1,0:T(8,128)}, u32[]{:S(2)}) copy-start(f32[256,256]{1,0:T(8,128)} %param.6) | copy-start | bytes 786436
  4.9 27.8 %copy-start.4 = (f32[256,768]{1,0:T(8,128)}, f32[256,768]{1,0:T(8,128)S(1)}, u32[]{:S(2)}) copy-start(f32[256,768]{1,0:T(8,128)S(1)} %get-tuple-element.10) | copy-start | bytes 2359300
  4.9 18.0 %all-to-all-start = ((f32[8,8,768]{2,1,0:T(8,128)}), f32[8,8,768]{2,1,0:T(8,128)S(1)}, u32[]{:S(2)}, u32[]{:S(2)}) async-start(f32[8,8,768]{2,1,0:T(8,128)} %get-tuple-element.12), calls=%async_computation | async-start | bytes 393216 | tf_op jit(solution)/shard_map/all_to_all | solution.py:266
  13.9 15.3 %collective-permute-start = (f32[256,256]{1,0:T(8,128)S(1)}, f32[256,256]{1,0:T(8,128)S(1)}, u32[]{:S(2)}, u32[]{:S(2)}) collective-permute-start(f32[256,256]{1,0:T(8,128)S(1)} %copy-done.9), channel_id=1, source_target_pairs={{0,192},{64,128},{128,64},{192,0},{1,193},{65,129},{129,65},{193,1... | collective-permute-start | bytes 786440 | tf_op jit(solution)/shard_map/ppermute | solution.py:268
  24.2 31.1 %all-to-all-start.1 = ((f32[8,8,8,768]{3,2,1,0:T(8,128)}), f32[8,8,8,768]{3,2,1,0:T(8,128)S(1)}, u32[]{:S(2)}, u32[]{:S(2)}) async-start(f32[8,8,8,768]{3,2,1,0:T(8,128)} %broadcast_in_dim.52), calls=%async_computation.1 | async-start | bytes 3145728 | tf_op jit(solution)/shard_map/all_to_all | solution.py:24
  30.0 6.6 %collective-permute-start.1 = (f32[512,256]{1,0:T(8,128)}, f32[512,256]{1,0:T(8,128)}, u32[]{:S(2)}, u32[]{:S(2)}) collective-permute-start(f32[512,256]{1,0:T(8,128)} %constant_dynamic-update-slice_fusion), channel_id=1, source_target_pairs={{0,1},{1,0},{2,3},{3,2},{4,5},{5,4},{6,7},{7,6},{8,9},{9,8},{10,11... | collective-permute-start | bytes 1572872 | tf_op jit(solution)/shard_map/ppermute | solution.py:269
  32.7 21.2 %collective-permute-start.2 = (f32[256,768]{1,0:T(8,128)S(1)}, f32[256,768]{1,0:T(8,128)}, u32[]{:S(2)}, u32[]{:S(2)}) collective-permute-start(f32[256,768]{1,0:T(8,128)S(1)} %get-tuple-element.10), channel_id=1, source_target_pairs={{0,192},{64,128},{128,64},{192,0},{1,193},{65,129},{129,65},{193,1... | collective-permute-start | bytes 2359304 | tf_op jit(solution)/shard_map/ppermute | solution.py:265
  37.9 16.0 %copy-start.5 = (f32[256,768]{1,0:T(8,128)S(1)}, f32[256,768]{1,0:T(8,128)}, u32[]{:S(2)}) copy-start(f32[256,768]{1,0:T(8,128)} %copy-done.4) | copy-start | bytes 2359300
  55.5 15.3 %collective-permute-start.3 = (f32[128,768]{1,0:T(8,128)S(1)}, f32[128,768]{1,0:T(8,128)}, u32[]{:S(2)}, u32[]{:S(2)}) collective-permute-start(f32[128,768]{1,0:T(8,128)S(1)} %slice.19), channel_id=1, source_target_pairs={{0,192},{64,128},{1,193},{65,129},{2,194},{66,130},{3,195},{67,131... | collective-permute-start | bytes 1179656 | tf_op jit(solution)/shard_map/ppermute | solution.py:297
  60.6 2.9 %copy-start.8 = (f32[512,512]{1,0:T(8,128)S(1)}, f32[512,512]{1,0:T(8,128)}, u32[]{:S(2)}) copy-start(f32[512,512]{1,0:T(8,128)} %pad_maximum_fusion.1) | copy-start | bytes 3145732
  65.5 1.0 copy-start
  66.5 27.6 %all-to-all-start.2 = ((f32[16,32,512]{2,1,0:T(8,128)}), f32[16,32,512]{2,1,0:T(8,128)}, u32[]{:S(2)}, u32[]{:S(2)}) async-start(f32[16,32,512]{2,1,0:T(8,128)} %bitcast.17), calls=%async_computation.2 | async-start | bytes 2097152 | tf_op jit(solution)/shard_map/all_to_all | solution.py:292
  70.8 3.0 %copy-start.1 = (f32[512,512]{1,0:T(8,128)S(1)}, f32[512,512]{1,0:T(8,128)}, u32[]{:S(2)}) copy-start(f32[512,512]{1,0:T(8,128)} %copy-done) | copy-start | bytes 3145732
  70.9 2.8 %collective-permute-start.4 = (f32[128,768]{1,0:T(8,128)S(1)}, f32[128,768]{1,0:T(8,128)S(1)}, u32[]{:S(2)}, u32[]{:S(2)}) collective-permute-start(f32[128,768]{1,0:T(8,128)S(1)} %broadcast_select_fusion.3), channel_id=1, source_target_pairs={{0,1},{1,0},{2,3},{3,2},{4,5},{5,4},{6,7},{7,6},{8,9},{9,8},{10,11... | collective-permute-start | bytes 1179656 | tf_op jit(solution)/shard_map/ppermute | solution.py:299
  89.4 0.8 copy-start.2
  90.2 16.2 %copy-start.3 = (f32[256,512]{1,0:T(8,128)S(1)}, f32[256,512]{1,0:T(8,128)}, u32[]{:S(2)}) copy-start(f32[256,512]{1,0:T(8,128)} %copy-done.2) | copy-start | bytes 1572868
  90.2 16.2 %collective-permute-start.5 = (f32[256,512]{1,0:T(8,128)}, f32[256,512]{1,0:T(8,128)S(1)}, u32[]{:S(2)}, u32[]{:S(2)}) collective-permute-start(f32[256,512]{1,0:T(8,128)} %get-tuple-element.15), channel_id=1, source_target_pairs={{0,192},{64,128},{128,64},{192,0},{1,193},{65,129},{129,65},{193,1... | collective-permute-start | bytes 1572872 | tf_op jit(solution)/shard_map/ppermute | solution.py:307

commit v8 on v7

--- a/solution.py
+++ b/solution.py
@@ -103,9 +103,15 @@
 
 
 def update_kernel(
-    place_ref, ridge_ref, head_0_ref, head_1_ref, rows_emb_ref, cols_emb_ref, tile_ref,
+    place_ref, ridge_ref, head_0_ref, head_1_ref, rows_emb_any, cols_emb_any, tile_any,
     panel_ref, mine_ref, given_ref, first_ref, second_ref, rows_ref, cols_ref,
+    rows_emb_ref, cols_emb_ref, tile_ref, rows_sem, cols_sem, tile_sem,
 ):
+    rows_copy = pltpu.make_async_copy(rows_emb_any, rows_emb_ref, rows_sem)
+    cols_copy = pltpu.make_async_copy(cols_emb_any, cols_emb_ref, cols_sem)
+    tile_copy = pltpu.make_async_copy(tile_any, tile_ref, tile_sem)
+    for copy in (rows_copy, cols_copy, tile_copy):
+        copy.start()
     head_emb = jnp.concatenate([head_0_ref[...], head_1_ref[...]], axis=0)
     heads = in_three(head_emb)
     n_heads, width = head_emb.shape
@@ -134,6 +140,8 @@
             if step < rows_ref.shape[0] // CHUNK
             else (cols_emb_ref, cols_ref, step * CHUNK - rows_ref.shape[0])
         )
+        if start == 0:
+            (rows_copy if emb_ref is rows_emb_ref else cols_copy).wait()
         emb = emb_ref[start : start + CHUNK, :]
         if emb_ref is rows_emb_ref:
             place = place_ref[start // kept] + start % kept + local
@@ -179,6 +187,7 @@
     def rows_of(two, part):
         return two[0][part], two[1][part]
 
+    tile_copy.wait()
     for out_ref, start in ((given_ref, kept), (mine_ref, 0)):
         part = slice(start, start + kept)
         out_ref[...] = (
@@ -195,10 +204,13 @@
     return pl.pallas_call(
         update_kernel,
         out_shape=(jax.ShapeDtypeStruct((kept, 2 * PW), jnp.float32), wide, wide),
-        in_specs=[scalar, scalar] + [pl.BlockSpec(memory_space=pltpu.VMEM)] * 5,
+        in_specs=[scalar, scalar]
+        + [pl.BlockSpec(memory_space=pltpu.VMEM)] * 2
+        + [pl.BlockSpec(memory_space=pl.ANY)] * 3,
         scratch_shapes=[pltpu.VMEM((PW, PW), jnp.float32)] * 2
-        + [pltpu.VMEM((emb.shape[0], 2 * PW), jnp.float32) for emb in (rows_emb, cols_emb)],
-        compiler_params=pltpu.CompilerParams(vmem_limit_bytes=32 * 2**20),
+        + [pltpu.VMEM((emb.shape[0], 2 * PW), jnp.float32) for emb in (rows_emb, cols_emb)]
+        + [pltpu.VMEM(whole.shape, jnp.float32) for whole in (rows_emb, cols_emb, tile)]
+        + [pltpu.SemaphoreType.DMA(())] * 3,
         cost_estimate=pl.CostEstimate(flops=900_000_000, bytes_accessed=8_000_000, transcendentals=256),
     )(place, ridge, head_0, head_1, rows_emb, cols_emb, tile)
 
@@ -301,9 +313,7 @@
     head_0 = jnp.where(swapped, peer_heads, own_heads)
     head_1 = jnp.where(swapped, own_heads, peer_heads)
 
-    panels, mine, given = updated(
-        places, ridge_shift, head_0, head_1, rows_emb, column_emb, tile
-    )
+    panels, mine, given = updated(places, ridge_shift, head_0, head_1, rows_emb, column_emb, tile)
     taken = lax.ppermute(given, Y, across)
     remainder = jnp.concatenate(
         [jnp.where(upper, taken, mine)[:, PW:], jnp.where(upper, mine, taken)], axis=1

time: 109 us -> 107 us (0.982); the launches traced: 108 us -> 107 us
  local copies, waits for them, and re-layouts: 6.76 us -> 4.65 us
  waiting for transfers between devices: 21.7 us -> 23.8 us
  Pallas kernels: 17.7 us -> 19.1 us
  starting transfers between devices: 37.5 us -> 36.2 us
    pallas_call x1, Pallas kernels: 15.6 us -> 16.9 us  [updated(): pl.pallas_call(update_kernel, out_shape=(jax.ShapeDtypeStruct((kept, 2 *...]
    unnamed x21 -> x19, local copies, waits for them, and re-layouts: 4.61 us -> 3.28 us
    reduce_sum x1, other arithmetic: 1.31 us -> 0.08 us  [per_device(): nearer = arrived.reshape(2, n_plane // 2, -1, half).sum(axis=1)]
    select_n x1, other arithmetic: 1.27 us -> 0.07 us  [ordered(): jnp.where(flag, other, mine)]
  transfers between devices with their start and end apart: 9 -> 9, of which waited for: 3 -> 4; matrix products, arithmetic and copies ran while one was open for 13% -> 11% of each run, Pallas kernels for 14% -> 16%
where the time goes in v8:
time: 107 us
  starting transfers between devices  36.2 us (34%)
  waiting for transfers between devices  23.8 us (22%)
  Pallas kernels  19.1 us (18%)
  blocking collectives  10.3 us (10%)
  other arithmetic  6.32 us (6%)
  matrix products  4.94 us (5%)
  local copies, waits for them, and re-layouts  4.65 us (4%)
  between operations  1.56 us (1%)
    pallas_call x1, Pallas kernels, updated(): pl.pallas_call(update_kernel, out_shape=(jax.ShapeDtypeStruct((kept, 2 *...  16.9 us
    ppermute x1, waiting for transfers between devices, per_device(): peer_embedded = lax.ppermute(embedded, Y, across)  15.4 us
    all_to_all x1, blocking collectives, per_device(): projected = lax.all_to_all(joined, 'z', 0, 0, tiled=True).sum(axis=0)  10.3 us
    all_to_all x1, starting transfers between devices, per_device(): own_line = lax.all_to_all(own_copies, 'z', 0, 0, tiled=True)  9 us
    all_to_all x1, waiting for transfers between devices, per_device(): own_line = lax.all_to_all(own_copies, 'z', 0, 0, tiled=True)  6.15 us
    all_to_all x1, starting transfers between devices, to_all(): lax.all_to_all(jnp.broadcast_to(x[None], (peers, *x.shape)), axis, 0, 0,...  5.03 us
    ppermute x1, starting transfers between devices, per_device(): lax.ppermute(column_emb[:PW], Y, [(y, n_y - 1 - y) for y in range(n_y //...  4.58 us
    all_to_all x1, starting transfers between devices, per_device(): lax.all_to_all(partial.reshape(n_plane, -1, half), PLANE, 0, 0, tiled=True)  4.07 us
  transfers between devices with their start and end apart: 9, of which 4 were waited for; matrix products, arithmetic and copies ran while one was open for 11% of the time, Pallas kernels for 16%

profile of v8, /device:TPU:1, one launch (start us, length us, event | category | flops | bytes accessed | tf_op | source)
XLA Modules:
  0.0 106.8 jit_solution(14416758523509504826)
XLA Ops:
  0.7 0.0 copy-start
  0.7 1.4 %copy-done = f32[512,768]{1,0:T(8,128)S(1)} copy-done((f32[512,768]{1,0:T(8,128)S(1)}, f32[512,768]{1,0:T(8,128)}, u32[]{:S(2)}) %copy-start) | copy-done | bytes 1572888
  2.1 0.7 copy-done.1
  2.8 2.1 %shard_map.67 = (f32[256,768]{1,0:T(8,128)S(1)}, f32[8,8,768]{2,1,0:T(8,128)}) custom-call(s32[3]{0:T(128)S(1)} %compare_select_fusion.6.start_ref, s32[1,256]{1,0:T(1,128)S(1)} %bitcast.11, f32[512,768]{1,0:T(8,128)S(1)} %copy-done), custom_call_target="tpu_custom_call" | custom-call | flops 600000000 | bytes 3000000 | tf_op jit(solution)/shard_map/pallas_call | solution.py:234
  4.9 9.0 %all-to-all-start = ((f32[8,8,768]{2,1,0:T(8,128)}), f32[8,8,768]{2,1,0:T(8,128)S(1)}, u32[]{:S(2)}, u32[]{:S(2)}) async-start(f32[8,8,768]{2,1,0:T(8,128)} %get-tuple-element.12), calls=%async_computation | async-start | bytes 393216 | tf_op jit(solution)/shard_map/all_to_all | solution.py:278
  13.9 0.0 copy-done.8
  13.9 2.8 %collective-permute-start = (f32[256,256]{1,0:T(8,128)S(1)}, f32[256,256]{1,0:T(8,128)S(1)}, u32[]{:S(2)}, u32[]{:S(2)}) collective-permute-start(f32[256,256]{1,0:T(8,128)S(1)} %copy-done.8), channel_id=1, source_target_pairs={{0,192},{64,128},{128,64},{192,0},{1,193},{65,129},{129,65},{193,1... | collective-permute-start | bytes 786440 | tf_op jit(solution)/shard_map/ppermute | solution.py:280
  16.7 6.1 %all-to-all-done = f32[8,8,768]{2,1,0:T(8,128)S(1)} async-done(((f32[8,8,768]{2,1,0:T(8,128)}), f32[8,8,768]{2,1,0:T(8,128)S(1)}, u32[]{:S(2)}, u32[]{:S(2)}) %all-to-all-start) | async-done | bytes 196640 | tf_op jit(solution)/shard_map/all_to_all | solution.py:278
  22.9 1.3 %broadcast_in_dim.52 = f32[8,8,8,768]{3,2,1,0:T(8,128)} broadcast(f32[8,8,768]{2,1,0:T(8,128)S(1)} %all-to-all-done), dimensions={1,2,3} | broadcast | bytes 1769472 | tf_op jit(solution)/shard_map/broadcast_in_dim | solution.py:24
  24.1 5.0 %all-to-all-start.1 = ((f32[8,8,8,768]{3,2,1,0:T(8,128)}), f32[8,8,8,768]{3,2,1,0:T(8,128)S(1)}, u32[]{:S(2)}, u32[]{:S(2)}) async-start(f32[8,8,8,768]{3,2,1,0:T(8,128)} %broadcast_in_dim.52), calls=%async_computation.1 | async-start | bytes 3145728 | tf_op jit(solution)/shard_map/all_to_all | solution.py:24
  29.2 0.0 collective-permute-done
  29.2 2.8 %collective-permute-start.1 = (f32[512,256]{1,0:T(8,128)S(1)}, f32[512,256]{1,0:T(8,128)S(1)}, u32[]{:S(2)}, u32[]{:S(2)}) collective-permute-start(f32[512,256]{1,0:T(8,128)S(1)} %constant_dynamic-update-slice_fusion), channel_id=1, source_target_pairs={{0,1},{1,0},{2,3},{3,2},{4,5},{5,4},{6,7},{7,6},{8,9},{9,8},{10,11... | collective-permute-start | bytes 1572872 | tf_op jit(solution)/shard_map/ppermute | solution.py:281
  32.0 3.2 %collective-permute-start.2 = (f32[256,768]{1,0:T(8,128)S(1)}, f32[256,768]{1,0:T(8,128)}, u32[]{:S(2)}, u32[]{:S(2)}) collective-permute-start(f32[256,768]{1,0:T(8,128)S(1)} %get-tuple-element.10), channel_id=1, source_target_pairs={{0,192},{64,128},{128,64},{192,0},{1,193},{65,129},{129,65},{193,1... | collective-permute-start | bytes 2359304 | tf_op jit(solution)/shard_map/ppermute | solution.py:277
  35.2 0.6 compare_select_fusion.3.place_ref
  36.5 0.0 collective-permute-done.1
  36.5 0.1 broadcast_select_fusion.2
  36.6 1.2 %pad_maximum_fusion.1 = f32[512,512]{1,0:T(8,128)} fusion(f32[512,256]{1,0:T(8,128)S(1)} %get-tuple-element.18, f32[512,256]{1,0:T(8,128)S(1)} %get-tuple-element.17), kind=kLoop, calls=%fused_computation.9 | loop fusion | flops 262144 | bytes 2097152 | tf_op jit(solution)/shard_map/concatenate | solution.py:272
  37.7 15.4 %collective-permute-done.2 = f32[256,768]{1,0:T(8,128)} collective-permute-done((f32[256,768]{1,0:T(8,128)S(1)}, f32[256,768]{1,0:T(8,128)}, u32[]{:S(2)}, u32[]{:S(2)}) %collective-permute-start.2) | collective-permute-done | bytes 786464 | tf_op jit(solution)/shard_map/ppermute | solution.py:277
  53.1 1.2 %pad_maximum_fusion.rows_emb_any = f32[512,768]{1,0:T(8,128)S(1)} fusion(f32[256,768]{1,0:T(8,128)} %collective-permute-done.2, f32[256,768]{1,0:T(8,128)S(1)} %get-tuple-element.10), kind=kLoop, calls=%fused_computation | loop fusion | flops 393216 | bytes 3145728 | tf_op jit(solution)/shard_map/concatenate | solution.py:286
  54.3 0.0 copy-start.3
  54.3 1.2 %copy-done.3 = f32[512,768]{1,0:T(8,128)} copy-done((f32[512,768]{1,0:T(8,128)}, f32[512,768]{1,0:T(8,128)S(1)}, u32[]{:S(2)}) %copy-start.3) | copy-done | bytes 1572888
  55.5 0.2 multiply_reduce_fusion.1
  55.7 0.0 all-to-all-done.1
  55.7 0.0 copy-start.2
  55.7 0.0 copy-start.4
  55.7 0.2 multiply_reduce_fusion
  55.9 4.6 %collective-permute-start.3 = (f32[128,768]{1,0:T(8,128)S(1)}, f32[128,768]{1,0:T(8,128)S(1)}, u32[]{:S(2)}, u32[]{:S(2)}) collective-permute-start(f32[128,768]{1,0:T(8,128)S(1)} %slice.19), channel_id=1, source_target_pairs={{0,192},{64,128},{1,193},{65,129},{2,194},{66,130},{3,195},{67,131... | collective-permute-start | bytes 1179656 | tf_op jit(solution)/shard_map/ppermute | solution.py:309
  60.5 0.0 copy-done.4
  60.5 0.0 copy-start.6
  60.5 2.9 %fusion.4.tile_any = f32[512,512]{1,0:T(8,128)S(1)} fusion(f32[512,768]{1,0:T(8,128)S(1)} %copy-done.4, f32[512,768]{1,0:T(8,128)S(1)} %bitcast.14, f32[]{:T(128)} %bitcast.10, s32[512]{0:T(512)S(1)} %fusion.7, f32[512]{0:T(512)S(1)} %multiply_reduce_fusion, f32[512]{0:T(512)S(1)} %multiply_reduce_fusion.1, s32[512]{0:T(512)S(1)} %pad_add_fusion), kind=kOutput, calls=%fused_computation.8 | convolution fusion | flops 2418016256 | bytes 4202500 | tf_op jit(solution)/shard_map/dot_general | solution.py:28
  63.4 0.0 copy-done.6
  63.4 2.1 %fusion.11 = f32[512,512]{1,0:T(8,128)} fusion(f32[512,512]{1,0:T(8,128)S(1)} %copy-done.6, f32[512,512]{1,0:T(8,128)S(1)} %fusion.4.tile_any), kind=kOutput, calls=%fused_computation.45 | convolution fusion | flops 805306368 | bytes 3145728 | tf_op jit(solution)/shard_map/dot_general | solution.py:300
  65.5 4.1 %all-to-all-start.2 = ((f32[16,32,512]{2,1,0:T(8,128)}), f32[16,32,512]{2,1,0:T(8,128)S(1)}, u32[]{:S(2)}, u32[]{:S(2)}) async-start(f32[16,32,512]{2,1,0:T(8,128)} %bitcast.17), calls=%async_computation.2 | async-start | bytes 2097152 | tf_op jit(solution)/shard_map/all_to_all | solution.py:304
  69.6 0.0 collective-permute-done.3
  69.6 1.8 %collective-permute-start.4 = (f32[128,768]{1,0:T(8,128)S(1)}, f32[128,768]{1,0:T(8,128)S(1)}, u32[]{:S(2)}, u32[]{:S(2)}) collective-permute-start(f32[128,768]{1,0:T(8,128)S(1)} %broadcast_select_fusion.3), channel_id=1, source_target_pairs={{0,1},{1,0},{2,3},{3,2},{4,5},{5,4},{6,7},{7,6},{8,9},{9,8},{10,11... | collective-permute-start | bytes 1179656 | tf_op jit(solution)/shard_map/ppermute | solution.py:311
  71.4 1.3 %collective-permute-done.4 = f32[128,768]{1,0:T(8,128)S(1)} collective-permute-done((f32[128,768]{1,0:T(8,128)S(1)}, f32[128,768]{1,0:T(8,128)S(1)}, u32[]{:S(2)}, u32[]{:S(2)}) %collective-permute-start.4) | collective-permute-done | bytes 393248 | tf_op jit(solution)/shard_map/ppermute | solution.py:311
  72.8 1.0 broadcast_select_fusion.4
  73.7 16.9 %shard_map.68 = (f32[256,256]{1,0:T(8,128)}, f32[256,512]{1,0:T(8,128)}, f32[256,512]{1,0:T(8,128)}) custom-call(s32[4]{0:T(128)} %compare_select_fusion.3.place_ref, f32[1]{0:T(128)} %copy.10.ridge_ref, f32[128,768]{1,0:T(8,128)} %get-tuple-element.20.head_0_ref, f32[128,768]{1,0:T(8,128)} %get-tuple-element.19.head_1_ref, f32[512,768]{1,0:T(8,128)} %copy-done.3, ...), custom_call_target="tpu_custom_call" | custom-call | flops 900000000 | bytes 8000000 | tf_op jit(solution)/shard_map/pallas_call | solution.py:204
  90.7 0.0 copy-start.7
  90.7 2.9 %collective-permute-start.5 = (f32[256,512]{1,0:T(8,128)}, f32[256,512]{1,0:T(8,128)S(1)}, u32[]{:S(2)}, u32[]{:S(2)}) collective-permute-start(f32[256,512]{1,0:T(8,128)} %get-tuple-element.15), channel_id=1, source_target_pairs={{0,192},{64,128},{128,64},{192,0},{1,193},{65,129},{129,65},{193,1... | collective-permute-start | bytes 1572872 | tf_op jit(solution)/shard_map/ppermute | solution.py:317
  93.6 0.0 all-to-all-done.2
  93.7 0.1 bitcast_reduce_fusion
  93.9 10.3 %all_to_all.20 = f32[8,4,1024]{2,1,0:T(4,128)S(1)} all-to-all(f32[8,4,1024]{2,1,0:T(4,128)S(1)} %pad_maximum_fusion.3), channel_id=1, replica_groups=mesh['half'=2,'near'=2,'x'=4,'z'=8,'cols'=2] {'z'}, dimensions={0} | all-to-all | bytes 262144 | tf_op jit(solution)/shard_map/all_to_all | solution.py:307
  104.1 0.6 reduce_sum.39
  104.8 0.9 collective-permute-done.5
  105.7 0.1 slice_select_fusion
  105.8 0.1 broadcast_select_fusion
  105.8 1.0 pad_maximum_fusion.2
  (18 shorter events, 0.2 us)
Async XLA Ops:
  0.7 1.4 %copy-start = (f32[512,768]{1,0:T(8,128)S(1)}, f32[512,768]{1,0:T(8,128)}, u32[]{:S(2)}) copy-start(f32[512,768]{1,0:T(8,128)} %points_ref.1) | copy-start | bytes 4718596
  2.1 0.7 copy-start.1
  2.8 11.1 %copy-start.8 = (f32[256,256]{1,0:T(8,128)S(1)}, f32[256,256]{1,0:T(8,128)}, u32[]{:S(2)}) copy-start(f32[256,256]{1,0:T(8,128)} %param.6) | copy-start | bytes 786436
  4.9 18.0 %all-to-all-start = ((f32[8,8,768]{2,1,0:T(8,128)}), f32[8,8,768]{2,1,0:T(8,128)S(1)}, u32[]{:S(2)}, u32[]{:S(2)}) async-start(f32[8,8,768]{2,1,0:T(8,128)} %get-tuple-element.12), calls=%async_computation | async-start | bytes 393216 | tf_op jit(solution)/shard_map/all_to_all | solution.py:278
  13.9 15.3 %collective-permute-start = (f32[256,256]{1,0:T(8,128)S(1)}, f32[256,256]{1,0:T(8,128)S(1)}, u32[]{:S(2)}, u32[]{:S(2)}) collective-permute-start(f32[256,256]{1,0:T(8,128)S(1)} %copy-done.8), channel_id=1, source_target_pairs={{0,192},{64,128},{128,64},{192,0},{1,193},{65,129},{129,65},{193,1... | collective-permute-start | bytes 786440 | tf_op jit(solution)/shard_map/ppermute | solution.py:280
  24.1 31.5 %all-to-all-start.1 = ((f32[8,8,8,768]{3,2,1,0:T(8,128)}), f32[8,8,8,768]{3,2,1,0:T(8,128)S(1)}, u32[]{:S(2)}, u32[]{:S(2)}) async-start(f32[8,8,8,768]{3,2,1,0:T(8,128)} %broadcast_in_dim.52), calls=%async_computation.1 | async-start | bytes 3145728 | tf_op jit(solution)/shard_map/all_to_all | solution.py:24
  29.2 7.3 %collective-permute-start.1 = (f32[512,256]{1,0:T(8,128)S(1)}, f32[512,256]{1,0:T(8,128)S(1)}, u32[]{:S(2)}, u32[]{:S(2)}) collective-permute-start(f32[512,256]{1,0:T(8,128)S(1)} %constant_dynamic-update-slice_fusion), channel_id=1, source_target_pairs={{0,1},{1,0},{2,3},{3,2},{4,5},{5,4},{6,7},{7,6},{8,9},{9,8},{10,11... | collective-permute-start | bytes 1572872 | tf_op jit(solution)/shard_map/ppermute | solution.py:281
  32.0 21.1 %collective-permute-start.2 = (f32[256,768]{1,0:T(8,128)S(1)}, f32[256,768]{1,0:T(8,128)}, u32[]{:S(2)}, u32[]{:S(2)}) collective-permute-start(f32[256,768]{1,0:T(8,128)S(1)} %get-tuple-element.10), channel_id=1, source_target_pairs={{0,192},{64,128},{128,64},{192,0},{1,193},{65,129},{129,65},{193,1... | collective-permute-start | bytes 2359304 | tf_op jit(solution)/shard_map/ppermute | solution.py:277
  54.3 1.2 %copy-start.3 = (f32[512,768]{1,0:T(8,128)}, f32[512,768]{1,0:T(8,128)S(1)}, u32[]{:S(2)}) copy-start(f32[512,768]{1,0:T(8,128)S(1)} %pad_maximum_fusion.rows_emb_any) | copy-start | bytes 4718596
  55.7 13.9 %copy-start.2 = (f32[8,8,8,768]{3,2,1,0:T(8,128)}, f32[8,8,8,768]{3,2,1,0:T(8,128)S(1)}, u32[]{:S(2)}) copy-start(f32[8,8,8,768]{3,2,1,0:T(8,128)S(1)} %all-to-all-done.1) | copy-start | bytes 4718596
  55.7 4.8 %copy-start.4 = (f32[512,768]{1,0:T(8,128)S(1)}, f32[512,768]{1,0:T(8,128)}, u32[]{:S(2)}) copy-start(f32[512,768]{1,0:T(8,128)} %copy-done.3) | copy-start | bytes 4718596
  55.9 13.7 %collective-permute-start.3 = (f32[128,768]{1,0:T(8,128)S(1)}, f32[128,768]{1,0:T(8,128)S(1)}, u32[]{:S(2)}, u32[]{:S(2)}) collective-permute-start(f32[128,768]{1,0:T(8,128)S(1)} %slice.19), channel_id=1, source_target_pairs={{0,192},{64,128},{1,193},{65,129},{2,194},{66,130},{3,195},{67,131... | collective-permute-start | bytes 1179656 | tf_op jit(solution)/shard_map/ppermute | solution.py:309
  60.5 2.9 %copy-start.6 = (f32[512,512]{1,0:T(8,128)S(1)}, f32[512,512]{1,0:T(8,128)}, u32[]{:S(2)}) copy-start(f32[512,512]{1,0:T(8,128)} %pad_maximum_fusion.1) | copy-start | bytes 3145732
  63.4 2.1 %copy-start.5 = (f32[512,512]{1,0:T(8,128)}, f32[512,512]{1,0:T(8,128)S(1)}, u32[]{:S(2)}) copy-start(f32[512,512]{1,0:T(8,128)S(1)} %fusion.4.tile_any) | copy-start | bytes 3145732
  65.5 28.2 %all-to-all-start.2 = ((f32[16,32,512]{2,1,0:T(8,128)}), f32[16,32,512]{2,1,0:T(8,128)S(1)}, u32[]{:S(2)}, u32[]{:S(2)}) async-start(f32[16,32,512]{2,1,0:T(8,128)} %bitcast.17), calls=%async_computation.2 | async-start | bytes 2097152 | tf_op jit(solution)/shard_map/all_to_all | solution.py:304
  69.6 3.1 %collective-permute-start.4 = (f32[128,768]{1,0:T(8,128)S(1)}, f32[128,768]{1,0:T(8,128)S(1)}, u32[]{:S(2)}, u32[]{:S(2)}) collective-permute-start(f32[128,768]{1,0:T(8,128)S(1)} %broadcast_select_fusion.3), channel_id=1, source_target_pairs={{0,1},{1,0},{2,3},{3,2},{4,5},{5,4},{6,7},{7,6},{8,9},{9,8},{10,11... | collective-permute-start | bytes 1179656 | tf_op jit(solution)/shard_map/ppermute | solution.py:311
  90.7 15.0 %copy-start.7 = (f32[256,512]{1,0:T(8,128)S(1)}, f32[256,512]{1,0:T(8,128)}, u32[]{:S(2)}) copy-start(f32[256,512]{1,0:T(8,128)} %get-tuple-element.16) | copy-start | bytes 1572868
  90.7 15.0 %collective-permute-start.5 = (f32[256,512]{1,0:T(8,128)}, f32[256,512]{1,0:T(8,128)S(1)}, u32[]{:S(2)}, u32[]{:S(2)}) collective-permute-start(f32[256,512]{1,0:T(8,128)} %get-tuple-element.15), channel_id=1, source_target_pairs={{0,192},{64,128},{128,64},{192,0},{1,193},{65,129},{129,65},{193,1... | collective-permute-start | bytes 1572872 | tf_op jit(solution)/shard_map/ppermute | solution.py:317
